TPU v7x, 16 devices: a 4x2x1 block of a 4x4x8 slice. The times are simulated.
16 devices in a mesh: data: 2 (over y, z), expert: 8 (over x, core).
Axes of the slice: x: 4, y: 2, z: 1, core: 2. Of those that a mesh axis runs over, the one named last changes fastest.
The devices are a block of a 4x4x8 slice.
Arguments:
- tok_x: bfloat16 [12288, 4096], P(('data', 'expert')), parts along dimension 0
- route_idx: int32 [12288, 2], P(('data', 'expert')), parts along dimension 0
- route_gate: float32 [12288, 2], P(('data', 'expert')), parts along dimension 0
- grad_y: bfloat16 [12288, 4096], P(('data', 'expert')), parts along dimension 0
- w_gate: bfloat16 [8, 4096, 1024], P('expert')
- w_up: bfloat16 [8, 4096, 1024], P('expert')
- w_down: bfloat16 [8, 1024, 4096], P('expert')
Outputs:
- output 1: bfloat16 [12288, 4096], P(('data', 'expert')), parts along dimension 0
- output 2: bfloat16 [12288, 4096], P(('data', 'expert')), parts along dimension 0
- output 3: float32 [16, 4096, 1024], P(('data', 'expert')), parts along dimension 0
- output 4: float32 [16, 4096, 1024], P(('data', 'expert')), parts along dimension 0
- output 5: float32 [16, 1024, 4096], P(('data', 'expert')), parts along dimension 0
There are 2 independent parts. A program takes and returns all parts, laid end to end along the dimension named above; an argument that names none is the same for every part.
All inputs are finite; a program needn't handle non-finite values.
Results may differ from a plain program's by a relative error of at most 0.00366429.
Values are sent between devices in bfloat16 or wider.
A program may use at most 768 MiB of HBM per device.

v0:
```python
import functools

import jax
import jax.numpy as jnp
from jax import lax
from jax.experimental import pallas as pl
from jax.experimental.layout import Layout, with_layout_constraint
from jax.experimental.pallas import tpu as pltpu
from jax.sharding import PartitionSpec as P

BF = jnp.bfloat16
F32 = jnp.float32
I32 = jnp.int32
PIECE = 16
TILE = 128
WINDOW = 144
SPAN = 256
VMEM_LIMIT = 50 * 2 ** 20


def dot(form, a, b):
    return jnp.einsum(form, a, b, preferred_element_type=F32)


def iota(shape, axis):
    return lax.broadcasted_iota(I32, shape, axis)


def count_before(mask):
    n = mask.shape[-1]
    earlier = iota((n, n), 0) < iota((n, n), 1)
    return dot('...u,us->...s', mask.astype(BF), earlier.astype(BF)).astype(I32)


def pick(table, index):
    sel = iota(table.shape, 0) == index
    return jnp.sum(jnp.where(sel, table, jnp.zeros_like(table)), axis=0)


def row_major(v):
    return with_layout_constraint(v, Layout(major_to_minor=tuple(range(v.ndim))))


def after(value, *others):
    return lax.optimization_barrier((value,) + others)[0]


def pack_kernel(scaled, dev_ref, seg_ref, low_ref, tab0, tab1, info, *refs):
    outs, (buf, pend, sem) = (refs[4:6], refs[6:8]), refs[8:]
    g = pl.program_id(0)
    toks = info.shape[2]
    length, start, extra, stage = [seg_ref[g, k] for k in range(4)]

    @pl.when(g == 0)
    def _():
        pend[0] = 0
        pend[1] = 0

    def drain(slot):
        def one(_, carry):
            pltpu.make_async_copy(buf.at[0, pl.ds(0, PIECE)], outs[0][0].at[pl.ds(0, PIECE)], sem.at[slot]).wait()
            return carry

        lax.fori_loop(0, pend[slot], one, 0)
        pend[slot] = 0

    def put(slot, p, side, at):
        for late, ref in enumerate(outs[side]):
            @pl.when((at >= stage) == bool(late))
            def _(ref=ref, late=late):
                spot = jnp.minimum(at - stage if late else at, ref.shape[0] - PIECE)
                src = buf.at[slot, pl.ds(pl.multiple_of(p * PIECE, PIECE), PIECE)]
                pltpu.make_async_copy(src, ref.at[pl.ds(pl.multiple_of(spot, PIECE), PIECE)], sem.at[slot]).start()
        pend[slot] = pend[slot] + 1

    def tile(i, carry):
        @pl.when(i * TILE < length)
        def _():
            slot = lax.rem(i, 2)
            drain(slot)
            vals = info[0]
            match = vals[0:1, :] == (iota((TILE, toks), 0) + i * TILE).astype(F32)

            def column(k, off):
                return jnp.sum(jnp.where(match, vals[k:k + 1, :] + off, 0.0), axis=1, keepdims=True)

            lows = [low_ref[g, 2 * i + k] for k in range(2)]

            def part(k, tab):
                at = column(1 + k, 1.0) - (lows[k] + 1).astype(F32)
                onehot = (at == iota((TILE, SPAN), 1).astype(F32)).astype(BF)
                got = jnp.dot(onehot, tab[0, pl.ds(pl.multiple_of(lows[k], PIECE), SPAN)], preferred_element_type=F32)
                return got * column(3 + k, 0.0) if scaled else got

            @pl.when((lows[0] >= 0) & (lows[1] < 0))
            def _():
                buf[slot] = part(0, tab0).astype(BF)

            @pl.when((lows[0] < 0) & (lows[1] >= 0))
            def _():
                buf[slot] = part(1, tab1).astype(BF)

            @pl.when((lows[0] >= 0) & (lows[1] >= 0))
            def _():
                buf[slot] = (part(0, tab0) + part(1, tab1)).astype(BF)

            def piece(p, carry):
                q = i * TILE + p * PIECE
                at = start + q
                near = jnp.where(at >= stage, at + extra, at)

                @pl.when((q < length) & (g < 2) & (at < extra))
                def _():
                    put(slot, p, 0, at)

                @pl.when((q < length) & (g < 2) & (at >= extra))
                def _():
                    put(slot, p, 1, at - extra)

                @pl.when((q < length) & (g >= 2) & (g < 4))
                def _():
                    put(slot, p, 0, near)

                @pl.when((q < length) & (g >= 4))
                def _():
                    put(slot, p, 1, near)

                return carry

            lax.fori_loop(0, TILE // PIECE, piece, 0)

        return carry

    lax.fori_loop(0, toks // TILE, tile, 0)

    @pl.when(g == pl.num_programs(0) - 1)
    def _():
        drain(0)
        drain(1)


def arrive_kernel(scaled, second, home_ref, win_ref, tab0, tab1, info, up1, up2, down1, down2, out, acc, wbuf, sem):
    t, last = pl.program_id(0), pl.num_programs(0) - 1
    windows = (up1, up2, up2, down1, down2, down2)

    def copies(step, do):
        slot = lax.rem(step, 2)
        for w, ref in enumerate(windows):
            begin = win_ref[step, w]

            @pl.when(begin >= 0)
            def _(ref=ref, w=w, begin=begin):
                src = ref.at[pl.ds(pl.multiple_of(jnp.maximum(begin, 0), PIECE), WINDOW)]
                do(pltpu.make_async_copy(src, wbuf.at[slot, w, pl.ds(0, WINDOW)], sem.at[slot, w]))

    @pl.when(t == 0)
    def _():
        wbuf[:, :, WINDOW:] = jnp.zeros((2, len(windows), SPAN - WINDOW, wbuf.shape[3]), BF)
        copies(0, lambda c: c.start())

    @pl.when(t < last)
    def _():
        copies(t + 1, lambda c: c.start())

    vals = info[0]
    eye = iota((TILE, TILE), 0) == iota((TILE, TILE), 1)

    def column(k):
        return jnp.sum(jnp.where(eye, vals[k:k + 1, :], 0.0), axis=1, keepdims=True)

    def add(begin, base, spot, weight, rows):
        @pl.when(begin >= 0)
        def _():
            at = column(spot) - (begin + base).astype(F32)
            onehot = (at == iota((TILE, SPAN), 1).astype(F32)).astype(BF)
            part = jnp.dot(onehot, rows(), preferred_element_type=F32)
            acc[...] = acc[...] + (part * column(weight) if scaled else part)

    acc[...] = jnp.zeros_like(acc)
    for k, tab in enumerate((tab0, tab1)):
        low = win_ref[t, len(windows) + k]
        add(low, 0, k, 2 + k, lambda tab=tab, low=low: tab[0, pl.ds(pl.multiple_of(low, PIECE), SPAN)])
    copies(t, lambda c: c.wait())
    slot = lax.rem(t, 2)
    for w, (spot, weight, base) in enumerate(((4, 8, 0), (4, 8, second), (6, 10, 0), (5, 9, 0), (5, 9, second), (7, 10, 0))):
        add(win_ref[t, w], base, spot, weight, lambda w=w: wbuf[slot, w])
    out[0] = acc[...].astype(BF)


def by_count(count, cap, run):
    for n in range(0, cap + 1, TILE):
        @pl.when((count > n - TILE) & (count <= n))
        def _(n=n):
            run(n)


def inner_kernel(count_ref, info, dy, w2t, a_ref, b_ref, g_ref, da_ref, db_ref):
    cap, dim = g_ref.shape[1:]
    step = dim // 4

    def run(n):
        if n:
            vals = info[0]
            match = vals[0:1, :] == iota((n, vals.shape[1]), 0).astype(F32)
            gate = jnp.sum(jnp.where(match, vals[1:2, :], 0.0), axis=1, keepdims=True)
            onehot = match.astype(BF)
            for c in range(0, dim, step):
                got = jnp.dot(onehot, dy[0, :, c:c + step], preferred_element_type=F32)
                g_ref[0, :n, c:c + step] = (gate * got).astype(BF)
            dh = jnp.dot(g_ref[0, :n], w2t[...], preferred_element_type=F32).astype(BF).astype(F32)
            a, b = a_ref[0, :n].astype(F32), b_ref[0, :n].astype(F32)
            sig = jax.nn.sigmoid(a)
            da_ref[0, :n] = (dh * b * (sig * (1.0 + a * (1.0 - sig)))).astype(BF)
            db_ref[0, :n] = (dh * (a * sig)).astype(BF)
        if n < cap:
            for ref in (g_ref, da_ref, db_ref):
                ref[0, n:] = jnp.zeros((cap - n, ref.shape[2]), BF)

    by_count(count_ref[pl.program_id(0)], cap, run)


def input_kernel(count_ref, da, db, w1t, w3t, out):
    cap, width = out.shape[1:]
    step = width // 2

    def run(n):
        if n:
            for c in range(0, width, step):
                got = jnp.dot(da[0, :n], w1t[:, c:c + step], preferred_element_type=F32)
                got = got + jnp.dot(db[0, :n], w3t[:, c:c + step], preferred_element_type=F32)
                out[0, :n, c:c + step] = got.astype(BF)
        if n < cap:
            out[0, n:] = jnp.zeros((cap - n, width), BF)

    by_count(count_ref[pl.program_id(0)], cap, run)


def solution(mesh):
    group = mesh.shape['expert']
    chips = group // 2
    tok_spec = P(('data', 'expert'))
    w_spec = P('expert')
    to_mate = [(i, i ^ 1) for i in range(group)]
    to_next = [(i, (i + 2) % group) for i in range(group)]
    to_prev = [(i, (i - 2) % group) for i in range(group)]

    def layer(tok_x, route_idx, route_gate, grad_y, w_gate, w_up, w_down):
        toks, dim = tok_x.shape
        tops = route_idx.shape[1]
        experts = w_gate.shape[0] * group
        stride = experts // min(4, experts // 8)
        cap = max(4, 2 * toks * tops // experts)
        rows = group * cap
        half = dim // 2
        tiles = toks // TILE
        small = toks * 13 // 12 // PIECE * PIECE
        stage = toks * 71 // 48 // PIECE * PIECE
        place = 2 * stage
        me = lax.axis_index('expert')
        chip, core = me // 2, me % 2
        up, down, far = (chip + 1) % chips, (chip + chips - 1) % chips, (chip + 2) % chips
        w1, w3, w2 = w_gate[0], w_up[0], w_down[0]

        def mate(v):
            return lax.ppermute(v, 'expert', to_mate)

        all_x = lax.all_gather(tok_x, 'expert')
        all_dy = lax.all_gather(grad_y, 'expert')

        route = jnp.concatenate([route_idx.astype(F32).T, route_gate.T], axis=0)
        every = lax.all_gather(route, 'expert').swapaxes(0, 1)
        idx, gates = every[:tops].astype(I32), every[tops:]
        expert_id = iota((experts, 1, 1), 0)
        taken = jnp.any(idx[None] == expert_id[:, None], axis=1)
        rank = count_before(taken)
        hot_id = expert_id % stride == 0
        kept = taken & (hot_id | (rank < cap))
        spot = jnp.where(kept, rank, -1)
        need = jnp.any(kept.reshape(chips, 2, group, toks), axis=1)
        single = jnp.sum(need.astype(I32), axis=0) == 1
        listed = jnp.where(need, count_before(need), -1)
        sizes = (jnp.sum(need.astype(I32), axis=2) + PIECE - 1) // PIECE * PIECE
        total = jnp.sum(sizes.reshape(chips, chips, 2), axis=2)

        def turn(table, by):
            return jnp.roll(table, -by, axis=-1)

        def hop(by):
            sel = (iota((chips, chips), 0) + by) % chips == iota((chips, chips), 1)
            return jnp.sum(jnp.where(sel, total, 0), axis=1)

        tries = 5 ** chips
        share = (iota((tries, chips), 0) // (5 ** iota((tries, chips), 1))) % 5
        go_up = hop(2)[None] * share // (4 * PIECE) * PIECE
        go_down = hop(2)[None] - go_up
        on_up = hop(1)[None] + go_up + turn(go_up, -1)
        on_down = hop(chips - 1)[None] + go_down + turn(go_down, 1)
        two_hop = jnp.max(jnp.maximum(go_up, go_down), axis=1)
        load = jnp.max(jnp.maximum(on_up, on_down), axis=1) + jnp.where(two_hop > small, 2 * place, 0)
        best = jnp.min(load)
        first_best = jnp.min(jnp.where(load == best, jnp.arange(tries, dtype=I32), tries))
        chosen = jnp.sum(jnp.where(iota((tries, 1), 0) == first_best, go_up, 0), axis=0)
        other = hop(2) - chosen
        full = jnp.any(taken & hot_id & (rank >= cap)) | (best > place)
        state = jnp.where(full, 2, jnp.where(best > 2 * small, 1, 0))
        state = lax.pmax(state.astype(I32), ('data', 'expert'))

        def gate_of(eid):
            return jnp.sum(jnp.where(idx == eid, gates, 0.0), axis=0)

        own_spot, mate_spot = pick(spot, me), pick(spot, me ^ 1)
        own_gate, mate_gate = gate_of(me), gate_of(me ^ 1)
        pad = jnp.zeros((group, toks), F32)
        send_info = jnp.stack([pick(listed, chip).astype(F32), own_spot.astype(F32), mate_spot.astype(F32),
                               jnp.where(single, own_gate, 1.0), jnp.where(single, mate_gate, 1.0), pad, pad, pad], axis=1)
        f_up, f_down = pick(chosen, chip), pick(other, chip)
        pass_up, pass_down = pick(chosen, down), pick(other, up)
        my_sizes = pick(sizes, chip)
        devs = jnp.stack([2 * to + k for to in (far, up, down) for k in range(2)])

        def lowest(at, ok):
            low = jnp.min(jnp.where(ok & (at >= 0), at, cap), axis=-1)
            return jnp.where(low < cap, jnp.minimum(low // PIECE * PIECE, cap - SPAN), -1)

        list_tile = (pick(listed, chip) // TILE)[None] == iota((tiles, 1, 1), 0)
        list_tile = list_tile & (pick(listed, chip) >= 0)[None]
        lows = jnp.stack([lowest(v[None], list_tile) for v in (own_spot, mate_spot)], axis=2)
        lows = lows.swapaxes(0, 1).reshape(group, 2 * tiles)
        low_rows = jnp.concatenate([lax.dynamic_slice_in_dim(lows, 2 * to, 2, 0) for to in (far, up, down)])

        def segments(size_of_stage):
            segs = []
            for to, lead, extra in ((far, 0, f_up), (up, f_up, pass_up), (down, f_down, pass_down)):
                for k in range(2):
                    size = pick(my_sizes, 2 * to + k)
                    segs.append(jnp.stack([size, jnp.asarray(lead, I32), extra, jnp.asarray(size_of_stage, I32)]))
                    lead = lead + size
            return jnp.stack(segs)

        tier_stage = jnp.where(state == 0, small, stage)
        segs = segments(tier_stage)

        def home(v):
            return lax.dynamic_slice_in_dim(v, 2 * chip, 2, 0)

        home_idx = [home(idx[j]) for j in range(tops)]
        home_gates = [home(gates[j]) for j in range(tops)]
        home_kept = home(jnp.sum(kept.astype(I32) * (1 << expert_id), axis=0))
        home_single = home(single.astype(I32)) > 0

        def listed_at(c):
            at = home(pick(listed, c))
            first = pick(pick(sizes, c), 2 * chip)
            return at >= 0, at + jnp.where(iota((2, 1), 0) == 1, first, 0)

        def weight_of(c):
            w = 0.0
            for j in range(tops):
                held = (home_kept >> home_idx[j]) % 2 == 1
                w = w + jnp.where((home_idx[j] // 2 == c) & held, home_gates[j], 0.0)
            return jnp.where(home_single, 1.0, w)

        far_ok, far_at = listed_at(far)
        far_cut = pick(chosen, far)
        far_by_up = jnp.where(far_ok & (far_at < far_cut), far_at, -1)
        far_by_down = jnp.where(far_ok & (far_at >= far_cut), far_at - far_cut, -1)
        home_spots = [home(own_spot), home(mate_spot)]
        weights = [weight_of(c) for c in (down, up, far)]
        own_lows = [lowest(v.reshape(2 * tiles, TILE), True) for v in home_spots]

        def arrival(size_of_stage):
            def near_spot(c, lead, passed):
                ok, at = listed_at(c)
                at = at + lead
                return jnp.where(ok, jnp.where(at >= size_of_stage, stage + at + passed - size_of_stage, at), -1)

            from_down = near_spot(down, pick(chosen, down), pick(chosen, far))
            from_up = near_spot(up, pick(other, up), pick(other, far))
            info = [v.astype(F32) for v in home_spots] + [home(own_gate), home(mate_gate)]
            info += [v.astype(F32) for v in (from_down, from_up, far_by_up, far_by_down)] + weights
            info = jnp.stack(info + [jnp.zeros((2, toks), F32)] * 5, axis=1)
            begins = []
            for near, by in ((from_down, far_by_up), (from_up, far_by_down)):
                begins.append(jnp.where((near >= 0) & (near < stage), near, place))
                begins.append(jnp.where(near >= stage, near - stage, place))
                begins.append(jnp.where(by >= 0, by, place))
            low = jnp.min(jnp.stack(begins).reshape(6, 2 * tiles, TILE), axis=2)
            low = jnp.where(low < place, jnp.minimum(low // PIECE * PIECE, size_of_stage - WINDOW), -1)
            return info, jnp.concatenate([low, jnp.stack(own_lows)]).T

        home_info, win = arrival(tier_stage)
        homes = jnp.stack([2 * chip, 2 * chip + 1])

        onehot_in = (own_spot[:, None, :] == iota((1, cap, 1), 1)).astype(BF)

        def columns(w, axis, mine):
            parts = jnp.split(w, 2, axis=axis)
            return jnp.where((core == 0) == mine, parts[0], parts[1])

        w2_halves = [columns(w2, 1, m) for m in (True, False)]
        w2t = row_major(w2.T)
        w13t_halves = [[row_major(columns(w, 0, m).T) for w in (w1, w3)] for m in (True, False)]
        counts = jnp.sum((own_spot >= 0).astype(I32), axis=1)
        pad = jnp.zeros((group, toks), F32)
        own_info = jnp.stack([own_spot.astype(F32), own_gate] + [pad] * 6, axis=1)
        rooms = [jnp.full((stage, half), jnp.where(state > 3 + k, 1.0, 0.0), BF) for k in range(8)]
        plan = (state, send_info, devs, segs, low_rows, home_info, win, homes, onehot_in, counts, own_info, w2_halves, w2t, w13t_halves, rooms)
        plan = lax.optimization_barrier(plan)
        all_x, plan = lax.optimization_barrier((all_x, plan))
        (state, send_info, devs, segs, low_rows, home_info, win, homes, onehot_in, counts, own_info, w2_halves, w2t, w13t_halves,
         rooms) = plan

        def take(onehot, tok, gate=None):
            got = dot('gcs,gsd->gcd', onehot, tok)
            return (got if gate is None else gate.reshape(group, cap, 1) * got).astype(BF).reshape(rows, dim)

        def up_front(x):
            pre_a = dot('cd,df->cf', x, w1).astype(BF)
            pre_b = dot('cd,df->cf', x, w3).astype(BF)
            pre_a, pre_b = lax.optimization_barrier((pre_a, pre_b))
            a = pre_a.astype(F32)
            hid = (a * jax.nn.sigmoid(a) * pre_b.astype(F32)).astype(BF)
            return pre_a, pre_b, hid

        def inner_grads(pre_a, pre_b, dh):
            dh = dh.astype(BF).astype(F32)
            a = pre_a.astype(F32)
            sig = jax.nn.sigmoid(a)
            da = (dh * pre_b.astype(F32) * (sig * (1.0 + a * (1.0 - sig)))).astype(BF)
            db = (dh * (a * sig)).astype(BF)
            return da, db

        any_spec = pl.BlockSpec(memory_space=pl.ANY)

        def packed(tables, segs, rooms, scaled):
            table_spec = pl.BlockSpec((1, cap, half), lambda g, dev, seg, low: (dev[g], 0, 0))
            res = pl.pallas_call(
                functools.partial(pack_kernel, scaled),
                grid_spec=pltpu.PrefetchScalarGridSpec(
                    num_scalar_prefetch=3, grid=(6,),
                    in_specs=[table_spec, table_spec, pl.BlockSpec((1, 8, toks), lambda g, dev, seg, low: (dev[g], 0, 0))] + [any_spec] * 4,
                    out_specs=[any_spec] * 4,
                    scratch_shapes=[pltpu.VMEM((2, TILE, half), BF), pltpu.SMEM((2,), I32),
                                    pltpu.SemaphoreType.DMA((2,))]),
                out_shape=[jax.ShapeDtypeStruct((stage, half), BF)] * 4,
                input_output_aliases={6 + k: k for k in range(4)},
                compiler_params=pltpu.CompilerParams(vmem_limit_bytes=VMEM_LIMIT),
                cost_estimate=pl.CostEstimate(flops=2 * rows * cap * half, bytes_accessed=12 * rows * half, transcendentals=0),
                name='pack',
            )(devs, segs, low_rows, *tables, send_info, *rooms)
            return res[:2], res[2:]

        def arrived(tables, info, win, got_up, got_down, scaled):
            table_spec = pl.BlockSpec((1, cap, half), lambda t, homes, win: (homes[t // tiles], 0, 0))
            info_spec = pl.BlockSpec((1, 16, TILE), lambda t, homes, win: (t // tiles, 0, t % tiles))
            return pl.pallas_call(
                functools.partial(arrive_kernel, scaled, stage),
                grid_spec=pltpu.PrefetchScalarGridSpec(
                    num_scalar_prefetch=2, grid=(2 * tiles,),
                    in_specs=[table_spec, table_spec, info_spec] + [any_spec] * 4,
                    out_specs=pl.BlockSpec((1, TILE, half), lambda t, homes, win: (t // tiles, t % tiles, 0)),
                    scratch_shapes=[pltpu.VMEM((TILE, half), F32), pltpu.VMEM((2, 6, SPAN, half), BF), pltpu.SemaphoreType.DMA((2, 6))]),
                out_shape=jax.ShapeDtypeStruct((2, toks, half), BF),
                compiler_params=pltpu.CompilerParams(vmem_limit_bytes=VMEM_LIMIT),
                cost_estimate=pl.CostEstimate(flops=2 * rows * cap * half, bytes_accessed=12 * rows * half, transcendentals=0),
                name='arrive',
            )(homes, win, *tables, info, *got_up, *got_down)

        def shift(up_rows, down_rows):
            got_up = lax.ppermute(up_rows, 'expert', to_next)
            got_down = lax.ppermute(down_rows, 'expert', to_prev)
            return got_up, got_down

        def second_rows(got, up_rows, down_rows):
            row = iota((up_rows.shape[0], 1), 0)
            return jnp.where(row < pass_up, got[0], up_rows), jnp.where(row < pass_down, got[1], down_rows)

        def whole(total):
            mine = jnp.where(core == 0, total[0], total[1])
            theirs = mate(jnp.where(core == 0, total[1], total[0]))
            return jnp.where(core == 0, jnp.concatenate([mine, theirs], axis=1), jnp.concatenate([theirs, mine], axis=1))

        def table(v):
            return v.reshape(group, cap, half)

        x = take(onehot_in, all_x)
        pre_a, pre_b, hid = up_front(x)
        theirs = dot('cf,fd->cd', hid, w2_halves[1]).astype(BF)
        out_got = mate(theirs)
        ours = dot('cf,fd->cd', after(hid, theirs), w2_halves[0]).astype(BF)
        out_tables = (table(ours), table(out_got))
        out_up, out_down = packed(out_tables, segs, rooms[:4], True)
        all_dy = after(all_dy, out_up, out_down)

        def block_spec(rows, width):
            return pl.BlockSpec((1, rows, width), lambda e, count: (e, 0, 0))

        def fixed_spec(w):
            return pl.BlockSpec(w.shape, lambda e, count: (0, 0), pipeline_mode=pl.Buffered(1))

        def inner_grads_of(dy):
            f = pre_a.shape[1]
            return pl.pallas_call(
                inner_kernel,
                grid_spec=pltpu.PrefetchScalarGridSpec(
                    num_scalar_prefetch=1, grid=(group,),
                    in_specs=[block_spec(8, toks), block_spec(toks, dim), fixed_spec(w2t), block_spec(cap, f), block_spec(cap, f)],
                    out_specs=[block_spec(cap, dim), block_spec(cap, f), block_spec(cap, f)]),
                out_shape=[jax.ShapeDtypeStruct((group, cap, n), BF) for n in (dim, f, f)],
                compiler_params=pltpu.CompilerParams(vmem_limit_bytes=VMEM_LIMIT),
                cost_estimate=pl.CostEstimate(flops=2 * rows * dim * (toks + f), bytes_accessed=2 * rows * dim * 4, transcendentals=rows * f),
                name='inner',
            )(counts, own_info, dy, w2t, pre_a.reshape(group, cap, f), pre_b.reshape(group, cap, f))

        def input_grad(da, db, k):
            w1t, w3t = w13t_halves[k]
            f = da.shape[2]
            return pl.pallas_call(
                input_kernel,
                grid_spec=pltpu.PrefetchScalarGridSpec(
                    num_scalar_prefetch=1, grid=(group,),
                    in_specs=[block_spec(cap, f), block_spec(cap, f), fixed_spec(w1t), fixed_spec(w3t)],
                    out_specs=block_spec(cap, half)),
                out_shape=jax.ShapeDtypeStruct((group, cap, half), BF),
                compiler_params=pltpu.CompilerParams(vmem_limit_bytes=VMEM_LIMIT),
                cost_estimate=pl.CostEstimate(flops=4 * rows * f * half, bytes_accessed=4 * rows * half, transcendentals=0),
                name='input_grad',
            )(counts, da, db, w1t, w3t)

        def rest(size):
            out_first = shift(out_up[0][:size], out_down[0][:size])
            g, da, db = inner_grads_of(all_dy)
            out_second = second_rows(after(out_first, da), out_up[1][:size], out_down[1][:size])
            out_last = shift(*out_second)
            da, db = after((da, db), *out_second)
            theirs = input_grad(da, db, 1)
            dx_got = mate(theirs)
            ours = input_grad(after(da, theirs), db, 0)
            dx_tables = (ours, dx_got)
            dx_up, dx_down = packed(dx_tables, segs, rooms[4:], False)
            dx_first = shift(dx_up[0][:size], dx_down[0][:size])
            out_first, out_last, da, db, g = after((out_first, out_last, da, db, g), dx_up, dx_down)
            f = da.shape[2]
            da, db, g = da.reshape(rows, f), db.reshape(rows, f), g.reshape(rows, dim)
            dw1 = dot('cd,cf->df', x, da)
            out_first, out_last = after((out_first, out_last), dw1[:8, :TILE])
            y = arrived(out_tables, home_info, win, (out_first[0], out_last[0]), (out_first[1], out_last[1]), True)
            y = whole(y)
            dx_second = second_rows(after(dx_first, y), dx_up[1][:size], dx_down[1][:size])
            dx_last = shift(*dx_second)
            db, hid_late = after((db, hid), *dx_second)
            dw3 = dot('cd,cf->df', x, db)
            dw2 = dot('cf,cd->fd', hid_late, g)
            gx = whole(arrived(dx_tables, home_info, win, (dx_first[0], dx_last[0]), (dx_first[1], dx_last[1]), False))
            return y, gx, row_major(dw1)[None], row_major(dw3)[None], row_major(dw2)[None]

        def general():
            my_rank, my_taken = pick(rank, me), pick(taken.astype(I32), me) > 0
            my_idx = route_idx.T
            home_rank = pick(jnp.moveaxis(rank, 1, 0), me)
            out_rank = jnp.stack([jnp.sum(jnp.where(my_idx[j] == expert_id[:, 0], home_rank, 0), axis=0) for j in range(tops)])
            out_hot = my_idx % stride == 0

            def one_pass(first):
                ok = my_taken & (my_rank >= first) & (my_rank < first + cap)
                ok_out = (out_rank >= first) & (out_rank < first + cap)
                if first:
                    ok = ok & (me % stride == 0)
                    ok_out = ok_out & out_hot
                onehot = jnp.where(ok, my_rank - first, -1)[:, None, :] == iota((1, cap, 1), 1)
                gate = jnp.sum(jnp.where(onehot, own_gate[:, None, :], 0.0), axis=2)
                onehot = onehot.astype(BF)
                goal = jnp.where(ok_out, my_idx * cap + out_rank - first, -1)
                onehot_out = (goal[:, :, None] == iota((1, 1, rows), 2)).astype(BF)

                def swap(r):
                    return lax.all_to_all(r.reshape(group, cap, dim), 'expert', 0, 0).reshape(rows, dim)

                x = take(onehot, all_x)
                pre_a, pre_b, hid = up_front(x)
                back = swap(dot('cf,fd->cd', hid, w2).astype(BF))
                g = lax.optimization_barrier(take(onehot, all_dy, gate))
                da, db = lax.optimization_barrier(inner_grads(pre_a, pre_b, dot('cd,fd->cf', g, w2)))
                dx = (dot('cf,df->cd', da, w1) + dot('cf,df->cd', db, w3)).astype(BF)
                back_dx = swap(after(dx, back))
                slots = dot('jtr,rd->jtd', onehot_out, back)
                y = jnp.sum(route_gate.T[:, :, None] * slots, axis=0)
                gx = dot('tr,rd->td', jnp.sum(onehot_out, axis=0), back_dx)
                return y, gx, dot('cd,cf->df', x, da), dot('cd,cf->df', x, db), dot('cf,cd->fd', hid, g)

            first = one_pass(0)
            second = one_pass(cap)
            sums = [u + v for u, v in zip(first, second)]
            return (sums[0].astype(BF), sums[1].astype(BF)) + tuple(v[None] for v in sums[2:])

        return lax.switch(state, [lambda: rest(small), lambda: rest(stage), general])

    return jax.shard_map(layer, mesh=mesh, in_specs=(tok_spec,) * 4 + (w_spec,) * 3, out_specs=(tok_spec,) * 5, check_vma=False)
```

profile of v0, /device:TPU:112, one launch (start us, length us, event | category | flops | bytes accessed | tf_op | source)
XLA Modules:
  0.0 962.6 jit_solution(16641309860999917487)
XLA Ops:
  8.9 24.7 %all-gather.3 = f32[8,4,768]{2,1,0:T(4,128)S(1)} all-gather(f32[1,4,768]{2,1,0:T(4,128)S(1)} %maximum_bitcast_fusion), channel_id=3, replica_groups=mesh['data'=2,'expert'=8] {'expert'}, dimensions={0}, use_global_device_ids=true | all-gather | bytes 110592 | tf_op jit(solution)/shard_map/all_gather | solution.py:271
  39.3 29.5 %pmax.7 = s32[]{:T(128)} all-reduce(s32[]{:T(128)S(6)} %select_n.772), channel_id=1, replica_groups=mesh['data'=2,'expert'=8] {'data','expert'}, use_global_device_ids=true, to_apply=%region_11.12 | all-reduce | flops 1 | bytes 8 | tf_op jit(solution)/shard_map/pmax | solution.py:306
  199.5 36.4 %all-gather.7.cloned.1.call-done = bf16[6144,4096]{1,0:T(8,128)(2,1)} async-done(((bf16[768,4096]{1,0:T(8,128)(2,1)}), bf16[6144,4096]{1,0:T(8,128)(2,1)}) %all-gather.7.cloned.1.call-update) | async-done | bytes 50331664 | tf_op jit(solution)/shard_map/all_gather | solution.py:267
  236.0 36.4 %convolution_convert_fusion.10 = bf16[8,384,4096]{2,1,0:T(8,128)(2,1)} fusion(bf16[8,384,768]{2,1,0:T(8,128)(2,1)} %fusion.41, bf16[8,768,4096]{2,1,0:T(8,128)(2,1)} %bitcast.410), kind=kOutput, calls=%fused_computation.121 | convolution fusion | flops 19339935744 | bytes 80216064 | tf_op jit(solution)/shard_map/gcs,gsd->gcd/dot_general | solution.py:22
  272.4 32.4 %convolution_convert_fusion.13 = bf16[3072,1024]{1,0:T(8,128)(2,1)S(1)} fusion(bf16[3072,4096]{1,0:T(8,128)(2,1)} %bitcast.415, bf16[1,4096,1024]{2,1,0:T(8,128)(2,1)} %param.15), kind=kOutput, calls=%fused_computation.131 | convolution fusion | flops 25772949504 | bytes 39845888 | tf_op jit(solution)/shard_map/cd,df->cf/dot_general | solution.py:22
  304.7 34.4 %convolution_convert_fusion.14 = bf16[3072,1024]{1,0:T(8,128)(2,1)S(1)} fusion(bf16[3072,4096]{1,0:T(8,128)(2,1)} %bitcast.416, bf16[1,4096,1024]{2,1,0:T(8,128)(2,1)} %param.14), kind=kOutput, calls=%fused_computation.132 | convolution fusion | flops 25772949504 | bytes 39845888 | tf_op jit(solution)/shard_map/cd,df->cf/dot_general | solution.py:22
  345.9 16.4 %convolution_convert_fusion.12 = bf16[3072,2048]{1,0:T(8,128)(2,1)} fusion(bf16[3072,1024]{1,0:T(8,128)(2,1)S(1)} %fusion.40, bf16[1024,2048]{0,1:T(8,128)(2,1)S(1)} %copy-done.21), kind=kOutput, calls=%fused_computation.128 | convolution fusion | flops 12891193344 | bytes 23068672 | tf_op jit(solution)/shard_map/cf,fd->cd/dot_general | solution.py:22
  362.9 19.5 %convolution_convert_fusion.11 = bf16[3072,2048]{1,0:T(8,128)(2,1)} fusion(bf16[3072,1024]{1,0:T(8,128)(2,1)} %copy-done.15, bf16[1024,2048]{0,1:T(8,128)(2,1)} %get-tuple-element.396), kind=kOutput, calls=%fused_computation.127 | convolution fusion | flops 12891193344 | bytes 23068672 | tf_op jit(solution)/shard_map/cf,fd->cd/dot_general | solution.py:22
  384.0 24.8 %pack.5 = (bf16[1136,2048]{1,0:T(8,128)(2,1)}, bf16[1136,2048]{1,0:T(8,128)(2,1)}, bf16[1136,2048]{1,0:T(8,128)(2,1)}, bf16[1136,2048]{1,0:T(8,128)(2,1)}) custom-call(s32[6]{0:T(128)S(1)} %copy-done.52, s32[6,4]{1,0:T(8,128)S(1)} %copy-done.38, s32[6,12]{1,0:T(8,128)S(1)} %copy-done.39, ...), custom_call_target="tpu_custom_call", output_to_operand_aliasing={{0}: (6, {}), {1}: (7, {}), {2}: (8, {}), {3}: (9, {})} | custom-call | flops 4831838208 | bytes 75497472 | tf_op jit(solution)/shard_map/pack/pallas_call | solution.py:437
  408.8 51.2 %all-gather.9.cloned.1.call-done = bf16[6144,4096]{1,0:T(8,128)(2,1)} async-done(((bf16[768,4096]{1,0:T(8,128)(2,1)}), bf16[6144,4096]{1,0:T(8,128)(2,1)}) %all-gather.9.cloned.1.call-update) | async-done | bytes 50331664 | tf_op jit(solution)/shard_map/all_gather | solution.py:268
  460.7 494.8 %conditional.1 = (bf16[768,4096]{1,0:T(8,128)(2,1)}, bf16[768,4096]{1,0:T(8,128)(2,1)}, f32[1,4096,1024]{2,1,0:T(8,128)}, f32[1,4096,1024]{2,1,0:T(8,128)}, f32[1,1024,4096]{2,1,0:T(8,128)}) conditional(s32[]{:T(128)} %clamp.3, (s32[]{:T(128)}, bf16[1136,2048]{1,0:T(8,128)(2,1)}, bf16[1136,2048]{1,0:T(8,128)(2,1)}, s32[]{:T(128)}, ...), branch_computations={%region_49.50_spmd, %region_50.51_spmd, %region_51.63_spmd} | conditional | flops 657602379776 | bytes 2084082560 | solution.py:596
  473.8 43.4 %inner.2 = (bf16[8,384,4096]{2,1,0:T(8,128)(2,1)}, bf16[8,384,1024]{2,1,0:T(8,128)(2,1)}, bf16[8,384,1024]{2,1,0:T(8,128)(2,1)}) custom-call(s32[8]{0:T(128)S(1)} %get-tuple-element.162.count_ref, f32[8,8,768]{2,1,0:T(8,128)S(1)} %copy-done.34, bf16[8,768,4096]{2,1,0:T(8,128)(2,1)} %get-tuple-element.164.dy, bf16[4096,1024]{1,0:T(8,128)(2,1)S(1)} %copy-done.1, ...), custom_call_target="tpu_custom_call" | custom-call | flops 45097156608 | bytes 100663296 | tf_op jit(solution)/shard_map/cond/branch_0_fun/inner/pallas_call | solution.py:503
  517.3 25.1 %collective-permute-done.up1 = bf16[832,2048]{1,0:T(8,128)(2,1)S(1)} collective-permute-done((bf16[832,2048]{1,0:T(8,128)(2,1)}, bf16[832,2048]{1,0:T(8,128)(2,1)S(1)}, u32[]{:S(2)}, u32[]{:S(2)}) %collective-permute-start) | collective-permute-done | bytes 3407904 | tf_op jit(solution)/shard_map/cond/branch_0_fun/ppermute | solution.py:470
  555.7 22.0 %input_grad.4 = bf16[8,384,2048]{2,1,0:T(8,128)(2,1)} custom-call(s32[8]{0:T(128)S(1)} %get-tuple-element.162.count_ref, bf16[8,384,1024]{2,1,0:T(8,128)(2,1)} %get-tuple-element.205.da, bf16[8,384,1024]{2,1,0:T(8,128)(2,1)} %get-tuple-element.207.db, bf16[1024,2048]{1,0:T(8,128)(2,1)S(1)} %copy-done.20, bf16[1024,2048]{1,0:T(8,128)(2,1)S(1)} %copy-done.18), custom_call_target="tpu_custom_call" | custom-call | flops 25769803776 | bytes 25165824 | tf_op jit(solution)/shard_map/cond/branch_0_fun/input_grad/pallas_call | solution.py:518
  582.9 24.6 %input_grad.5.tab0 = bf16[8,384,2048]{2,1,0:T(8,128)(2,1)} custom-call(s32[8]{0:T(128)S(1)} %get-tuple-element.162.count_ref, bf16[8,384,1024]{2,1,0:T(8,128)(2,1)} %get-tuple-element.205.da, bf16[8,384,1024]{2,1,0:T(8,128)(2,1)} %get-tuple-element.207.db, bf16[1024,2048]{1,0:T(8,128)(2,1)} %get-tuple-element.184.w1t, bf16[1024,2048]{1,0:T(8,128)(2,1)} %get-tuple-element.185.w3t), custom_call_target="tpu_custom_call" | custom-call | flops 25769803776 | bytes 25165824 | tf_op jit(solution)/shard_map/cond/branch_0_fun/input_grad/pallas_call | solution.py:518
  607.5 23.5 %pack.3 = (bf16[1136,2048]{1,0:T(8,128)(2,1)}, bf16[1136,2048]{1,0:T(8,128)(2,1)}, bf16[1136,2048]{1,0:T(8,128)(2,1)}, bf16[1136,2048]{1,0:T(8,128)(2,1)}) custom-call(s32[6]{0:T(128)S(1)} %get-tuple-element.178.dev_ref, s32[6,4]{1,0:T(8,128)S(1)} %get-tuple-element.179.seg_ref, ...), custom_call_target="tpu_custom_call", output_to_operand_aliasing={{0}: (6, {}), {1}: (7, {}), {2}: (8, {}), {3}: (9, {})} | custom-call | flops 4831838208 | bytes 75497472 | tf_op jit(solution)/shard_map/cond/branch_0_fun/pack/pallas_call | solution.py:437
  631.0 26.4 %collective-permute-done.2.up2 = bf16[832,2048]{1,0:T(8,128)(2,1)} collective-permute-done((bf16[832,2048]{1,0:T(8,128)(2,1)}, bf16[832,2048]{1,0:T(8,128)(2,1)}, u32[]{:S(2)}, u32[]{:S(2)}) %collective-permute-start.2) | collective-permute-done | bytes 3407904 | tf_op jit(solution)/shard_map/cond/branch_0_fun/ppermute | solution.py:470
  657.4 19.3 %arrive.4 = bf16[2,768,2048]{2,1,0:T(8,128)(2,1)} custom-call(s32[2]{0:T(128)S(1)} %get-tuple-element.154.home_ref, s32[12,8]{1,0:T(8,128)S(1)} %copy.145.win_ref, bf16[8,384,2048]{2,1,0:T(8,128)(2,1)} %get-tuple-element.156.tab0, bf16[8,384,2048]{2,1,0:T(8,128)(2,1)} %get-tuple-element.157.tab1, f32[2,16,768]{2,1,0:T(8,128)S(1)} %get-tuple-element.158.info, ...), custom_call_target="tpu_custom_call" | custom-call | flops 4831838208 | bytes 75497472 | tf_op jit(solution)/shard_map/cond/branch_0_fun/arrive/pallas_call | solution.py:456
  700.8 64.6 %collective-permute-done.7.down1 = bf16[832,2048]{1,0:T(8,128)(2,1)S(1)} collective-permute-done((bf16[832,2048]{1,0:T(8,128)(2,1)S(1)}, bf16[832,2048]{1,0:T(8,128)(2,1)S(1)}, u32[]{:S(2)}, u32[]{:S(2)}) %collective-permute-start.7) | collective-permute-done | bytes 3407904 | tf_op jit(solution)/shard_map/cond/branch_0_fun/ppermute | solution.py:471
  776.6 33.8 %convolution_bitcast_fusion.2 = f32[1,4096,1024]{2,1,0:T(8,128)} fusion(bf16[3072,1024]{1,0:T(8,128)(2,1)} %bitcast.435, bf16[3072,4096]{1,0:T(8,128)(2,1)} %get-tuple-element.206), kind=kOutput, calls=%fused_computation.2 | convolution fusion | flops 25769803776 | bytes 48234496 | tf_op jit(solution)/shard_map/cond/branch_0_fun/cd,cf->df/dot_general | solution.py:22
  810.4 38.5 %collective-permute-done.8.up2 = bf16[832,2048]{1,0:T(8,128)(2,1)S(1)} collective-permute-done((bf16[832,2048]{1,0:T(8,128)(2,1)}, bf16[832,2048]{1,0:T(8,128)(2,1)S(1)}, u32[]{:S(2)}, u32[]{:S(2)}) %collective-permute-start.8) | collective-permute-done | bytes 3407904 | tf_op jit(solution)/shard_map/cond/branch_0_fun/ppermute | solution.py:470
  852.5 19.2 %arrive.5 = bf16[2,768,2048]{2,1,0:T(8,128)(2,1)} custom-call(s32[2]{0:T(128)S(1)} %get-tuple-element.154.home_ref, s32[12,8]{1,0:T(8,128)S(1)} %copy.145.win_ref, bf16[8,384,2048]{2,1,0:T(8,128)(2,1)} %input_grad.5.tab0, bf16[8,384,2048]{2,1,0:T(8,128)(2,1)} %collective-permute-done.4.tab1, f32[2,16,768]{2,1,0:T(8,128)S(1)} %get-tuple-element.158.info, ...), custom_call_target="tpu_custom_call" | custom-call | flops 4831838208 | bytes 75497472 | tf_op jit(solution)/shard_map/cond/branch_0_fun/arrive/pallas_call | solution.py:456
  876.0 34.2 %convolution_bitcast_fusion.1 = f32[1,4096,1024]{2,1,0:T(8,128)} fusion(bf16[3072,1024]{1,0:T(8,128)(2,1)} %bitcast.433, bf16[3072,4096]{1,0:T(8,128)(2,1)} %get-tuple-element.206), kind=kOutput, calls=%fused_computation.1 | convolution fusion | flops 25769803776 | bytes 48234496 | tf_op jit(solution)/shard_map/cond/branch_0_fun/cd,cf->df/dot_general | solution.py:22
  910.2 31.8 %convolution_bitcast_fusion = f32[1,1024,4096]{2,1,0:T(8,128)} fusion(bf16[3072,1024]{1,0:T(8,128)(2,1)S(1)} %bitcast.399, bf16[3072,4096]{1,0:T(8,128)(2,1)} %bitcast.419), kind=kOutput, calls=%fused_computation | convolution fusion | flops 25769803776 | bytes 48234496 | tf_op jit(solution)/shard_map/cond/branch_0_fun/cf,cd->fd/dot_general | solution.py:22
  (277 shorter events, 216.0 us)
Async XLA Ops:
  7.2 228.8 %all-gather.7.cloned.1.call-start = ((), (), s32[]{:S(2)}) async-start(), calls=%async_computation.4 | async-start | bytes 56623104 | tf_op jit(solution)/shard_map/all_gather | solution.py:267
  8.0 452.1 %all-gather.9.cloned.1.call-start = ((), (), s32[]{:S(2)}) async-start(), calls=%async_computation.5 | async-start | bytes 56623104 | tf_op jit(solution)/shard_map/all_gather | solution.py:268
  33.7 117.3 %copy-start.30 = (f32[8,768]{1,0:T(8,128)}, f32[8,768]{1,0:T(8,128)S(1)}, u32[]{:S(2)}) copy-start(f32[8,768]{1,0:T(8,128)S(1)} %get-tuple-element.624) | copy-start | bytes 73732
  33.8 65.1 %copy-start.29 = (pred[8,8,768]{2,1,0:T(8,128)(4,1)}, pred[8,8,768]{2,1,0:T(8,128)(4,1)S(1)}, u32[]{:S(2)}) copy-start(pred[8,8,768]{2,1,0:T(8,128)(4,1)S(1)} %fusion.56) | copy-start | bytes 147460
  362.2 21.7 %collective-permute-start.22 = (bf16[3072,2048]{1,0:T(8,128)(2,1)}, bf16[3072,2048]{1,0:T(8,128)(2,1)}, u32[]{:S(2)}, u32[]{:S(2)}) collective-permute-start(bf16[3072,2048]{1,0:T(8,128)(2,1)} %convolution_convert_fusion.12), channel_id=1, source_target_pairs={{0,1},{1,0},{2,3},{3,2},{4,5},{5,4},{6,7},{7,6},{8,9},{9,8},{10,11... | collective-permute-start | bytes 37748744 | tf_op jit(solution)/shard_map/ppermute | solution.py:265
  384.0 76.7 %copy-start.27 = (f32[2,16,768]{2,1,0:T(8,128)S(1)}, f32[2,16,768]{2,1,0:T(8,128)}, u32[]{:S(2)}) copy-start(f32[2,16,768]{2,1,0:T(8,128)} %stack.257) | copy-start | bytes 294916
  384.0 76.7 %copy-start.43 = (s32[12,8]{0,1:T(8,128)S(1)}, s32[12,8]{0,1:T(8,128)}, u32[]{:S(2)}) copy-start(s32[12,8]{0,1:T(8,128)} %add_bitcast_fusion.4) | copy-start | bytes 1156
  384.0 76.7 %copy-start.51 = (s32[2]{0:T(128)S(1)}, s32[2]{0:T(128)}, u32[]{:S(2)}) copy-start(s32[2]{0:T(128)} %pad_add_fusion.2) | copy-start | bytes 28
  384.0 76.7 %copy-start.56 = (s32[8]{0:T(128)S(1)}, s32[8]{0:T(128)}, u32[]{:S(2)}) copy-start(s32[8]{0:T(128)} %get-tuple-element.404) | copy-start | bytes 100
  465.0 77.3 %collective-permute-start = (bf16[832,2048]{1,0:T(8,128)(2,1)}, bf16[832,2048]{1,0:T(8,128)(2,1)S(1)}, u32[]{:S(2)}, u32[]{:S(2)}) collective-permute-start(bf16[832,2048]{1,0:T(8,128)(2,1)} %slice.76), channel_id=1, source_target_pairs={{0,2},{1,3},{2,4},{3,5},{4,6},{5,7},{6,0},{7,1},{8,10},{9,11},{10,... | collective-permute-start | bytes 10223624 | tf_op jit(solution)/shard_map/cond/branch_0_fun/ppermute | solution.py:470
  469.6 76.3 %collective-permute-start.1 = (bf16[832,2048]{1,0:T(8,128)(2,1)}, bf16[832,2048]{1,0:T(8,128)(2,1)}, u32[]{:S(2)}, u32[]{:S(2)}) collective-permute-start(bf16[832,2048]{1,0:T(8,128)(2,1)} %slice.77), channel_id=1, source_target_pairs={{0,6},{1,7},{2,0},{3,1},{4,2},{5,3},{6,4},{7,5},{8,14},{9,15},{10,... | collective-permute-start | bytes 10223624 | tf_op jit(solution)/shard_map/cond/branch_0_fun/ppermute | solution.py:471
  577.7 29.9 %collective-permute-start.4 = (bf16[8,384,2048]{2,1,0:T(8,128)(2,1)}, bf16[8,384,2048]{2,1,0:T(8,128)(2,1)}, u32[]{:S(2)}, u32[]{:S(2)}) collective-permute-start(bf16[8,384,2048]{2,1,0:T(8,128)(2,1)} %input_grad.4), channel_id=1, source_target_pairs={{0,1},{1,0},{2,3},{3,2},{4,5},{5,4},{6,7},{7,6},{8,9},{9,8},{10,11... | collective-permute-start | bytes 37748744 | tf_op jit(solution)/shard_map/cond/branch_0_fun/ppermute | solution.py:265
  577.7 79.8 %collective-permute-start.2 = (bf16[832,2048]{1,0:T(8,128)(2,1)}, bf16[832,2048]{1,0:T(8,128)(2,1)}, u32[]{:S(2)}, u32[]{:S(2)}) collective-permute-start(bf16[832,2048]{1,0:T(8,128)(2,1)} %slice_select_fusion.3), channel_id=1, source_target_pairs={{0,2},{1,3},{2,4},{3,5},{4,6},{5,7},{6,0},{7,1},{8,10},{9,11},{10,... | collective-permute-start | bytes 10223624 | tf_op jit(solution)/shard_map/cond/branch_0_fun/ppermute | solution.py:470
  577.7 79.8 %collective-permute-start.3 = (bf16[832,2048]{1,0:T(8,128)(2,1)}, bf16[832,2048]{1,0:T(8,128)(2,1)}, u32[]{:S(2)}, u32[]{:S(2)}) collective-permute-start(bf16[832,2048]{1,0:T(8,128)(2,1)} %slice_select_fusion.2), channel_id=1, source_target_pairs={{0,6},{1,7},{2,0},{3,1},{4,2},{5,3},{6,4},{7,5},{8,14},{9,15},{10,... | collective-permute-start | bytes 10223624 | tf_op jit(solution)/shard_map/cond/branch_0_fun/ppermute | solution.py:471
  680.0 12.7 %collective-permute-start.5 = (bf16[768,2048]{1,0:T(8,128)(2,1)S(1)}, bf16[768,2048]{1,0:T(8,128)(2,1)}, u32[]{:S(2)}, u32[]{:S(2)}) collective-permute-start(bf16[768,2048]{1,0:T(8,128)(2,1)S(1)} %get-tuple-element.676), channel_id=1, source_target_pairs={{0,1},{1,0},{2,3},{3,2},{4,5},{5,4},{6,7},{7,6},{8,9},{9,8},{10,11... | collective-permute-start | bytes 9437192 | tf_op jit(solution)/shard_map/cond/branch_0_fun/ppermute | solution.py:265
  681.2 87.7 %slice-start.4 = ((s8[4653056]{0:T(1024)(128)(4,1)}), s8[4194304]{0:T(1024)(128)(4,1)S(1)}, s32[]{:S(2)}) async-start(s8[4653056]{0:T(1024)(128)(4,1)} %bitcast.380), calls=%async_computation.10 | async-start | bytes 8388608 | tf_op jit(solution)/shard_map/cond
  683.6 81.9 %collective-permute-start.7 = (bf16[832,2048]{1,0:T(8,128)(2,1)S(1)}, bf16[832,2048]{1,0:T(8,128)(2,1)S(1)}, u32[]{:S(2)}, u32[]{:S(2)}) collective-permute-start(bf16[832,2048]{1,0:T(8,128)(2,1)S(1)} %slice.83), channel_id=1, source_target_pairs={{0,6},{1,7},{2,0},{3,1},{4,2},{5,3},{6,4},{7,5},{8,14},{9,15},{10,... | collective-permute-start | bytes 10223624 | tf_op jit(solution)/shard_map/cond/branch_0_fun/ppermute | solution.py:471
  692.7 76.2 %collective-permute-start.6 = (bf16[832,2048]{1,0:T(8,128)(2,1)S(1)}, bf16[832,2048]{1,0:T(8,128)(2,1)S(1)}, u32[]{:S(2)}, u32[]{:S(2)}) collective-permute-start(bf16[832,2048]{1,0:T(8,128)(2,1)S(1)} %slice.82), channel_id=1, source_target_pairs={{0,2},{1,3},{2,4},{3,5},{4,6},{5,7},{6,0},{7,1},{8,10},{9,11},{10,... | collective-permute-start | bytes 10223624 | tf_op jit(solution)/shard_map/cond/branch_0_fun/ppermute | solution.py:470
  692.7 78.5 %slice-start = ((s8[4653056]{0:T(1024)(128)(4,1)}), s8[4194304]{0:T(1024)(128)(4,1)S(1)}, s32[]{:S(2)}) async-start(s8[4653056]{0:T(1024)(128)(4,1)} %bitcast.376), calls=%async_computation.6 | async-start | bytes 8388608 | tf_op jit(solution)/shard_map/cond
  692.7 76.2 %slice-start.5 = ((s8[4653056]{0:T(1024)(128)(4,1)}), s8[458752]{0:T(1024)(128)(4,1)S(1)}, s32[]{:S(2)}) async-start(s8[4653056]{0:T(1024)(128)(4,1)} %bitcast.380), calls=%async_computation.11 | async-start | bytes 917504 | tf_op jit(solution)/shard_map/cond
  692.8 78.4 %slice-start.1 = ((s8[4653056]{0:T(1024)(128)(4,1)}), s8[458752]{0:T(1024)(128)(4,1)S(1)}, s32[]{:S(2)}) async-start(s8[4653056]{0:T(1024)(128)(4,1)} %bitcast.376), calls=%async_computation.7 | async-start | bytes 917504 | tf_op jit(solution)/shard_map/cond
  773.4 75.5 %collective-permute-start.8 = (bf16[832,2048]{1,0:T(8,128)(2,1)}, bf16[832,2048]{1,0:T(8,128)(2,1)S(1)}, u32[]{:S(2)}, u32[]{:S(2)}) collective-permute-start(bf16[832,2048]{1,0:T(8,128)(2,1)} %slice_select_fusion.1), channel_id=1, source_target_pairs={{0,2},{1,3},{2,4},{3,5},{4,6},{5,7},{6,0},{7,1},{8,10},{9,11},{10,... | collective-permute-start | bytes 10223624 | tf_op jit(solution)/shard_map/cond/branch_0_fun/ppermute | solution.py:470
  773.4 75.5 %collective-permute-start.9 = (bf16[832,2048]{1,0:T(8,128)(2,1)}, bf16[832,2048]{1,0:T(8,128)(2,1)S(1)}, u32[]{:S(2)}, u32[]{:S(2)}) collective-permute-start(bf16[832,2048]{1,0:T(8,128)(2,1)} %slice_select_fusion), channel_id=1, source_target_pairs={{0,6},{1,7},{2,0},{3,1},{4,2},{5,3},{6,4},{7,5},{8,14},{9,15},{10,... | collective-permute-start | bytes 10223624 | tf_op jit(solution)/shard_map/cond/branch_0_fun/ppermute | solution.py:471
  876.0 66.1 %collective-permute-start.10 = (bf16[768,2048]{1,0:T(8,128)(2,1)}, bf16[768,2048]{1,0:T(8,128)(2,1)S(1)}, u32[]{:S(2)}, u32[]{:S(2)}) collective-permute-start(bf16[768,2048]{1,0:T(8,128)(2,1)} %get-tuple-element.674), channel_id=1, source_target_pairs={{0,1},{1,0},{2,3},{3,2},{4,5},{5,4},{6,7},{7,6},{8,9},{9,8},{10,11... | collective-permute-start | bytes 9437192 | tf_op jit(solution)/shard_map/cond/branch_0_fun/ppermute | solution.py:265
  (26 other events, 338.7 us)
Sparse Core Ops, SparseCore 0:
  9.6 226.2 all-gather.6
  237.5 222.5 all-gather.8
where the time goes:
time: 971 us; the launch traced here: 963 us
  waiting for transfers between devices  252 us (26%)
  matrix products  239 us (25%)
  Pallas kernels  177 us (18%)
  local copies, waits for them, and re-layouts  101 us (10%)
  other arithmetic  83.4 us (9%)
  blocking collectives  54.1 us (6%)
  between operations  25.2 us (3%)
  starting transfers between devices  20.9 us (2%)
    dot_general x10, matrix products, dot(): return jnp.einsum(form, a, b, preferred_element_type=F32)  239 us
    ppermute x4, waiting for transfers between devices, shift(): got_up = lax.ppermute(up_rows, 'expert', to_next)  93.4 us
    ppermute x4, waiting for transfers between devices, shift(): got_down = lax.ppermute(down_rows, 'expert', to_prev)  68.2 us
    all_gather x1, waiting for transfers between devices, layer(): all_dy = lax.all_gather(grad_y, 'expert')  51.2 us
    pallas_call x2, Pallas kernels, packed(): pl.pallas_call(functools.partial(pack_kernel, scaled), grid_spec=pltpu.Pr...  48.3 us
    pallas_call x2, Pallas kernels, input_grad(): pl.pallas_call(input_kernel, grid_spec=pltpu.PrefetchScalarGridSpec(num_s...  46.6 us
    unnamed x55, local copies, waits for them, and re-layouts  46.4 us
    pallas_call x1, Pallas kernels, inner_grads_of(): pl.pallas_call(inner_kernel, grid_spec=pltpu.PrefetchScalarGridSpec(num_s...  43.4 us
  transfers between devices with their start and end apart: 14, of which 9 were waited for; matrix products, arithmetic and copies ran while one was open for 40% of the time, Pallas kernels for 12%

commit v1 on v0

--- a/solution.py
+++ b/solution.py
@@ -46,7 +46,7 @@
 
 
 def pack_kernel(scaled, dev_ref, seg_ref, low_ref, tab0, tab1, info, *refs):
-    outs, (buf, pend, sem) = (refs[4:6], refs[6:8]), refs[8:]
+    outs, (buf, pend, sem) = (refs[0:2], refs[2:4]), refs[4:]
     g = pl.program_id(0)
     toks = info.shape[2]
     length, start, extra, stage = [seg_ref[g, k] for k in range(4)]
@@ -177,13 +177,25 @@
             acc[...] = acc[...] + (part * column(weight) if scaled else part)
 
     acc[...] = jnp.zeros_like(acc)
+    count = len(windows)
     for k, tab in enumerate((tab0, tab1)):
-        low = win_ref[t, len(windows) + k]
+        low = win_ref[t, count + k]
         add(low, 0, k, 2 + k, lambda tab=tab, low=low: tab[0, pl.ds(pl.multiple_of(low, PIECE), SPAN)])
     copies(t, lambda c: c.wait())
     slot = lax.rem(t, 2)
+
+    def arrived_rows(w):
+        used = (win_ref[t, count + 2 + w] - win_ref[t, w] + PIECE - 1) // PIECE
+
+        def clear(p, carry):
+            wbuf[slot, w, pl.ds(pl.multiple_of(p * PIECE, PIECE), PIECE)] = jnp.zeros((PIECE, wbuf.shape[3]), BF)
+            return carry
+
+        lax.fori_loop(used, WINDOW // PIECE, clear, 0)
+        return wbuf[slot, w]
+
     for w, (spot, weight, base) in enumerate(((4, 8, 0), (4, 8, second), (6, 10, 0), (5, 9, 0), (5, 9, second), (7, 10, 0))):
-        add(win_ref[t, w], base, spot, weight, lambda w=w: wbuf[slot, w])
+        add(win_ref[t, w], base, spot, weight, lambda w=w: arrived_rows(w))
     out[0] = acc[...].astype(BF)
 
 
@@ -253,8 +265,8 @@
         rows = group * cap
         half = dim // 2
         tiles = toks // TILE
-        small = toks * 13 // 12 // PIECE * PIECE
-        stage = toks * 71 // 48 // PIECE * PIECE
+        tiers = [toks * n // 48 for n in (44, 49, 55, 71)]
+        stage = tiers[-1]
         place = 2 * stage
         me = lax.axis_index('expert')
         chip, core = me // 2, me % 2
@@ -283,27 +295,28 @@
         total = jnp.sum(sizes.reshape(chips, chips, 2), axis=2)
 
         def turn(table, by):
-            return jnp.roll(table, -by, axis=-1)
+            return jnp.roll(table, -by, axis=0)
 
         def hop(by):
             sel = (iota((chips, chips), 0) + by) % chips == iota((chips, chips), 1)
             return jnp.sum(jnp.where(sel, total, 0), axis=1)
 
-        tries = 5 ** chips
-        share = (iota((tries, chips), 0) // (5 ** iota((tries, chips), 1))) % 5
-        go_up = hop(2)[None] * share // (4 * PIECE) * PIECE
-        go_down = hop(2)[None] - go_up
-        on_up = hop(1)[None] + go_up + turn(go_up, -1)
-        on_down = hop(chips - 1)[None] + go_down + turn(go_down, 1)
-        two_hop = jnp.max(jnp.maximum(go_up, go_down), axis=1)
-        load = jnp.max(jnp.maximum(on_up, on_down), axis=1) + jnp.where(two_hop > small, 2 * place, 0)
+        parts = 8
+        tries = (parts + 1) ** chips
+        share = (iota((chips, tries), 1) // ((parts + 1) ** iota((chips, tries), 0))) % (parts + 1)
+        two_hops = hop(2)[:, None]
+        go_up = two_hops * share // (parts * PIECE) * PIECE
+        go_down = two_hops - go_up
+        on_up = hop(1)[:, None] + go_up + turn(go_up, -1)
+        on_down = hop(chips - 1)[:, None] + go_down + turn(go_down, 1)
+        load = jnp.max(jnp.maximum(jnp.maximum(on_up, on_down), 2 * jnp.maximum(go_up, go_down)), axis=0)
         best = jnp.min(load)
         first_best = jnp.min(jnp.where(load == best, jnp.arange(tries, dtype=I32), tries))
-        chosen = jnp.sum(jnp.where(iota((tries, 1), 0) == first_best, go_up, 0), axis=0)
+        chosen = jnp.sum(jnp.where(iota((1, tries), 1) == first_best, go_up, 0), axis=1)
         other = hop(2) - chosen
-        full = jnp.any(taken & hot_id & (rank >= cap)) | (best > place)
-        state = jnp.where(full, 2, jnp.where(best > 2 * small, 1, 0))
-        state = lax.pmax(state.astype(I32), ('data', 'expert'))
+        full = jnp.any(taken & hot_id & (rank >= cap))
+        state = sum([(best > 2 * size).astype(I32) for size in tiers])
+        state = lax.pmax(jnp.where(full, len(tiers), state), ('data', 'expert'))
 
         def gate_of(eid):
             return jnp.sum(jnp.where(idx == eid, gates, 0.0), axis=0)
@@ -337,7 +350,7 @@
                     lead = lead + size
             return jnp.stack(segs)
 
-        tier_stage = jnp.where(state == 0, small, stage)
+        tier_stage = sum([jnp.where(state == k, size, 0) for k, size in enumerate(tiers)]) + jnp.where(state == len(tiers), stage, 0)
         segs = segments(tier_stage)
 
         def home(v):
@@ -384,9 +397,11 @@
                 begins.append(jnp.where((near >= 0) & (near < stage), near, place))
                 begins.append(jnp.where(near >= stage, near - stage, place))
                 begins.append(jnp.where(by >= 0, by, place))
-            low = jnp.min(jnp.stack(begins).reshape(6, 2 * tiles, TILE), axis=2)
+            begins = jnp.stack(begins).reshape(6, 2 * tiles, TILE)
+            low = jnp.min(begins, axis=2)
+            end = jnp.max(jnp.where(begins < place, begins, -1), axis=2) + 1
             low = jnp.where(low < place, jnp.minimum(low // PIECE * PIECE, size_of_stage - WINDOW), -1)
-            return info, jnp.concatenate([low, jnp.stack(own_lows)]).T
+            return info, jnp.concatenate([low, jnp.stack(own_lows), end]).T
 
         home_info, win = arrival(tier_stage)
         homes = jnp.stack([2 * chip, 2 * chip + 1])
@@ -403,12 +418,10 @@
         counts = jnp.sum((own_spot >= 0).astype(I32), axis=1)
         pad = jnp.zeros((group, toks), F32)
         own_info = jnp.stack([own_spot.astype(F32), own_gate] + [pad] * 6, axis=1)
-        rooms = [jnp.full((stage, half), jnp.where(state > 3 + k, 1.0, 0.0), BF) for k in range(8)]
-        plan = (state, send_info, devs, segs, low_rows, home_info, win, homes, onehot_in, counts, own_info, w2_halves, w2t, w13t_halves, rooms)
+        plan = (state, send_info, devs, segs, low_rows, home_info, win, homes, onehot_in, counts, own_info, w2_halves, w2t, w13t_halves)
         plan = lax.optimization_barrier(plan)
         all_x, plan = lax.optimization_barrier((all_x, plan))
-        (state, send_info, devs, segs, low_rows, home_info, win, homes, onehot_in, counts, own_info, w2_halves, w2t, w13t_halves,
-         rooms) = plan
+        (state, send_info, devs, segs, low_rows, home_info, win, homes, onehot_in, counts, own_info, w2_halves, w2t, w13t_halves) = plan
 
         def take(onehot, tok, gate=None):
             got = dot('gcs,gsd->gcd', onehot, tok)
@@ -432,22 +445,21 @@
 
         any_spec = pl.BlockSpec(memory_space=pl.ANY)
 
-        def packed(tables, segs, rooms, scaled):
+        def packed(tables, size, scaled):
             table_spec = pl.BlockSpec((1, cap, half), lambda g, dev, seg, low: (dev[g], 0, 0))
             res = pl.pallas_call(
                 functools.partial(pack_kernel, scaled),
                 grid_spec=pltpu.PrefetchScalarGridSpec(
                     num_scalar_prefetch=3, grid=(6,),
-                    in_specs=[table_spec, table_spec, pl.BlockSpec((1, 8, toks), lambda g, dev, seg, low: (dev[g], 0, 0))] + [any_spec] * 4,
+                    in_specs=[table_spec, table_spec, pl.BlockSpec((1, 8, toks), lambda g, dev, seg, low: (dev[g], 0, 0))],
                     out_specs=[any_spec] * 4,
                     scratch_shapes=[pltpu.VMEM((2, TILE, half), BF), pltpu.SMEM((2,), I32),
                                     pltpu.SemaphoreType.DMA((2,))]),
-                out_shape=[jax.ShapeDtypeStruct((stage, half), BF)] * 4,
-                input_output_aliases={6 + k: k for k in range(4)},
+                out_shape=[jax.ShapeDtypeStruct((size, half), BF)] * 4,
                 compiler_params=pltpu.CompilerParams(vmem_limit_bytes=VMEM_LIMIT),
                 cost_estimate=pl.CostEstimate(flops=2 * rows * cap * half, bytes_accessed=12 * rows * half, transcendentals=0),
                 name='pack',
-            )(devs, segs, low_rows, *tables, send_info, *rooms)
+            )(devs, segs, low_rows, *tables, send_info)
             return res[:2], res[2:]
 
         def arrived(tables, info, win, got_up, got_down, scaled):
@@ -475,9 +487,11 @@
             row = iota((up_rows.shape[0], 1), 0)
             return jnp.where(row < pass_up, got[0], up_rows), jnp.where(row < pass_down, got[1], down_rows)
 
-        def whole(total):
+        def parts_of(total):
             mine = jnp.where(core == 0, total[0], total[1])
-            theirs = mate(jnp.where(core == 0, total[1], total[0]))
+            return mine, mate(jnp.where(core == 0, total[1], total[0]))
+
+        def join(mine, theirs):
             return jnp.where(core == 0, jnp.concatenate([mine, theirs], axis=1), jnp.concatenate([theirs, mine], axis=1))
 
         def table(v):
@@ -489,8 +503,9 @@
         out_got = mate(theirs)
         ours = dot('cf,fd->cd', after(hid, theirs), w2_halves[0]).astype(BF)
         out_tables = (table(ours), table(out_got))
-        out_up, out_down = packed(out_tables, segs, rooms[:4], True)
-        all_dy = after(all_dy, out_up, out_down)
+        out_up, out_down = packed(out_tables, stage, True)
+        cut = [(out_up[0][:size], out_down[0][:size]) for size in tiers[:-1]] + [(out_up[0], out_down[0])]
+        all_dy = after(all_dy, out_up, out_down, cut)
 
         def block_spec(rows, width):
             return pl.BlockSpec((1, rows, width), lambda e, count: (e, 0, 0))
@@ -527,32 +542,32 @@
                 name='input_grad',
             )(counts, da, db, w1t, w3t)
 
-        def rest(size):
-            out_first = shift(out_up[0][:size], out_down[0][:size])
+        def rest(tier):
+            size = tiers[tier]
+            out_first = shift(*cut[tier])
             g, da, db = inner_grads_of(all_dy)
-            out_second = second_rows(after(out_first, da), out_up[1][:size], out_down[1][:size])
-            out_last = shift(*out_second)
-            da, db = after((da, db), *out_second)
             theirs = input_grad(da, db, 1)
             dx_got = mate(theirs)
-            ours = input_grad(after(da, theirs), db, 0)
+            out_second = second_rows(after(out_first, theirs), out_up[1][:size], out_down[1][:size])
+            out_last = shift(*out_second)
+            ours = input_grad(*after((da, db), *out_second), 0)
             dx_tables = (ours, dx_got)
-            dx_up, dx_down = packed(dx_tables, segs, rooms[4:], False)
-            dx_first = shift(dx_up[0][:size], dx_down[0][:size])
+            dx_up, dx_down = packed(dx_tables, size, False)
+            dx_first = shift(dx_up[0], dx_down[0])
             out_first, out_last, da, db, g = after((out_first, out_last, da, db, g), dx_up, dx_down)
             f = da.shape[2]
             da, db, g = da.reshape(rows, f), db.reshape(rows, f), g.reshape(rows, dim)
             dw1 = dot('cd,cf->df', x, da)
             out_first, out_last = after((out_first, out_last), dw1[:8, :TILE])
             y = arrived(out_tables, home_info, win, (out_first[0], out_last[0]), (out_first[1], out_last[1]), True)
-            y = whole(y)
-            dx_second = second_rows(after(dx_first, y), dx_up[1][:size], dx_down[1][:size])
+            y = join(*parts_of(y))
+            dx_second = second_rows(after(dx_first, y), dx_up[1], dx_down[1])
             dx_last = shift(*dx_second)
             db, hid_late = after((db, hid), *dx_second)
             dw3 = dot('cd,cf->df', x, db)
             dw2 = dot('cf,cd->fd', hid_late, g)
-            gx = whole(arrived(dx_tables, home_info, win, (dx_first[0], dx_last[0]), (dx_first[1], dx_last[1]), False))
-            return y, gx, row_major(dw1)[None], row_major(dw3)[None], row_major(dw2)[None]
+            gx = parts_of(arrived(dx_tables, home_info, win, (dx_first[0], dx_last[0]), (dx_first[1], dx_last[1]), False))
+            return y, *gx, row_major(dw1)[None], row_major(dw3)[None], row_major(dw2)[None]
 
         def general():
             my_rank, my_taken = pick(rank, me), pick(taken.astype(I32), me) > 0
@@ -591,8 +606,12 @@
             first = one_pass(0)
             second = one_pass(cap)
             sums = [u + v for u, v in zip(first, second)]
-            return (sums[0].astype(BF), sums[1].astype(BF)) + tuple(v[None] for v in sums[2:])
-
-        return lax.switch(state, [lambda: rest(small), lambda: rest(stage), general])
+            gx = jnp.split(sums[1].astype(BF), 2, axis=1)
+            gx = [jnp.where(core == k, gx[0], gx[1]) for k in range(2)]
+            return sums[0].astype(BF), *gx, *[v[None] for v in sums[2:]]
+
+        branches = [functools.partial(rest, tier) for tier in range(len(tiers))] + [general]
+        y, mine, theirs, dw1, dw3, dw2 = lax.switch(state, branches)
+        return y, join(mine, theirs), dw1, dw3, dw2
 
     return jax.shard_map(layer, mesh=mesh, in_specs=(tok_spec,) * 4 + (w_spec,) * 3, out_specs=(tok_spec,) * 5, check_vma=False)

time: 971 us -> 1040 us (1.071)
  waiting for transfers between devices: 252 us -> 303 us
  Pallas kernels: 177 us -> 197 us
  local copies, waits for them, and re-layouts: 101 us -> 81 us
    ppermute x4, waiting for transfers between devices: 93.4 us -> 142 us  [shift(): got_up = lax.ppermute(up_rows, 'expert', to_next)]
    all_gather x1, waiting for transfers between devices: 51.2 us -> 28 us  [layer(): all_dy = lax.all_gather(grad_y, 'expert')]
    broadcast_in_dim x8 -> x0, local copies, waits for them, and re-layouts: 21.6 us -> none  [layer(): jnp.full((stage, half), jnp.where(state > 3 + k, 1.0, 0.0), BF)]
    all_gather x1, waiting for transfers between devices: 36.4 us -> 51.7 us  [layer(): all_x = lax.all_gather(tok_x, 'expert')]
    pallas_call x2, Pallas kernels: 48.3 us -> 63.3 us  [packed(): pl.pallas_call(functools.partial(pack_kernel, scaled), grid_spec=pltpu.Pr...]
    unnamed x55 -> x65, local copies, waits for them, and re-layouts: 46.4 us -> 46.5 us
  transfers between devices with their start and end apart: 14 -> 14, of which waited for: 9 -> 9; matrix products, arithmetic and copies ran while one was open for 40% -> 36% of each run, Pallas kernels for 12% -> 9%
where the time goes in v1:
time: 1040 us; the launch traced here: 1030 us
  waiting for transfers between devices  303 us (29%)
  matrix products  240 us (23%)
  Pallas kernels  197 us (19%)
  other arithmetic  84.4 us (8%)
  local copies, waits for them, and re-layouts  81 us (8%)
  blocking collectives  54.2 us (5%)
  starting transfers between devices  26.6 us (3%)
  between operations  24.9 us (2%)
  loops' own time  18.6 us (2%)
    dot_general x10, matrix products, dot(): return jnp.einsum(form, a, b, preferred_element_type=F32)  240 us
    ppermute x4, waiting for transfers between devices, shift(): got_up = lax.ppermute(up_rows, 'expert', to_next)  142 us
    ppermute x4, waiting for transfers between devices, shift(): got_down = lax.ppermute(down_rows, 'expert', to_prev)  78.2 us
    pallas_call x2, Pallas kernels, packed(): pl.pallas_call(functools.partial(pack_kernel, scaled), grid_spec=pltpu.Pr...  63.3 us
    all_gather x1, waiting for transfers between devices, layer(): all_x = lax.all_gather(tok_x, 'expert')  51.7 us
    pallas_call x2, Pallas kernels, input_grad(): pl.pallas_call(input_kernel, grid_spec=pltpu.PrefetchScalarGridSpec(num_s...  47.1 us
    unnamed x65, local copies, waits for them, and re-layouts  46.5 us
    pallas_call x1, Pallas kernels, inner_grads_of(): pl.pallas_call(inner_kernel, grid_spec=pltpu.PrefetchScalarGridSpec(num_s...  45.7 us
  transfers between devices with their start and end apart: 14, of which 9 were waited for; matrix products, arithmetic and copies ran while one was open for 36% of the time, Pallas kernels for 9%

profile of v1, /device:TPU:112, one launch (start us, length us, event | category | flops | bytes accessed | tf_op | source)
XLA Modules:
  0.0 1028.8 jit_solution(6045097209033352414)
XLA Ops:
  8.9 24.7 %all-gather.3 = f32[8,4,768]{2,1,0:T(4,128)S(1)} all-gather(f32[1,4,768]{2,1,0:T(4,128)S(1)} %maximum_bitcast_fusion), channel_id=3, replica_groups=mesh['data'=2,'expert'=8] {'expert'}, dimensions={0}, use_global_device_ids=true | all-gather | bytes 110592 | tf_op jit(solution)/shard_map/all_gather | solution.py:283
  45.2 29.5 %pmax.7 = s32[]{:T(128)} all-reduce(s32[]{:T(128)S(6)} %select_n.859), channel_id=1, replica_groups=mesh['data'=2,'expert'=8] {'data','expert'}, use_global_device_ids=true, to_apply=%region_10.11 | all-reduce | flops 1 | bytes 8 | tf_op jit(solution)/shard_map/pmax | solution.py:319
  184.3 51.7 %all-gather.7.cloned.1.call-done = bf16[6144,4096]{1,0:T(8,128)(2,1)} async-done(((bf16[768,4096]{1,0:T(8,128)(2,1)}), bf16[6144,4096]{1,0:T(8,128)(2,1)}) %all-gather.7.cloned.1.call-update) | async-done | bytes 50331664 | tf_op jit(solution)/shard_map/all_gather | solution.py:279
  236.0 36.6 %convolution_convert_fusion.10 = bf16[8,384,4096]{2,1,0:T(8,128)(2,1)} fusion(bf16[8,384,768]{2,1,0:T(8,128)(2,1)} %fusion.41, bf16[8,768,4096]{2,1,0:T(8,128)(2,1)} %bitcast.480), kind=kOutput, calls=%fused_computation.149 | convolution fusion | flops 19339935744 | bytes 80216064 | tf_op jit(solution)/shard_map/gcs,gsd->gcd/dot_general | solution.py:22
  272.5 32.3 %convolution_convert_fusion.13 = bf16[3072,1024]{1,0:T(8,128)(2,1)S(1)} fusion(bf16[3072,4096]{1,0:T(8,128)(2,1)} %bitcast.487, bf16[1,4096,1024]{2,1,0:T(8,128)(2,1)} %param.17), kind=kOutput, calls=%fused_computation.160 | convolution fusion | flops 25772949504 | bytes 39845888 | tf_op jit(solution)/shard_map/cd,df->cf/dot_general | solution.py:22
  304.8 34.4 %convolution_convert_fusion.14 = bf16[3072,1024]{1,0:T(8,128)(2,1)S(1)} fusion(bf16[3072,4096]{1,0:T(8,128)(2,1)} %bitcast.488, bf16[1,4096,1024]{2,1,0:T(8,128)(2,1)} %param.16), kind=kOutput, calls=%fused_computation.161 | convolution fusion | flops 25772949504 | bytes 39845888 | tf_op jit(solution)/shard_map/cd,df->cf/dot_general | solution.py:22
  345.9 16.4 %convolution_convert_fusion.12 = bf16[3072,2048]{1,0:T(8,128)(2,1)} fusion(bf16[3072,1024]{1,0:T(8,128)(2,1)S(1)} %fusion.40, bf16[1024,2048]{0,1:T(8,128)(2,1)S(1)} %copy-done.49), kind=kOutput, calls=%fused_computation.156 | convolution fusion | flops 12891193344 | bytes 23068672 | tf_op jit(solution)/shard_map/cf,fd->cd/dot_general | solution.py:22
  363.0 19.6 %convolution_convert_fusion.11 = bf16[3072,2048]{1,0:T(8,128)(2,1)} fusion(bf16[3072,1024]{1,0:T(8,128)(2,1)} %copy-done.39, bf16[1024,2048]{0,1:T(8,128)(2,1)} %get-tuple-element.575), kind=kOutput, calls=%fused_computation.155 | convolution fusion | flops 12891193344 | bytes 23068672 | tf_op jit(solution)/shard_map/cf,fd->cd/dot_general | solution.py:22
  384.1 34.2 %pack.9 = (bf16[1136,2048]{1,0:T(8,128)(2,1)S(1)}, bf16[1136,2048]{1,0:T(8,128)(2,1)}, bf16[1136,2048]{1,0:T(8,128)(2,1)S(1)}, bf16[1136,2048]{1,0:T(8,128)(2,1)}) custom-call(s32[6]{0:T(128)S(1)} %copy-done.94, s32[6,4]{1,0:T(8,128)S(1)} %copy-done.74, s32[6,12]{1,0:T(8,128)S(1)} %copy-done.77, bf16[8,384,2048]{2,1,0:T(8,128)(2,1)} %bitcast.431, ...), custom_call_target="tpu_custom_call" | custom-call | flops 4831838208 | bytes 75497472 | tf_op jit(solution)/shard_map/pack/pallas_call | solution.py:450
  432.1 28.0 %all-gather.9.cloned.1.call-done = bf16[6144,4096]{1,0:T(8,128)(2,1)} async-done(((bf16[768,4096]{1,0:T(8,128)(2,1)}), bf16[6144,4096]{1,0:T(8,128)(2,1)}) %all-gather.9.cloned.1.call-update) | async-done | bytes 50331664 | tf_op jit(solution)/shard_map/all_gather | solution.py:280
  460.6 553.1 %conditional.1 = (bf16[768,4096]{1,0:T(8,128)(2,1)}, bf16[768,2048]{1,0:T(8,128)(2,1)S(1)}, bf16[768,2048]{1,0:T(8,128)(2,1)}, f32[1,4096,1024]{2,1,0:T(8,128)},...) conditional(s32[]{:T(128)} %clamp.3, (s32[]{:T(128)}, ...), branch_computations={%region_49.50_spmd, %region_50.51_spmd, %region_51.52_spmd, %regio... | conditional | flops 657605525504 | bytes 2096665344 | solution.py:614
  469.1 45.7 %inner.6 = (bf16[8,384,4096]{2,1,0:T(8,128)(2,1)}, bf16[8,384,1024]{2,1,0:T(8,128)(2,1)}, bf16[8,384,1024]{2,1,0:T(8,128)(2,1)}) custom-call(s32[8]{0:T(128)S(1)} %get-tuple-element.368.count_ref, f32[8,8,768]{2,1,0:T(8,128)S(1)} %get-tuple-element.369.info, bf16[8,768,4096]{2,1,0:T(8,128)(2,1)} %get-tuple-element.370.dy, ...), custom_call_target="tpu_custom_call" | custom-call | flops 45097156608 | bytes 100663296 | tf_op jit(solution)/shard_map/cond/branch_2_fun/inner/pallas_call | solution.py:518
  514.8 22.5 %input_grad.12 = bf16[8,384,2048]{2,1,0:T(8,128)(2,1)} custom-call(s32[8]{0:T(128)S(1)} %get-tuple-element.368.count_ref, bf16[8,384,1024]{2,1,0:T(8,128)(2,1)} %get-tuple-element.406.da, bf16[8,384,1024]{2,1,0:T(8,128)(2,1)} %get-tuple-element.408.db, bf16[1024,2048]{1,0:T(8,128)(2,1)S(1)} %copy-done.48, bf16[1024,2048]{1,0:T(8,128)(2,1)S(1)} %copy-done.45), custom_call_target="tpu_custom_call" | custom-call | flops 25769803776 | bytes 25165824 | tf_op jit(solution)/shard_map/cond/branch_2_fun/input_grad/pallas_call | solution.py:533
  547.7 76.8 %collective-permute-done.23.down1 = bf16[880,2048]{1,0:T(8,128)(2,1)S(1)} collective-permute-done((bf16[880,2048]{1,0:T(8,128)(2,1)}, bf16[880,2048]{1,0:T(8,128)(2,1)S(1)}, u32[]{:S(2)}, u32[]{:S(2)}) %collective-permute-start.23) | collective-permute-done | bytes 3604512 | tf_op jit(solution)/shard_map/cond/branch_2_fun/ppermute | solution.py:483
  635.8 24.6 %input_grad.13.tab0 = bf16[8,384,2048]{2,1,0:T(8,128)(2,1)} custom-call(s32[8]{0:T(128)S(1)} %get-tuple-element.368.count_ref, bf16[8,384,1024]{2,1,0:T(8,128)(2,1)} %get-tuple-element.406.da, bf16[8,384,1024]{2,1,0:T(8,128)(2,1)} %get-tuple-element.408.db, bf16[1024,2048]{1,0:T(8,128)(2,1)} %get-tuple-element.389.w1t, bf16[1024,2048]{1,0:T(8,128)(2,1)} %get-tuple-element.390.w3t), custom_call_target="tpu_custom_call" | custom-call | flops 25769803776 | bytes 25165824 | tf_op jit(solution)/shard_map/cond/branch_2_fun/input_grad/pallas_call | solution.py:533
  660.4 29.2 %pack.7 = (bf16[880,2048]{1,0:T(8,128)(2,1)S(1)}, bf16[880,2048]{1,0:T(8,128)(2,1)}, bf16[880,2048]{1,0:T(8,128)(2,1)}, bf16[880,2048]{1,0:T(8,128)(2,1)}) custom-call(s32[6]{0:T(128)S(1)} %get-tuple-element.384.dev_ref, s32[6,4]{1,0:T(8,128)S(1)} %get-tuple-element.385.seg_ref, s32[6,12]{1,0:T(8,128)S(1)} %get-tuple-element.386.low_ref, ...), custom_call_target="tpu_custom_call" | custom-call | flops 4831838208 | bytes 75497472 | tf_op jit(solution)/shard_map/cond/branch_2_fun/pack/pallas_call | solution.py:450
  689.6 21.4 %collective-permute-done.24.up2 = bf16[880,2048]{1,0:T(8,128)(2,1)} collective-permute-done((bf16[880,2048]{1,0:T(8,128)(2,1)}, bf16[880,2048]{1,0:T(8,128)(2,1)}, u32[]{:S(2)}, u32[]{:S(2)}) %collective-permute-start.24) | collective-permute-done | bytes 3604512 | tf_op jit(solution)/shard_map/cond/branch_2_fun/ppermute | solution.py:482
  712.4 20.4 %arrive.12 = bf16[2,768,2048]{2,1,0:T(8,128)(2,1)} custom-call(s32[2]{0:T(128)S(1)} %get-tuple-element.360.home_ref, s32[12,14]{1,0:T(8,128)S(1)} %copy.122.win_ref, bf16[8,384,2048]{2,1,0:T(8,128)(2,1)} %get-tuple-element.362.tab0, bf16[8,384,2048]{2,1,0:T(8,128)(2,1)} %get-tuple-element.363.tab1, f32[2,16,768]{2,1,0:T(8,128)S(1)} %get-tuple-element.364.info, ...), custom_call_target="tpu_custom_call" | custom-call | flops 4831838208 | bytes 75497472 | tf_op jit(solution)/shard_map/cond/branch_2_fun/arrive/pallas_call | solution.py:468
  751.1 73.7 %collective-permute-done.28.up1 = bf16[880,2048]{1,0:T(8,128)(2,1)S(1)} collective-permute-done((bf16[880,2048]{1,0:T(8,128)(2,1)S(1)}, bf16[880,2048]{1,0:T(8,128)(2,1)S(1)}, u32[]{:S(2)}, u32[]{:S(2)}) %collective-permute-start.28) | collective-permute-done | bytes 3604512 | tf_op jit(solution)/shard_map/cond/branch_2_fun/ppermute | solution.py:482
  832.9 34.0 %convolution_bitcast_fusion.8 = f32[1,4096,1024]{2,1,0:T(8,128)} fusion(bf16[3072,1024]{1,0:T(8,128)(2,1)} %bitcast.515, bf16[3072,4096]{1,0:T(8,128)(2,1)} %get-tuple-element.407), kind=kOutput, calls=%fused_computation.30 | convolution fusion | flops 25769803776 | bytes 48234496 | tf_op jit(solution)/shard_map/cond/branch_2_fun/cd,cf->df/dot_general | solution.py:22
  866.9 43.8 %collective-permute-done.30.up2 = bf16[880,2048]{1,0:T(8,128)(2,1)S(1)} collective-permute-done((bf16[880,2048]{1,0:T(8,128)(2,1)}, bf16[880,2048]{1,0:T(8,128)(2,1)S(1)}, u32[]{:S(2)}, u32[]{:S(2)}) %collective-permute-start.30) | collective-permute-done | bytes 3604512 | tf_op jit(solution)/shard_map/cond/branch_2_fun/ppermute | solution.py:482
  914.5 20.2 %arrive.13 = bf16[2,768,2048]{2,1,0:T(8,128)(2,1)} custom-call(s32[2]{0:T(128)S(1)} %get-tuple-element.360.home_ref, s32[12,14]{1,0:T(8,128)S(1)} %copy.122.win_ref, bf16[8,384,2048]{2,1,0:T(8,128)(2,1)} %input_grad.13.tab0, bf16[8,384,2048]{2,1,0:T(8,128)(2,1)} %collective-permute-done.26.tab1, f32[2,16,768]{2,1,0:T(8,128)S(1)} %get-tuple-element.364.info, ...), custom_call_target="tpu_custom_call" | custom-call | flops 4831838208 | bytes 75497472 | tf_op jit(solution)/shard_map/cond/branch_2_fun/arrive/pallas_call | solution.py:468
  937.9 33.9 %convolution_bitcast_fusion.7 = f32[1,4096,1024]{2,1,0:T(8,128)} fusion(bf16[3072,1024]{1,0:T(8,128)(2,1)} %bitcast.511, bf16[3072,4096]{1,0:T(8,128)(2,1)} %get-tuple-element.407), kind=kOutput, calls=%fused_computation.29 | convolution fusion | flops 25769803776 | bytes 48234496 | tf_op jit(solution)/shard_map/cond/branch_2_fun/cd,cf->df/dot_general | solution.py:22
  971.9 31.8 %convolution_bitcast_fusion.6 = f32[1,1024,4096]{2,1,0:T(8,128)} fusion(bf16[3072,1024]{1,0:T(8,128)(2,1)S(1)} %bitcast.467, bf16[3072,4096]{1,0:T(8,128)(2,1)} %bitcast.495), kind=kOutput, calls=%fused_computation.28 | convolution fusion | flops 25769803776 | bytes 48234496 | tf_op jit(solution)/shard_map/cond/branch_2_fun/cf,cd->fd/dot_general | solution.py:22
  (283 shorter events, 200.1 us)
Async XLA Ops:
  7.2 228.8 %all-gather.7.cloned.1.call-start = ((), (), s32[]{:S(2)}) async-start(), calls=%async_computation.4 | async-start | bytes 56623104 | tf_op jit(solution)/shard_map/all_gather | solution.py:279
  8.0 452.1 %all-gather.9.cloned.1.call-start = ((), (), s32[]{:S(2)}) async-start(), calls=%async_computation.5 | async-start | bytes 56623104 | tf_op jit(solution)/shard_map/all_gather | solution.py:280
  33.7 123.4 %copy-start.66 = (f32[8,768]{1,0:T(8,128)}, f32[8,768]{1,0:T(8,128)S(1)}, u32[]{:S(2)}) copy-start(f32[8,768]{1,0:T(8,128)S(1)} %get-tuple-element.896) | copy-start | bytes 73732
  33.8 71.5 %copy-start.64 = (pred[8,8,768]{2,1,0:T(8,128)(4,1)}, pred[8,8,768]{2,1,0:T(8,128)(4,1)S(1)}, u32[]{:S(2)}) copy-start(pred[8,8,768]{2,1,0:T(8,128)(4,1)S(1)} %fusion.56) | copy-start | bytes 147460
  304.8 34.4 %copy-start.37 = (bf16[3072,1024]{1,0:T(8,128)(2,1)}, bf16[3072,1024]{1,0:T(8,128)(2,1)S(1)}, u32[]{:S(2)}) copy-start(bf16[3072,1024]{1,0:T(8,128)(2,1)S(1)} %convolution_convert_fusion.13) | copy-start | bytes 18874372
  362.3 21.7 %collective-permute-start.44 = (bf16[3072,2048]{1,0:T(8,128)(2,1)}, bf16[3072,2048]{1,0:T(8,128)(2,1)}, u32[]{:S(2)}, u32[]{:S(2)}) collective-permute-start(bf16[3072,2048]{1,0:T(8,128)(2,1)} %convolution_convert_fusion.12), channel_id=1, source_target_pairs={{0,1},{1,0},{2,3},{3,2},{4,5},{5,4},{6,7},{7,6},{8,9},{9,8},{10,11... | collective-permute-start | bytes 37748744 | tf_op jit(solution)/shard_map/ppermute | solution.py:277
  469.1 45.7 %copy-start.45 = (bf16[1024,2048]{1,0:T(8,128)(2,1)S(1)}, bf16[1024,2048]{1,0:T(8,128)(2,1)}, u32[]{:S(2)}) copy-start(bf16[1024,2048]{1,0:T(8,128)(2,1)} %get-tuple-element.377.w3t) | copy-start | bytes 12582916 | tf_op jit(solution)/shard_map/cond
  469.1 45.7 %copy-start.48 = (bf16[1024,2048]{1,0:T(8,128)(2,1)S(1)}, bf16[1024,2048]{1,0:T(8,128)(2,1)}, u32[]{:S(2)}) copy-start(bf16[1024,2048]{1,0:T(8,128)(2,1)} %get-tuple-element.376.w1t) | copy-start | bytes 12582916 | tf_op jit(solution)/shard_map/cond
  514.8 112.9 %copy-start.4 = (bf16[1136,2048]{1,0:T(8,128)(2,1)S(1)}, bf16[1136,2048]{1,0:T(8,128)(2,1)}, u32[]{:S(2)}) copy-start(bf16[1136,2048]{1,0:T(8,128)(2,1)} %get-tuple-element.379) | copy-start | bytes 13959172 | tf_op jit(solution)/shard_map/cond
  537.3 93.0 %slice-start.4 = ((s8[4653056]{0:T(1024)(128)(4,1)}), s8[4194304]{0:T(1024)(128)(4,1)S(1)}, s32[]{:S(2)}) async-start(s8[4653056]{0:T(1024)(128)(4,1)} %bitcast.440), calls=%async_computation.10 | async-start | bytes 8388608 | tf_op jit(solution)/shard_map/cond
  537.3 123.1 %collective-permute-start.26 = (bf16[8,384,2048]{2,1,0:T(8,128)(2,1)}, bf16[8,384,2048]{2,1,0:T(8,128)(2,1)}, u32[]{:S(2)}, u32[]{:S(2)}) collective-permute-start(bf16[8,384,2048]{2,1,0:T(8,128)(2,1)} %input_grad.12), channel_id=1, source_target_pairs={{0,1},{1,0},{2,3},{3,2},{4,5},{5,4},{6,7},{7,6},{8,9},{9,8},{10,11... | collective-permute-start | bytes 37748744 | tf_op jit(solution)/shard_map/cond/branch_2_fun/ppermute | solution.py:277
  544.3 80.1 %collective-permute-start.23 = (bf16[880,2048]{1,0:T(8,128)(2,1)}, bf16[880,2048]{1,0:T(8,128)(2,1)S(1)}, u32[]{:S(2)}, u32[]{:S(2)}) collective-permute-start(bf16[880,2048]{1,0:T(8,128)(2,1)} %get-tuple-element.366), channel_id=1, source_target_pairs={{0,6},{1,7},{2,0},{3,1},{4,2},{5,3},{6,4},{7,5},{8,14},{9,15},{10,... | collective-permute-start | bytes 10813448 | tf_op jit(solution)/shard_map/cond/branch_2_fun/ppermute | solution.py:483
  546.3 81.4 %collective-permute-start.22 = (bf16[880,2048]{1,0:T(8,128)(2,1)}, bf16[880,2048]{1,0:T(8,128)(2,1)S(1)}, u32[]{:S(2)}, u32[]{:S(2)}) collective-permute-start(bf16[880,2048]{1,0:T(8,128)(2,1)} %get-tuple-element.365), channel_id=1, source_target_pairs={{0,2},{1,3},{2,4},{3,5},{4,6},{5,7},{6,0},{7,1},{8,10},{9,11},{10,... | collective-permute-start | bytes 10813448 | tf_op jit(solution)/shard_map/cond/branch_2_fun/ppermute | solution.py:482
  630.3 80.7 %collective-permute-start.24 = (bf16[880,2048]{1,0:T(8,128)(2,1)}, bf16[880,2048]{1,0:T(8,128)(2,1)}, u32[]{:S(2)}, u32[]{:S(2)}) collective-permute-start(bf16[880,2048]{1,0:T(8,128)(2,1)} %slice_select_fusion.5), channel_id=1, source_target_pairs={{0,2},{1,3},{2,4},{3,5},{4,6},{5,7},{6,0},{7,1},{8,10},{9,11},{10,... | collective-permute-start | bytes 10813448 | tf_op jit(solution)/shard_map/cond/branch_2_fun/ppermute | solution.py:482
  632.5 79.9 %collective-permute-start.25 = (bf16[880,2048]{1,0:T(8,128)(2,1)}, bf16[880,2048]{1,0:T(8,128)(2,1)}, u32[]{:S(2)}, u32[]{:S(2)}) collective-permute-start(bf16[880,2048]{1,0:T(8,128)(2,1)} %slice_select_fusion.4), channel_id=1, source_target_pairs={{0,6},{1,7},{2,0},{3,1},{4,2},{5,3},{6,4},{7,5},{8,14},{9,15},{10,... | collective-permute-start | bytes 10813448 | tf_op jit(solution)/shard_map/cond/branch_2_fun/ppermute | solution.py:483
  660.4 52.0 %copy-start.1 = (bf16[880,2048]{1,0:T(8,128)(2,1)S(1)}, bf16[880,2048]{1,0:T(8,128)(2,1)}, u32[]{:S(2)}) copy-start(bf16[880,2048]{1,0:T(8,128)(2,1)} %copy-done) | copy-start | bytes 10813444 | tf_op jit(solution)/shard_map/cond
  736.0 10.8 %collective-permute-start.27 = (bf16[768,2048]{1,0:T(8,128)(2,1)S(1)}, bf16[768,2048]{1,0:T(8,128)(2,1)S(1)}, u32[]{:S(2)}, u32[]{:S(2)}) collective-permute-start(bf16[768,2048]{1,0:T(8,128)(2,1)S(1)} %get-tuple-element.954), channel_id=1, source_target_pairs={{0,1},{1,0},{2,3},{3,2},{4,5},{5,4},{6,7},{7,6},{8,9},{9,8},{10,11... | collective-permute-start | bytes 9437192 | tf_op jit(solution)/shard_map/cond/branch_2_fun/ppermute | solution.py:277
  736.1 88.7 %collective-permute-start.28 = (bf16[880,2048]{1,0:T(8,128)(2,1)S(1)}, bf16[880,2048]{1,0:T(8,128)(2,1)S(1)}, u32[]{:S(2)}, u32[]{:S(2)}) collective-permute-start(bf16[880,2048]{1,0:T(8,128)(2,1)S(1)} %get-tuple-element.392), channel_id=1, source_target_pairs={{0,2},{1,3},{2,4},{3,5},{4,6},{5,7},{6,0},{7,1},{8,10},{9,11},{10,... | collective-permute-start | bytes 10813448 | tf_op jit(solution)/shard_map/cond/branch_2_fun/ppermute | solution.py:482
  742.3 82.6 %collective-permute-start.29 = (bf16[880,2048]{1,0:T(8,128)(2,1)S(1)}, bf16[880,2048]{1,0:T(8,128)(2,1)S(1)}, u32[]{:S(2)}, u32[]{:S(2)}) collective-permute-start(bf16[880,2048]{1,0:T(8,128)(2,1)S(1)} %copy-done.103), channel_id=1, source_target_pairs={{0,6},{1,7},{2,0},{3,1},{4,2},{5,3},{6,4},{7,5},{8,14},{9,15},{10,... | collective-permute-start | bytes 10813448 | tf_op jit(solution)/shard_map/cond/branch_2_fun/ppermute | solution.py:483
  746.8 78.0 %copy-start.53 = (bf16[880,2048]{1,0:T(8,128)(2,1)S(1)}, bf16[880,2048]{1,0:T(8,128)(2,1)}, u32[]{:S(2)}) copy-start(bf16[880,2048]{1,0:T(8,128)(2,1)} %get-tuple-element.395) | copy-start | bytes 10813444 | tf_op jit(solution)/shard_map/cond
  751.1 76.3 %copy-start.52 = (bf16[880,2048]{1,0:T(8,128)(2,1)S(1)}, bf16[880,2048]{1,0:T(8,128)(2,1)}, u32[]{:S(2)}) copy-start(bf16[880,2048]{1,0:T(8,128)(2,1)} %get-tuple-element.393) | copy-start | bytes 10813444 | tf_op jit(solution)/shard_map/cond
  829.7 81.1 %collective-permute-start.30 = (bf16[880,2048]{1,0:T(8,128)(2,1)}, bf16[880,2048]{1,0:T(8,128)(2,1)S(1)}, u32[]{:S(2)}, u32[]{:S(2)}) collective-permute-start(bf16[880,2048]{1,0:T(8,128)(2,1)} %broadcast_select_fusion.5), channel_id=1, source_target_pairs={{0,2},{1,3},{2,4},{3,5},{4,6},{5,7},{6,0},{7,1},{8,10},{9,11},{10,... | collective-permute-start | bytes 10813448 | tf_op jit(solution)/shard_map/cond/branch_2_fun/ppermute | solution.py:482
  830.8 79.9 %collective-permute-start.31 = (bf16[880,2048]{1,0:T(8,128)(2,1)}, bf16[880,2048]{1,0:T(8,128)(2,1)S(1)}, u32[]{:S(2)}, u32[]{:S(2)}) collective-permute-start(bf16[880,2048]{1,0:T(8,128)(2,1)} %broadcast_select_fusion.4), channel_id=1, source_target_pairs={{0,6},{1,7},{2,0},{3,1},{4,2},{5,3},{6,4},{7,5},{8,14},{9,15},{10,... | collective-permute-start | bytes 10813448 | tf_op jit(solution)/shard_map/cond/branch_2_fun/ppermute | solution.py:483
  937.8 65.9 %collective-permute-start.32 = (bf16[768,2048]{1,0:T(8,128)(2,1)S(1)}, bf16[768,2048]{1,0:T(8,128)(2,1)}, u32[]{:S(2)}, u32[]{:S(2)}) collective-permute-start(bf16[768,2048]{1,0:T(8,128)(2,1)S(1)} %get-tuple-element.951), channel_id=1, source_target_pairs={{0,1},{1,0},{2,3},{3,2},{4,5},{5,4},{6,7},{7,6},{8,9},{9,8},{10,11... | collective-permute-start | bytes 9437192 | tf_op jit(solution)/shard_map/cond/branch_2_fun/ppermute | solution.py:277
  (32 other events, 503.6 us)
Sparse Core Ops, SparseCore 0:
  9.6 226.2 all-gather.6
  237.5 222.5 all-gather.8

commit v2 on v1

--- a/solution.py
+++ b/solution.py
@@ -13,8 +13,8 @@
 I32 = jnp.int32
 PIECE = 16
 TILE = 128
-WINDOW = 144
 SPAN = 256
+ROOM = 512
 VMEM_LIMIT = 50 * 2 ** 20
 
 
@@ -45,10 +45,10 @@
     return lax.optimization_barrier((value,) + others)[0]
 
 
-def pack_kernel(scaled, dev_ref, seg_ref, low_ref, tab0, tab1, info, *refs):
+def pack_kernel(scaled, dev_ref, seg_ref, low_ref, tab0, tab1, cols, *refs):
     outs, (buf, pend, sem) = (refs[0:2], refs[2:4]), refs[4:]
     g = pl.program_id(0)
-    toks = info.shape[2]
+    toks = cols.shape[1]
     length, start, extra, stage = [seg_ref[g, k] for k in range(4)]
 
     @pl.when(g == 0)
@@ -78,19 +78,14 @@
         def _():
             slot = lax.rem(i, 2)
             drain(slot)
-            vals = info[0]
-            match = vals[0:1, :] == (iota((TILE, toks), 0) + i * TILE).astype(F32)
-
-            def column(k, off):
-                return jnp.sum(jnp.where(match, vals[k:k + 1, :] + off, 0.0), axis=1, keepdims=True)
-
+            vals = cols[0, pl.ds(pl.multiple_of(i * TILE, TILE), TILE)]
             lows = [low_ref[g, 2 * i + k] for k in range(2)]
 
             def part(k, tab):
-                at = column(1 + k, 1.0) - (lows[k] + 1).astype(F32)
+                at = vals[:, k:k + 1] - lows[k].astype(F32)
                 onehot = (at == iota((TILE, SPAN), 1).astype(F32)).astype(BF)
                 got = jnp.dot(onehot, tab[0, pl.ds(pl.multiple_of(lows[k], PIECE), SPAN)], preferred_element_type=F32)
-                return got * column(3 + k, 0.0) if scaled else got
+                return got * vals[:, 2 + k:3 + k] if scaled else got
 
             @pl.when((lows[0] >= 0) & (lows[1] < 0))
             def _():
@@ -139,64 +134,47 @@
         drain(1)
 
 
-def arrive_kernel(scaled, second, home_ref, win_ref, tab0, tab1, info, up1, up2, down1, down2, out, acc, wbuf, sem):
+def arrive_kernel(scaled, home_ref, plan_ref, info, tab0, tab1, up1, up2, down1, down2, out, wbuf, sem):
     t, last = pl.program_id(0), pl.num_programs(0) - 1
-    windows = (up1, up2, up2, down1, down2, down2)
-
-    def copies(step, do):
+    sources = (tab0.at[home_ref[0]], tab1.at[home_ref[0]], up1, up2, up2, down1, down2, down2)
+
+    def pieces(step, do):
         slot = lax.rem(step, 2)
-        for w, ref in enumerate(windows):
-            begin = win_ref[step, w]
-
-            @pl.when(begin >= 0)
-            def _(ref=ref, w=w, begin=begin):
-                src = ref.at[pl.ds(pl.multiple_of(jnp.maximum(begin, 0), PIECE), WINDOW)]
-                do(pltpu.make_async_copy(src, wbuf.at[slot, w, pl.ds(0, WINDOW)], sem.at[slot, w]))
+        for w, ref in enumerate(sources):
+            begin, count, to = [plan_ref[step, 3 * w + k] for k in range(3)]
+
+            def one(p, carry, ref=ref, begin=begin, to=to):
+                src = ref.at[pl.ds(pl.multiple_of(begin + p * PIECE, PIECE), PIECE)]
+                do(pltpu.make_async_copy(src, wbuf.at[slot, pl.ds(pl.multiple_of(to + p * PIECE, PIECE), PIECE)], sem.at[slot]))
+                return carry
+
+            lax.fori_loop(0, count, one, 0)
 
     @pl.when(t == 0)
     def _():
-        wbuf[:, :, WINDOW:] = jnp.zeros((2, len(windows), SPAN - WINDOW, wbuf.shape[3]), BF)
-        copies(0, lambda c: c.start())
+        wbuf[...] = jnp.zeros_like(wbuf)
+        pieces(0, lambda c: c.start())
 
     @pl.when(t < last)
     def _():
-        copies(t + 1, lambda c: c.start())
+        pieces(t + 1, lambda c: c.start())
 
     vals = info[0]
     eye = iota((TILE, TILE), 0) == iota((TILE, TILE), 1)
+    lane = iota((TILE, wbuf.shape[1]), 1).astype(F32)
 
     def column(k):
         return jnp.sum(jnp.where(eye, vals[k:k + 1, :], 0.0), axis=1, keepdims=True)
 
-    def add(begin, base, spot, weight, rows):
-        @pl.when(begin >= 0)
-        def _():
-            at = column(spot) - (begin + base).astype(F32)
-            onehot = (at == iota((TILE, SPAN), 1).astype(F32)).astype(BF)
-            part = jnp.dot(onehot, rows(), preferred_element_type=F32)
-            acc[...] = acc[...] + (part * column(weight) if scaled else part)
-
-    acc[...] = jnp.zeros_like(acc)
-    count = len(windows)
-    for k, tab in enumerate((tab0, tab1)):
-        low = win_ref[t, count + k]
-        add(low, 0, k, 2 + k, lambda tab=tab, low=low: tab[0, pl.ds(pl.multiple_of(low, PIECE), SPAN)])
-    copies(t, lambda c: c.wait())
-    slot = lax.rem(t, 2)
-
-    def arrived_rows(w):
-        used = (win_ref[t, count + 2 + w] - win_ref[t, w] + PIECE - 1) // PIECE
-
-        def clear(p, carry):
-            wbuf[slot, w, pl.ds(pl.multiple_of(p * PIECE, PIECE), PIECE)] = jnp.zeros((PIECE, wbuf.shape[3]), BF)
-            return carry
-
-        lax.fori_loop(used, WINDOW // PIECE, clear, 0)
-        return wbuf[slot, w]
-
-    for w, (spot, weight, base) in enumerate(((4, 8, 0), (4, 8, second), (6, 10, 0), (5, 9, 0), (5, 9, second), (7, 10, 0))):
-        add(win_ref[t, w], base, spot, weight, lambda w=w: arrived_rows(w))
-    out[0] = acc[...].astype(BF)
+    first, second = column(0) == lane, column(1) == lane
+    pieces(t, lambda c: c.wait())
+    rows = wbuf.at[lax.rem(t, 2)]
+    if scaled:
+        total = column(2) * jnp.dot(first.astype(BF), rows[...], preferred_element_type=F32)
+        total = total + column(3) * jnp.dot(second.astype(BF), rows[...], preferred_element_type=F32)
+    else:
+        total = jnp.dot((first | second).astype(BF), rows[...], preferred_element_type=F32)
+    out[...] = total.astype(BF)
 
 
 def by_count(count, cap, run):
@@ -206,18 +184,21 @@
             run(n)
 
 
-def inner_kernel(count_ref, info, dy, w2t, a_ref, b_ref, g_ref, da_ref, db_ref):
+def inner_kernel(count_ref, from_ref, info, dy, w2t, a_ref, b_ref, g_ref, da_ref, db_ref):
+    e = pl.program_id(0)
     cap, dim = g_ref.shape[1:]
+    toks = dy.shape[1]
     step = dim // 4
-
-    def run(n):
+    count, begin = count_ref[e], from_ref[e]
+
+    def fill(n, begin, span):
         if n:
-            vals = info[0]
-            match = vals[0:1, :] == iota((n, vals.shape[1]), 0).astype(F32)
+            vals = info[0, :, pl.ds(begin, span)]
+            match = vals[0:1, :] == iota((n, span), 0).astype(F32)
             gate = jnp.sum(jnp.where(match, vals[1:2, :], 0.0), axis=1, keepdims=True)
             onehot = match.astype(BF)
             for c in range(0, dim, step):
-                got = jnp.dot(onehot, dy[0, :, c:c + step], preferred_element_type=F32)
+                got = jnp.dot(onehot, dy[0, pl.ds(begin, span), c:c + step], preferred_element_type=F32)
                 g_ref[0, :n, c:c + step] = (gate * got).astype(BF)
             dh = jnp.dot(g_ref[0, :n], w2t[...], preferred_element_type=F32).astype(BF).astype(F32)
             a, b = a_ref[0, :n].astype(F32), b_ref[0, :n].astype(F32)
@@ -228,7 +209,13 @@
             for ref in (g_ref, da_ref, db_ref):
                 ref[0, n:] = jnp.zeros((cap - n, ref.shape[2]), BF)
 
-    by_count(count_ref[pl.program_id(0)], cap, run)
+    @pl.when(begin >= 0)
+    def _():
+        by_count(count, cap, lambda n: fill(n, pl.multiple_of(begin, TILE), toks * 2 // 3))
+
+    @pl.when(begin < 0)
+    def _():
+        fill(cap, 0, toks)
 
 
 def input_kernel(count_ref, da, db, w1t, w3t, out):
@@ -323,9 +310,6 @@
 
         own_spot, mate_spot = pick(spot, me), pick(spot, me ^ 1)
         own_gate, mate_gate = gate_of(me), gate_of(me ^ 1)
-        pad = jnp.zeros((group, toks), F32)
-        send_info = jnp.stack([pick(listed, chip).astype(F32), own_spot.astype(F32), mate_spot.astype(F32),
-                               jnp.where(single, own_gate, 1.0), jnp.where(single, mate_gate, 1.0), pad, pad, pad], axis=1)
         f_up, f_down = pick(chosen, chip), pick(other, chip)
         pass_up, pass_down = pick(chosen, down), pick(other, up)
         my_sizes = pick(sizes, chip)
@@ -350,12 +334,34 @@
                     lead = lead + size
             return jnp.stack(segs)
 
+        def of_chips(v):
+            return jnp.concatenate([lax.dynamic_slice_in_dim(v, 2 * to, 2, 0) for to in (far, up, down)])
+
+        def thirds(v):
+            high = v.astype(BF)
+            middle = (v - high.astype(F32)).astype(BF)
+            return [high, middle, (v - high.astype(F32) - middle.astype(F32)).astype(BF)]
+
+        values = []
+        for v in (own_spot, mate_spot):
+            v = of_chips(v) + 1
+            values += [(v // 256).astype(BF), (v % 256).astype(BF)]
+        for v in (own_gate, mate_gate):
+            values += thirds(of_chips(jnp.where(single, v, 1.0)))
+        in_list = of_chips(pick(listed, chip))[:, None, :] == iota((1, toks, 1), 1)
+        got = dot('gqs,gsk->gqk', in_list.astype(BF), jnp.stack(values, axis=2))
+        list_cols = [got[:, :, 2 * k] * 256.0 + got[:, :, 2 * k + 1] - 1.0 for k in range(2)]
+        list_cols += [got[:, :, 4 + 3 * k] + got[:, :, 5 + 3 * k] + got[:, :, 6 + 3 * k] for k in range(2)]
+        list_cols = jnp.stack(list_cols + [jnp.zeros_like(list_cols[0])] * 4, axis=2)
+
         tier_stage = sum([jnp.where(state == k, size, 0) for k, size in enumerate(tiers)]) + jnp.where(state == len(tiers), stage, 0)
         segs = segments(tier_stage)
 
         def home(v):
-            return lax.dynamic_slice_in_dim(v, 2 * chip, 2, 0)
-
+            v = lax.dynamic_slice_in_dim(v, 2 * chip, 2, 0)
+            return jnp.where(core == 0, v[::-1], v)
+
+        home_core = jnp.where((core == 0) == (iota((2, 1), 0) == 0), 1, 0)
         home_idx = [home(idx[j]) for j in range(tops)]
         home_gates = [home(gates[j]) for j in range(tops)]
         home_kept = home(jnp.sum(kept.astype(I32) * (1 << expert_id), axis=0))
@@ -364,7 +370,7 @@
         def listed_at(c):
             at = home(pick(listed, c))
             first = pick(pick(sizes, c), 2 * chip)
-            return at >= 0, at + jnp.where(iota((2, 1), 0) == 1, first, 0)
+            return at >= 0, at + jnp.where(home_core == 1, first, 0)
 
         def weight_of(c):
             w = 0.0
@@ -373,38 +379,34 @@
                 w = w + jnp.where((home_idx[j] // 2 == c) & held, home_gates[j], 0.0)
             return jnp.where(home_single, 1.0, w)
 
+        def near_spots(c, lead, passed):
+            ok, at = listed_at(c)
+            at = at + lead
+            late = at >= tier_stage
+            return [jnp.where(ok & jnp.logical_not(late), at, -1), jnp.where(ok & late, at + passed - tier_stage, -1)]
+
         far_ok, far_at = listed_at(far)
         far_cut = pick(chosen, far)
-        far_by_up = jnp.where(far_ok & (far_at < far_cut), far_at, -1)
-        far_by_down = jnp.where(far_ok & (far_at >= far_cut), far_at - far_cut, -1)
-        home_spots = [home(own_spot), home(mate_spot)]
-        weights = [weight_of(c) for c in (down, up, far)]
-        own_lows = [lowest(v.reshape(2 * tiles, TILE), True) for v in home_spots]
-
-        def arrival(size_of_stage):
-            def near_spot(c, lead, passed):
-                ok, at = listed_at(c)
-                at = at + lead
-                return jnp.where(ok, jnp.where(at >= size_of_stage, stage + at + passed - size_of_stage, at), -1)
-
-            from_down = near_spot(down, pick(chosen, down), pick(chosen, far))
-            from_up = near_spot(up, pick(other, up), pick(other, far))
-            info = [v.astype(F32) for v in home_spots] + [home(own_gate), home(mate_gate)]
-            info += [v.astype(F32) for v in (from_down, from_up, far_by_up, far_by_down)] + weights
-            info = jnp.stack(info + [jnp.zeros((2, toks), F32)] * 5, axis=1)
-            begins = []
-            for near, by in ((from_down, far_by_up), (from_up, far_by_down)):
-                begins.append(jnp.where((near >= 0) & (near < stage), near, place))
-                begins.append(jnp.where(near >= stage, near - stage, place))
-                begins.append(jnp.where(by >= 0, by, place))
-            begins = jnp.stack(begins).reshape(6, 2 * tiles, TILE)
-            low = jnp.min(begins, axis=2)
-            end = jnp.max(jnp.where(begins < place, begins, -1), axis=2) + 1
-            low = jnp.where(low < place, jnp.minimum(low // PIECE * PIECE, size_of_stage - WINDOW), -1)
-            return info, jnp.concatenate([low, jnp.stack(own_lows), end]).T
-
-        home_info, win = arrival(tier_stage)
-        homes = jnp.stack([2 * chip, 2 * chip + 1])
+        spots = [home(own_spot), home(mate_spot)]
+        spots += near_spots(down, pick(chosen, down), pick(chosen, far)) + [jnp.where(far_ok & (far_at < far_cut), far_at, -1)]
+        spots += near_spots(up, pick(other, up), pick(other, far)) + [jnp.where(far_ok & (far_at >= far_cut), far_at - far_cut, -1)]
+        w_down, w_up, w_far = [weight_of(c) for c in (down, up, far)]
+        weights = [home(own_gate), home(mate_gate), w_down, w_down, w_far, w_up, w_up, w_far]
+        spots = jnp.stack(spots).reshape(8, 2 * tiles, TILE)
+        weights = jnp.stack(weights).reshape(8, 2 * tiles, TILE)
+        there = spots >= 0
+        begin = jnp.min(jnp.where(there, spots, place), axis=2) // PIECE * PIECE
+        count = jnp.maximum(jnp.max(spots, axis=2) - begin + PIECE, 0) // PIECE
+        to = jnp.cumsum(count, axis=0) * PIECE - count * PIECE
+        at = jnp.where(there, spots + (to - begin)[:, :, None], -1)
+        first = jnp.max(at, axis=0)
+        second = jnp.sum(at + 1, axis=0) - first - 2
+        w_first = jnp.sum(jnp.where(there & (at == first[None]), weights, 0.0), axis=0)
+        w_second = jnp.sum(jnp.where(there & (at == second[None]), weights, 0.0), axis=0)
+        home_info = [first.astype(F32), second.astype(F32), w_first, w_second]
+        home_info = jnp.stack(home_info + [jnp.zeros_like(w_first)] * 4, axis=1).reshape(2, tiles, 8, TILE)
+        home_plan = jnp.stack([begin, count, to], axis=1).reshape(24, 2 * tiles).T.reshape(2, tiles, 24)
+        homes = 2 * chip + home_core
 
         onehot_in = (own_spot[:, None, :] == iota((1, cap, 1), 1)).astype(BF)
 
@@ -418,10 +420,16 @@
         counts = jnp.sum((own_spot >= 0).astype(I32), axis=1)
         pad = jnp.zeros((group, toks), F32)
         own_info = jnp.stack([own_spot.astype(F32), own_gate] + [pad] * 6, axis=1)
-        plan = (state, send_info, devs, segs, low_rows, home_info, win, homes, onehot_in, counts, own_info, w2_halves, w2t, w13t_halves)
+        span = toks * 2 // 3
+        s_first = jnp.min(jnp.where(own_spot >= 0, iota(own_spot.shape, 1), toks), axis=1)
+        s_last = jnp.max(jnp.where(own_spot >= 0, iota(own_spot.shape, 1), 0), axis=1)
+        froms = jnp.minimum(s_first // TILE * TILE, toks - span)
+        froms = jnp.where(s_last < froms + span, froms, -1)
+        plan = (state, list_cols, devs, segs, low_rows, home_info, home_plan, homes, onehot_in, counts, froms, own_info, w2_halves, w2t, w13t_halves)
         plan = lax.optimization_barrier(plan)
         all_x, plan = lax.optimization_barrier((all_x, plan))
-        (state, send_info, devs, segs, low_rows, home_info, win, homes, onehot_in, counts, own_info, w2_halves, w2t, w13t_halves) = plan
+        (state, list_cols, devs, segs, low_rows, home_info, home_plan, homes, onehot_in, counts, froms, own_info, w2_halves, w2t,
+         w13t_halves) = plan
 
         def take(onehot, tok, gate=None):
             got = dot('gcs,gsd->gcd', onehot, tok)
@@ -451,7 +459,7 @@
                 functools.partial(pack_kernel, scaled),
                 grid_spec=pltpu.PrefetchScalarGridSpec(
                     num_scalar_prefetch=3, grid=(6,),
-                    in_specs=[table_spec, table_spec, pl.BlockSpec((1, 8, toks), lambda g, dev, seg, low: (dev[g], 0, 0))],
+                    in_specs=[table_spec, table_spec, pl.BlockSpec((1, toks, 8), lambda g, dev, seg, low: (g, 0, 0))],
                     out_specs=[any_spec] * 4,
                     scratch_shapes=[pltpu.VMEM((2, TILE, half), BF), pltpu.SMEM((2,), I32),
                                     pltpu.SemaphoreType.DMA((2,))]),
@@ -459,24 +467,28 @@
                 compiler_params=pltpu.CompilerParams(vmem_limit_bytes=VMEM_LIMIT),
                 cost_estimate=pl.CostEstimate(flops=2 * rows * cap * half, bytes_accessed=12 * rows * half, transcendentals=0),
                 name='pack',
-            )(devs, segs, low_rows, *tables, send_info)
+            )(devs, segs, low_rows, *tables, list_cols)
             return res[:2], res[2:]
 
-        def arrived(tables, info, win, got_up, got_down, scaled):
-            table_spec = pl.BlockSpec((1, cap, half), lambda t, homes, win: (homes[t // tiles], 0, 0))
-            info_spec = pl.BlockSpec((1, 16, TILE), lambda t, homes, win: (t // tiles, 0, t % tiles))
+        def arrived(which, tables, got_up, got_down, scaled):
             return pl.pallas_call(
-                functools.partial(arrive_kernel, scaled, stage),
+                functools.partial(arrive_kernel, scaled),
                 grid_spec=pltpu.PrefetchScalarGridSpec(
-                    num_scalar_prefetch=2, grid=(2 * tiles,),
-                    in_specs=[table_spec, table_spec, info_spec] + [any_spec] * 4,
-                    out_specs=pl.BlockSpec((1, TILE, half), lambda t, homes, win: (t // tiles, t % tiles, 0)),
-                    scratch_shapes=[pltpu.VMEM((TILE, half), F32), pltpu.VMEM((2, 6, SPAN, half), BF), pltpu.SemaphoreType.DMA((2, 6))]),
-                out_shape=jax.ShapeDtypeStruct((2, toks, half), BF),
+                    num_scalar_prefetch=2, grid=(tiles,),
+                    in_specs=[pl.BlockSpec((1, 8, TILE), lambda t, homes, plan: (t, 0, 0))] + [any_spec] * 6,
+                    out_specs=pl.BlockSpec((TILE, half), lambda t, homes, plan: (t, 0)),
+                    scratch_shapes=[pltpu.VMEM((2, ROOM, half), BF), pltpu.SemaphoreType.DMA((2,))]),
+                out_shape=jax.ShapeDtypeStruct((toks, half), BF),
                 compiler_params=pltpu.CompilerParams(vmem_limit_bytes=VMEM_LIMIT),
-                cost_estimate=pl.CostEstimate(flops=2 * rows * cap * half, bytes_accessed=12 * rows * half, transcendentals=0),
+                cost_estimate=pl.CostEstimate(flops=2 * rows * cap * half, bytes_accessed=6 * rows * half, transcendentals=0),
                 name='arrive',
-            )(homes, win, *tables, info, *got_up, *got_down)
+            )(homes[which], home_plan[which], home_info[which], *tables, *got_up, *got_down)
+
+        def all_arrived(tables, got_up, got_down, scaled):
+            theirs = arrived(0, tables, got_up, got_down, scaled)
+            mine = arrived(1, after(tables, theirs), got_up, got_down, scaled)
+            theirs = mate(theirs)
+            return jnp.where(core == 0, jnp.concatenate([mine, theirs], axis=1), jnp.concatenate([theirs, mine], axis=1))
 
         def shift(up_rows, down_rows):
             got_up = lax.ppermute(up_rows, 'expert', to_next)
@@ -486,13 +498,6 @@
         def second_rows(got, up_rows, down_rows):
             row = iota((up_rows.shape[0], 1), 0)
             return jnp.where(row < pass_up, got[0], up_rows), jnp.where(row < pass_down, got[1], down_rows)
-
-        def parts_of(total):
-            mine = jnp.where(core == 0, total[0], total[1])
-            return mine, mate(jnp.where(core == 0, total[1], total[0]))
-
-        def join(mine, theirs):
-            return jnp.where(core == 0, jnp.concatenate([mine, theirs], axis=1), jnp.concatenate([theirs, mine], axis=1))
 
         def table(v):
             return v.reshape(group, cap, half)
@@ -508,24 +513,24 @@
         all_dy = after(all_dy, out_up, out_down, cut)
 
         def block_spec(rows, width):
-            return pl.BlockSpec((1, rows, width), lambda e, count: (e, 0, 0))
+            return pl.BlockSpec((1, rows, width), lambda e, *tables: (e, 0, 0))
 
         def fixed_spec(w):
-            return pl.BlockSpec(w.shape, lambda e, count: (0, 0), pipeline_mode=pl.Buffered(1))
+            return pl.BlockSpec(w.shape, lambda e, *tables: (0, 0), pipeline_mode=pl.Buffered(1))
 
         def inner_grads_of(dy):
             f = pre_a.shape[1]
             return pl.pallas_call(
                 inner_kernel,
                 grid_spec=pltpu.PrefetchScalarGridSpec(
-                    num_scalar_prefetch=1, grid=(group,),
+                    num_scalar_prefetch=2, grid=(group,),
                     in_specs=[block_spec(8, toks), block_spec(toks, dim), fixed_spec(w2t), block_spec(cap, f), block_spec(cap, f)],
                     out_specs=[block_spec(cap, dim), block_spec(cap, f), block_spec(cap, f)]),
                 out_shape=[jax.ShapeDtypeStruct((group, cap, n), BF) for n in (dim, f, f)],
                 compiler_params=pltpu.CompilerParams(vmem_limit_bytes=VMEM_LIMIT),
                 cost_estimate=pl.CostEstimate(flops=2 * rows * dim * (toks + f), bytes_accessed=2 * rows * dim * 4, transcendentals=rows * f),
                 name='inner',
-            )(counts, own_info, dy, w2t, pre_a.reshape(group, cap, f), pre_b.reshape(group, cap, f))
+            )(counts, froms, own_info, dy, w2t, pre_a.reshape(group, cap, f), pre_b.reshape(group, cap, f))
 
         def input_grad(da, db, k):
             w1t, w3t = w13t_halves[k]
@@ -559,15 +564,14 @@
             da, db, g = da.reshape(rows, f), db.reshape(rows, f), g.reshape(rows, dim)
             dw1 = dot('cd,cf->df', x, da)
             out_first, out_last = after((out_first, out_last), dw1[:8, :TILE])
-            y = arrived(out_tables, home_info, win, (out_first[0], out_last[0]), (out_first[1], out_last[1]), True)
-            y = join(*parts_of(y))
+            y = all_arrived(out_tables, (out_first[0], out_last[0]), (out_first[1], out_last[1]), True)
             dx_second = second_rows(after(dx_first, y), dx_up[1], dx_down[1])
             dx_last = shift(*dx_second)
             db, hid_late = after((db, hid), *dx_second)
             dw3 = dot('cd,cf->df', x, db)
             dw2 = dot('cf,cd->fd', hid_late, g)
-            gx = parts_of(arrived(dx_tables, home_info, win, (dx_first[0], dx_last[0]), (dx_first[1], dx_last[1]), False))
-            return y, *gx, row_major(dw1)[None], row_major(dw3)[None], row_major(dw2)[None]
+            gx = all_arrived(dx_tables, (dx_first[0], dx_last[0]), (dx_first[1], dx_last[1]), False)
+            return y, gx, row_major(dw1)[None], row_major(dw3)[None], row_major(dw2)[None]
 
         def general():
             my_rank, my_taken = pick(rank, me), pick(taken.astype(I32), me) > 0
@@ -606,12 +610,9 @@
             first = one_pass(0)
             second = one_pass(cap)
             sums = [u + v for u, v in zip(first, second)]
-            gx = jnp.split(sums[1].astype(BF), 2, axis=1)
-            gx = [jnp.where(core == k, gx[0], gx[1]) for k in range(2)]
-            return sums[0].astype(BF), *gx, *[v[None] for v in sums[2:]]
+            return sums[0].astype(BF), sums[1].astype(BF), *[v[None] for v in sums[2:]]
 
         branches = [functools.partial(rest, tier) for tier in range(len(tiers))] + [general]
-        y, mine, theirs, dw1, dw3, dw2 = lax.switch(state, branches)
-        return y, join(mine, theirs), dw1, dw3, dw2
+        return lax.switch(state, branches)
 
     return jax.shard_map(layer, mesh=mesh, in_specs=(tok_spec,) * 4 + (w_spec,) * 3, out_specs=(tok_spec,) * 5, check_vma=False)

time: 1040 us -> 972 us (0.935)
  waiting for transfers between devices: 303 us -> 254 us
  Pallas kernels: 197 us -> 174 us
  local copies, waits for them, and re-layouts: 81 us -> 91.5 us
    ppermute x4, waiting for transfers between devices: 142 us -> 100 us  [shift(): got_up = lax.ppermute(up_rows, 'expert', to_next)]
    pallas_call x2, Pallas kernels: 63.3 us -> 51.6 us  [packed(): pl.pallas_call(functools.partial(pack_kernel, scaled), grid_spec=pltpu.Pr...]
    pallas_call x2 -> x4, Pallas kernels: 40.6 us -> 32.4 us  [arrived(): pl.pallas_call(functools.partial(arrive_kernel, scaled), grid_spec=pltpu....]
    select_n x13 -> x19, other arithmetic: 24.1 us -> 18.9 us  [the longest x2 12.8 us: all_arrived(): jnp.where(core == 0, jnp.concatenate([mine, theirs], axis=1), jnp.concate...]
    dot_general x10 -> x11, matrix products: 240 us -> 243 us  [dot(): return jnp.einsum(form, a, b, preferred_element_type=F32)]
    unnamed x65 -> x82, local copies, waits for them, and re-layouts: 46.5 us -> 47.5 us
  transfers between devices with their start and end apart: 14 -> 14, of which waited for: 9 -> 9; matrix products, arithmetic and copies ran while one was open for 36% -> 41% of each run, Pallas kernels for 9% -> 10%
where the time goes in v2:
time: 972 us; the launch traced here: 962 us
  waiting for transfers between devices  254 us (26%)
  matrix products  243 us (25%)
  Pallas kernels  174 us (18%)
  local copies, waits for them, and re-layouts  91.5 us (9%)
  other arithmetic  79.4 us (8%)
  blocking collectives  54.3 us (6%)
  between operations  25.6 us (3%)
  loops' own time  20.5 us (2%)
  starting transfers between devices  19.4 us (2%)
    dot_general x11, matrix products, dot(): return jnp.einsum(form, a, b, preferred_element_type=F32)  243 us
    ppermute x4, waiting for transfers between devices, shift(): got_up = lax.ppermute(up_rows, 'expert', to_next)  100 us
    ppermute x4, waiting for transfers between devices, shift(): got_down = lax.ppermute(down_rows, 'expert', to_prev)  78.2 us
    pallas_call x2, Pallas kernels, packed(): pl.pallas_call(functools.partial(pack_kernel, scaled), grid_spec=pltpu.Pr...  51.6 us
    unnamed x82, local copies, waits for them, and re-layouts  47.5 us
    pallas_call x2, Pallas kernels, input_grad(): pl.pallas_call(input_kernel, grid_spec=pltpu.PrefetchScalarGridSpec(num_s...  46.9 us
    all_gather x1, waiting for transfers between devices, layer(): all_x = lax.all_gather(tok_x, 'expert')  44.6 us
    pallas_call x1, Pallas kernels, inner_grads_of(): pl.pallas_call(inner_kernel, grid_spec=pltpu.PrefetchScalarGridSpec(num_s...  43.5 us
  transfers between devices with their start and end apart: 14, of which 9 were waited for; matrix products, arithmetic and copies ran while one was open for 41% of the time, Pallas kernels for 10%

profile of v2, /device:TPU:112, one launch (start us, length us, event | category | flops | bytes accessed | tf_op | source)
XLA Modules:
  0.0 962.4 jit_solution(14137280162996486549)
XLA Ops:
  8.9 24.7 %all-gather.3 = f32[8,4,768]{2,1,0:T(4,128)S(1)} all-gather(f32[1,4,768]{2,1,0:T(4,128)S(1)} %maximum_bitcast_fusion), channel_id=3, replica_groups=mesh['data'=2,'expert'=8] {'expert'}, dimensions={0}, use_global_device_ids=true | all-gather | bytes 110592 | tf_op jit(solution)/shard_map/all_gather | solution.py:270
  45.2 29.6 %pmax.7 = s32[]{:T(128)} all-reduce(s32[]{:T(128)S(6)} %select_n.856), channel_id=1, replica_groups=mesh['data'=2,'expert'=8] {'data','expert'}, use_global_device_ids=true, to_apply=%region_10.11 | all-reduce | flops 1 | bytes 8 | tf_op jit(solution)/shard_map/pmax | solution.py:306
  97.8 12.0 %copy.116 = bf16[1,1024,4096]{1,2,0:T(8,128)(2,1)} copy(bf16[1,1024,4096]{2,1,0:T(8,128)(2,1)} %param.18) | data formatting | bytes 16777216 | tf_op args[6]
  191.3 44.6 %all-gather.7.cloned.1.call-done = bf16[6144,4096]{1,0:T(8,128)(2,1)} async-done(((bf16[768,4096]{1,0:T(8,128)(2,1)}), bf16[6144,4096]{1,0:T(8,128)(2,1)}) %all-gather.7.cloned.1.call-update) | async-done | bytes 50331664 | tf_op jit(solution)/shard_map/all_gather | solution.py:266
  236.0 36.3 %convolution_convert_fusion.10 = bf16[8,384,4096]{2,1,0:T(8,128)(2,1)} fusion(bf16[8,384,768]{2,1,0:T(8,128)(2,1)} %fusion.42, bf16[8,768,4096]{2,1,0:T(8,128)(2,1)} %bitcast.441), kind=kOutput, calls=%fused_computation.153 | convolution fusion | flops 19339935744 | bytes 80216064 | tf_op jit(solution)/shard_map/gcs,gsd->gcd/dot_general | solution.py:22
  272.3 32.5 %convolution_convert_fusion.13 = bf16[3072,1024]{1,0:T(8,128)(2,1)S(1)} fusion(bf16[3072,4096]{1,0:T(8,128)(2,1)} %bitcast.448, bf16[1,4096,1024]{2,1,0:T(8,128)(2,1)} %param.17), kind=kOutput, calls=%fused_computation.164 | convolution fusion | flops 25772949504 | bytes 39845888 | tf_op jit(solution)/shard_map/cd,df->cf/dot_general | solution.py:22
  304.8 34.4 %convolution_convert_fusion.14 = bf16[3072,1024]{1,0:T(8,128)(2,1)S(1)} fusion(bf16[3072,4096]{1,0:T(8,128)(2,1)} %bitcast.449, bf16[1,4096,1024]{2,1,0:T(8,128)(2,1)} %param.16), kind=kOutput, calls=%fused_computation.165 | convolution fusion | flops 25772949504 | bytes 39845888 | tf_op jit(solution)/shard_map/cd,df->cf/dot_general | solution.py:22
  345.9 16.8 %convolution_convert_fusion.12 = bf16[3072,2048]{1,0:T(8,128)(2,1)} fusion(bf16[3072,1024]{1,0:T(8,128)(2,1)S(1)} %fusion.41, bf16[1024,2048]{0,1:T(8,128)(2,1)S(1)} %copy-done.48), kind=kOutput, calls=%fused_computation.160 | convolution fusion | flops 12891193344 | bytes 23068672 | tf_op jit(solution)/shard_map/cf,fd->cd/dot_general | solution.py:22
  364.0 19.3 %convolution_convert_fusion.11 = bf16[3072,2048]{1,0:T(8,128)(2,1)} fusion(bf16[3072,1024]{1,0:T(8,128)(2,1)} %copy-done.36, bf16[1024,2048]{0,1:T(8,128)(2,1)} %get-tuple-element.600), kind=kOutput, calls=%fused_computation.159 | convolution fusion | flops 12891193344 | bytes 23068672 | tf_op jit(solution)/shard_map/cf,fd->cd/dot_general | solution.py:22
  384.4 28.5 %pack.9 = (bf16[1136,2048]{1,0:T(8,128)(2,1)S(1)}, bf16[1136,2048]{1,0:T(8,128)(2,1)}, bf16[1136,2048]{1,0:T(8,128)(2,1)}, bf16[1136,2048]{1,0:T(8,128)(2,1)}) custom-call(s32[6]{0:T(128)S(1)} %copy-done.80, s32[6,4]{1,0:T(8,128)S(1)} %copy-done.66, s32[6,12]{1,0:T(8,128)S(1)} %copy-done.67, bf16[8,384,2048]{2,1,0:T(8,128)(2,1)} %bitcast.394, ...), custom_call_target="tpu_custom_call" | custom-call | flops 4831838208 | bytes 75497472 | tf_op jit(solution)/shard_map/pack/pallas_call | solution.py:458
  431.6 28.4 %all-gather.9.cloned.1.call-done = bf16[6144,4096]{1,0:T(8,128)(2,1)} async-done(((bf16[768,4096]{1,0:T(8,128)(2,1)}), bf16[6144,4096]{1,0:T(8,128)(2,1)}) %all-gather.9.cloned.1.call-update) | async-done | bytes 50331664 | tf_op jit(solution)/shard_map/all_gather | solution.py:267
  460.7 494.3 %conditional.1 = (bf16[768,4096]{1,0:T(8,128)(2,1)}, bf16[768,4096]{1,0:T(8,128)(2,1)}, f32[1,4096,1024]{2,1,0:T(8,128)}, f32[1,4096,1024]{2,1,0:T(8,128)}, f32[1,1024,4096]{2,1,0:T(8,128)}) conditional(s32[]{:T(128)} %clamp.3, (s32[]{:T(128)}, s32[2,1]{0,1:T(1,128)S(1)}, s32[2,6,24]{2,1,0:T(8,128)S(1)}, ...), branch_computations={%region_54.55_spmd, %region_55.56_spmd, %region_56.57_spmd, %regio... | conditional | flops 657602379776 | bytes 2084082560 | solution.py:616
  471.5 43.5 %inner.6 = (bf16[8,384,4096]{2,1,0:T(8,128)(2,1)}, bf16[8,384,1024]{2,1,0:T(8,128)(2,1)}, bf16[8,384,1024]{2,1,0:T(8,128)(2,1)}) custom-call(s32[8]{0:T(128)S(1)} %get-tuple-element.384.count_ref, s32[8]{0:T(128)S(1)} %get-tuple-element.385.from_ref, f32[8,8,768]{2,1,0:T(8,128)S(1)} %get-tuple-element.386.info, bf16[8,768,4096]{2,1,0:T(8,128)(2,1)} %get-tuple-element.387.dy, ...), custom_call_target="tpu_custom_call" | custom-call | flops 45097156608 | bytes 100663296 | tf_op jit(solution)/shard_map/cond/branch_2_fun/inner/pallas_call | solution.py:523
  515.0 22.3 %input_grad.12 = bf16[8,384,2048]{2,1,0:T(8,128)(2,1)} custom-call(s32[8]{0:T(128)S(1)} %get-tuple-element.384.count_ref, bf16[8,384,1024]{2,1,0:T(8,128)(2,1)} %get-tuple-element.427.da, bf16[8,384,1024]{2,1,0:T(8,128)(2,1)} %get-tuple-element.429.db, bf16[1024,2048]{1,0:T(8,128)(2,1)S(1)} %copy-done.47, bf16[1024,2048]{1,0:T(8,128)(2,1)S(1)} %copy-done.43), custom_call_target="tpu_custom_call" | custom-call | flops 25769803776 | bytes 25165824 | tf_op jit(solution)/shard_map/cond/branch_2_fun/input_grad/pallas_call | solution.py:538
  547.1 76.8 %collective-permute-done.23.down1 = bf16[880,2048]{1,0:T(8,128)(2,1)S(1)} collective-permute-done((bf16[880,2048]{1,0:T(8,128)(2,1)}, bf16[880,2048]{1,0:T(8,128)(2,1)S(1)}, u32[]{:S(2)}, u32[]{:S(2)}) %collective-permute-start.23) | collective-permute-done | bytes 3604512 | tf_op jit(solution)/shard_map/cond/branch_2_fun/ppermute | solution.py:495
  635.4 24.6 %input_grad.13.tab0 = bf16[8,384,2048]{2,1,0:T(8,128)(2,1)} custom-call(s32[8]{0:T(128)S(1)} %get-tuple-element.384.count_ref, bf16[8,384,1024]{2,1,0:T(8,128)(2,1)} %get-tuple-element.427.da, bf16[8,384,1024]{2,1,0:T(8,128)(2,1)} %get-tuple-element.429.db, bf16[1024,2048]{1,0:T(8,128)(2,1)} %get-tuple-element.406.w1t, bf16[1024,2048]{1,0:T(8,128)(2,1)} %get-tuple-element.407.w3t), custom_call_target="tpu_custom_call" | custom-call | flops 25769803776 | bytes 25165824 | tf_op jit(solution)/shard_map/cond/branch_2_fun/input_grad/pallas_call | solution.py:538
  660.1 23.2 %pack.7 = (bf16[880,2048]{1,0:T(8,128)(2,1)}, bf16[880,2048]{1,0:T(8,128)(2,1)}, bf16[880,2048]{1,0:T(8,128)(2,1)}, bf16[880,2048]{1,0:T(8,128)(2,1)}) custom-call(s32[6]{0:T(128)S(1)} %get-tuple-element.401.dev_ref, s32[6,4]{1,0:T(8,128)S(1)} %get-tuple-element.402.seg_ref, s32[6,12]{1,0:T(8,128)S(1)} %get-tuple-element.403.low_ref, ...), custom_call_target="tpu_custom_call" | custom-call | flops 4831838208 | bytes 75497472 | tf_op jit(solution)/shard_map/cond/branch_2_fun/pack/pallas_call | solution.py:458
  683.2 26.2 %collective-permute-done.24.up2 = bf16[880,2048]{1,0:T(8,128)(2,1)} collective-permute-done((bf16[880,2048]{1,0:T(8,128)(2,1)}, bf16[880,2048]{1,0:T(8,128)(2,1)}, u32[]{:S(2)}, u32[]{:S(2)}) %collective-permute-start.24) | collective-permute-done | bytes 3604512 | tf_op jit(solution)/shard_map/cond/branch_2_fun/ppermute | solution.py:494
  724.1 9.0 arrive.25
  733.1 33.6 %convolution_bitcast_fusion.8 = f32[1,4096,1024]{2,1,0:T(8,128)} fusion(bf16[3072,1024]{1,0:T(8,128)(2,1)} %bitcast.476, bf16[3072,4096]{1,0:T(8,128)(2,1)} %get-tuple-element.428), kind=kOutput, calls=%fused_computation.32 | convolution fusion | flops 25769803776 | bytes 48234496 | tf_op jit(solution)/shard_map/cond/branch_2_fun/cd,cf->df/dot_general | solution.py:22
  775.2 27.5 %collective-permute-done.28.up1 = bf16[880,2048]{1,0:T(8,128)(2,1)S(1)} collective-permute-done((bf16[880,2048]{1,0:T(8,128)(2,1)}, bf16[880,2048]{1,0:T(8,128)(2,1)S(1)}, u32[]{:S(2)}, u32[]{:S(2)}) %collective-permute-start.28) | collective-permute-done | bytes 3604512 | tf_op jit(solution)/shard_map/cond/branch_2_fun/ppermute | solution.py:494
  811.2 33.6 %convolution_bitcast_fusion.7 = f32[1,4096,1024]{2,1,0:T(8,128)} fusion(bf16[3072,1024]{1,0:T(8,128)(2,1)} %bitcast.472, bf16[3072,4096]{1,0:T(8,128)(2,1)} %get-tuple-element.428), kind=kOutput, calls=%fused_computation.31 | convolution fusion | flops 25769803776 | bytes 48234496 | tf_op jit(solution)/shard_map/cond/branch_2_fun/cd,cf->df/dot_general | solution.py:22
  844.8 44.2 %collective-permute-done.30.up2 = bf16[880,2048]{1,0:T(8,128)(2,1)S(1)} collective-permute-done((bf16[880,2048]{1,0:T(8,128)(2,1)}, bf16[880,2048]{1,0:T(8,128)(2,1)S(1)}, u32[]{:S(2)}, u32[]{:S(2)}) %collective-permute-start.30) | collective-permute-done | bytes 3604512 | tf_op jit(solution)/shard_map/cond/branch_2_fun/ppermute | solution.py:494
  900.0 33.9 %convolution_bitcast_fusion.6 = f32[1,1024,4096]{2,1,0:T(8,128)} fusion(bf16[3072,1024]{1,0:T(8,128)(2,1)} %get-tuple-element.432, bf16[3072,4096]{1,0:T(8,128)(2,1)} %bitcast.456), kind=kOutput, calls=%fused_computation.30 | convolution fusion | flops 25769803776 | bytes 48234496 | tf_op jit(solution)/shard_map/cond/branch_2_fun/cf,cd->fd/dot_general | solution.py:22
  (337 shorter events, 211.0 us)
Async XLA Ops:
  7.2 228.8 %all-gather.7.cloned.1.call-start = ((), (), s32[]{:S(2)}) async-start(), calls=%async_computation.4 | async-start | bytes 56623104 | tf_op jit(solution)/shard_map/all_gather | solution.py:266
  8.0 452.1 %all-gather.9.cloned.1.call-start = ((), (), s32[]{:S(2)}) async-start(), calls=%async_computation.5 | async-start | bytes 56623104 | tf_op jit(solution)/shard_map/all_gather | solution.py:267
  33.7 117.3 %copy-start.60 = (f32[8,768]{1,0:T(8,128)}, f32[8,768]{1,0:T(8,128)S(1)}, u32[]{:S(2)}) copy-start(f32[8,768]{1,0:T(8,128)S(1)} %get-tuple-element.924) | copy-start | bytes 73732
  33.8 76.0 %copy-start.58 = (pred[8,8,768]{2,1,0:T(8,128)(4,1)}, pred[8,8,768]{2,1,0:T(8,128)(4,1)S(1)}, u32[]{:S(2)}) copy-start(pred[8,8,768]{2,1,0:T(8,128)(4,1)S(1)} %fusion.58) | copy-start | bytes 147460
  362.7 21.7 %collective-permute-start.44 = (bf16[3072,2048]{1,0:T(8,128)(2,1)}, bf16[3072,2048]{1,0:T(8,128)(2,1)}, u32[]{:S(2)}, u32[]{:S(2)}) collective-permute-start(bf16[3072,2048]{1,0:T(8,128)(2,1)} %convolution_convert_fusion.12), channel_id=1, source_target_pairs={{0,1},{1,0},{2,3},{3,2},{4,5},{5,4},{6,7},{7,6},{8,9},{9,8},{10,11... | collective-permute-start | bytes 37748744 | tf_op jit(solution)/shard_map/ppermute | solution.py:264
  425.0 35.7 %copy-start.55 = (f32[2,6,8,128]{3,2,1,0:T(8,128)S(1)}, f32[2,6,8,128]{3,2,1,0:T(8,128)}, u32[]{:S(2)}) copy-start(f32[2,6,8,128]{3,2,1,0:T(8,128)} %stack.282) | copy-start | bytes 147460
  425.0 35.7 %copy-start.57 = (s32[8,8,768]{2,1,0:T(8,128)S(1)}, s32[8,8,768]{2,1,0:T(8,128)}, u32[]{:S(2)}) copy-start(s32[8,8,768]{2,1,0:T(8,128)} %copy-done.56) | copy-start | bytes 589828
  425.0 35.7 %copy-start.59 = (pred[8,8,768]{2,1,0:T(8,128)(4,1)S(1)}, pred[8,8,768]{2,1,0:T(8,128)(4,1)}, u32[]{:S(2)}) copy-start(pred[8,8,768]{2,1,0:T(8,128)(4,1)} %copy-done.58) | copy-start | bytes 147460
  471.4 43.6 %copy-start.43 = (bf16[1024,2048]{1,0:T(8,128)(2,1)S(1)}, bf16[1024,2048]{1,0:T(8,128)(2,1)}, u32[]{:S(2)}) copy-start(bf16[1024,2048]{1,0:T(8,128)(2,1)} %get-tuple-element.394.w3t) | copy-start | bytes 12582916 | tf_op jit(solution)/shard_map/cond
  471.5 43.6 %copy-start.47 = (bf16[1024,2048]{1,0:T(8,128)(2,1)S(1)}, bf16[1024,2048]{1,0:T(8,128)(2,1)}, u32[]{:S(2)}) copy-start(bf16[1024,2048]{1,0:T(8,128)(2,1)} %get-tuple-element.393.w1t) | copy-start | bytes 12582916 | tf_op jit(solution)/shard_map/cond
  515.0 111.1 %copy-start.3 = (bf16[1136,2048]{1,0:T(8,128)(2,1)S(1)}, bf16[1136,2048]{1,0:T(8,128)(2,1)}, u32[]{:S(2)}) copy-start(bf16[1136,2048]{1,0:T(8,128)(2,1)} %get-tuple-element.396) | copy-start | bytes 13959172 | tf_op jit(solution)/shard_map/cond
  537.3 91.4 %slice-start.4 = ((s8[4653056]{0:T(1024)(128)(4,1)}), s8[4194304]{0:T(1024)(128)(4,1)S(1)}, s32[]{:S(2)}) async-start(s8[4653056]{0:T(1024)(128)(4,1)} %bitcast.403), calls=%async_computation.10 | async-start | bytes 8388608 | tf_op jit(solution)/shard_map/cond
  537.3 122.8 %collective-permute-start.26 = (bf16[8,384,2048]{2,1,0:T(8,128)(2,1)}, bf16[8,384,2048]{2,1,0:T(8,128)(2,1)}, u32[]{:S(2)}, u32[]{:S(2)}) collective-permute-start(bf16[8,384,2048]{2,1,0:T(8,128)(2,1)} %input_grad.12), channel_id=1, source_target_pairs={{0,1},{1,0},{2,3},{3,2},{4,5},{5,4},{6,7},{7,6},{8,9},{9,8},{10,11... | collective-permute-start | bytes 37748744 | tf_op jit(solution)/shard_map/cond/branch_2_fun/ppermute | solution.py:264
  543.7 80.1 %collective-permute-start.23 = (bf16[880,2048]{1,0:T(8,128)(2,1)}, bf16[880,2048]{1,0:T(8,128)(2,1)S(1)}, u32[]{:S(2)}, u32[]{:S(2)}) collective-permute-start(bf16[880,2048]{1,0:T(8,128)(2,1)} %get-tuple-element.382), channel_id=1, source_target_pairs={{0,6},{1,7},{2,0},{3,1},{4,2},{5,3},{6,4},{7,5},{8,14},{9,15},{10,... | collective-permute-start | bytes 10813448 | tf_op jit(solution)/shard_map/cond/branch_2_fun/ppermute | solution.py:495
  544.7 81.4 %collective-permute-start.22 = (bf16[880,2048]{1,0:T(8,128)(2,1)}, bf16[880,2048]{1,0:T(8,128)(2,1)S(1)}, u32[]{:S(2)}, u32[]{:S(2)}) collective-permute-start(bf16[880,2048]{1,0:T(8,128)(2,1)} %get-tuple-element.381), channel_id=1, source_target_pairs={{0,2},{1,3},{2,4},{3,5},{4,6},{5,7},{6,0},{7,1},{8,10},{9,11},{10,... | collective-permute-start | bytes 10813448 | tf_op jit(solution)/shard_map/cond/branch_2_fun/ppermute | solution.py:494
  628.7 80.7 %collective-permute-start.24 = (bf16[880,2048]{1,0:T(8,128)(2,1)}, bf16[880,2048]{1,0:T(8,128)(2,1)}, u32[]{:S(2)}, u32[]{:S(2)}) collective-permute-start(bf16[880,2048]{1,0:T(8,128)(2,1)} %slice_select_fusion.5), channel_id=1, source_target_pairs={{0,2},{1,3},{2,4},{3,5},{4,6},{5,7},{6,0},{7,1},{8,10},{9,11},{10,... | collective-permute-start | bytes 10813448 | tf_op jit(solution)/shard_map/cond/branch_2_fun/ppermute | solution.py:494
  631.0 79.9 %collective-permute-start.25 = (bf16[880,2048]{1,0:T(8,128)(2,1)}, bf16[880,2048]{1,0:T(8,128)(2,1)}, u32[]{:S(2)}, u32[]{:S(2)}) collective-permute-start(bf16[880,2048]{1,0:T(8,128)(2,1)} %slice_select_fusion.4), channel_id=1, source_target_pairs={{0,6},{1,7},{2,0},{3,1},{4,2},{5,3},{6,4},{7,5},{8,14},{9,15},{10,... | collective-permute-start | bytes 10813448 | tf_op jit(solution)/shard_map/cond/branch_2_fun/ppermute | solution.py:495
  719.8 46.9 %collective-permute-start.27 = (bf16[768,2048]{1,0:T(8,128)(2,1)S(1)}, bf16[768,2048]{1,0:T(8,128)(2,1)}, u32[]{:S(2)}, u32[]{:S(2)}) collective-permute-start(bf16[768,2048]{1,0:T(8,128)(2,1)S(1)} %arrive.24), channel_id=1, source_target_pairs={{0,1},{1,0},{2,3},{3,2},{4,5},{5,4},{6,7},{7,6},{8,9},{9,8},{10,11... | collective-permute-start | bytes 9437192 | tf_op jit(solution)/shard_map/cond/branch_2_fun/ppermute | solution.py:264
  719.9 82.8 %collective-permute-start.28 = (bf16[880,2048]{1,0:T(8,128)(2,1)}, bf16[880,2048]{1,0:T(8,128)(2,1)S(1)}, u32[]{:S(2)}, u32[]{:S(2)}) collective-permute-start(bf16[880,2048]{1,0:T(8,128)(2,1)} %get-tuple-element.409), channel_id=1, source_target_pairs={{0,2},{1,3},{2,4},{3,5},{4,6},{5,7},{6,0},{7,1},{8,10},{9,11},{10,... | collective-permute-start | bytes 10813448 | tf_op jit(solution)/shard_map/cond/branch_2_fun/ppermute | solution.py:494
  720.0 82.7 %collective-permute-start.29 = (bf16[880,2048]{1,0:T(8,128)(2,1)}, bf16[880,2048]{1,0:T(8,128)(2,1)S(1)}, u32[]{:S(2)}, u32[]{:S(2)}) collective-permute-start(bf16[880,2048]{1,0:T(8,128)(2,1)} %get-tuple-element.411), channel_id=1, source_target_pairs={{0,6},{1,7},{2,0},{3,1},{4,2},{5,3},{6,4},{7,5},{8,14},{9,15},{10,... | collective-permute-start | bytes 10813448 | tf_op jit(solution)/shard_map/cond/branch_2_fun/ppermute | solution.py:495
  766.7 36.0 %copy-start.50 = (bf16[880,2048]{1,0:T(8,128)(2,1)S(1)}, bf16[880,2048]{1,0:T(8,128)(2,1)}, u32[]{:S(2)}) copy-start(bf16[880,2048]{1,0:T(8,128)(2,1)} %get-tuple-element.412) | copy-start | bytes 10813444 | tf_op jit(solution)/shard_map/cond
  807.9 81.1 %collective-permute-start.30 = (bf16[880,2048]{1,0:T(8,128)(2,1)}, bf16[880,2048]{1,0:T(8,128)(2,1)S(1)}, u32[]{:S(2)}, u32[]{:S(2)}) collective-permute-start(bf16[880,2048]{1,0:T(8,128)(2,1)} %broadcast_select_fusion.5), channel_id=1, source_target_pairs={{0,2},{1,3},{2,4},{3,5},{4,6},{5,7},{6,0},{7,1},{8,10},{9,11},{10,... | collective-permute-start | bytes 10813448 | tf_op jit(solution)/shard_map/cond/branch_2_fun/ppermute | solution.py:494
  808.7 82.1 %collective-permute-start.31 = (bf16[880,2048]{1,0:T(8,128)(2,1)}, bf16[880,2048]{1,0:T(8,128)(2,1)S(1)}, u32[]{:S(2)}, u32[]{:S(2)}) collective-permute-start(bf16[880,2048]{1,0:T(8,128)(2,1)} %broadcast_select_fusion.4), channel_id=1, source_target_pairs={{0,6},{1,7},{2,0},{3,1},{4,2},{5,3},{6,4},{7,5},{8,14},{9,15},{10,... | collective-permute-start | bytes 10813448 | tf_op jit(solution)/shard_map/cond/branch_2_fun/ppermute | solution.py:495
  899.9 41.2 %collective-permute-start.32 = (bf16[768,2048]{1,0:T(8,128)(2,1)S(1)}, bf16[768,2048]{1,0:T(8,128)(2,1)S(1)}, u32[]{:S(2)}, u32[]{:S(2)}) collective-permute-start(bf16[768,2048]{1,0:T(8,128)(2,1)S(1)} %arrive.26), channel_id=1, source_target_pairs={{0,1},{1,0},{2,3},{3,2},{4,5},{5,4},{6,7},{7,6},{8,9},{9,8},{10,11... | collective-permute-start | bytes 9437192 | tf_op jit(solution)/shard_map/cond/branch_2_fun/ppermute | solution.py:264
  (29 other events, 427.8 us)
Sparse Core Ops, SparseCore 0:
  9.6 226.2 all-gather.6
  237.5 222.5 all-gather.8

commit v3 on v2

--- a/solution.py
+++ b/solution.py
@@ -188,7 +188,7 @@
     e = pl.program_id(0)
     cap, dim = g_ref.shape[1:]
     toks = dy.shape[1]
-    step = dim // 4
+    step, narrow = dim // 4, da_ref.shape[2] // 4
     count, begin = count_ref[e], from_ref[e]
 
     def fill(n, begin, span):
@@ -197,14 +197,25 @@
             match = vals[0:1, :] == iota((n, span), 0).astype(F32)
             gate = jnp.sum(jnp.where(match, vals[1:2, :], 0.0), axis=1, keepdims=True)
             onehot = match.astype(BF)
-            for c in range(0, dim, step):
-                got = jnp.dot(onehot, dy[0, pl.ds(begin, span), c:c + step], preferred_element_type=F32)
-                g_ref[0, :n, c:c + step] = (gate * got).astype(BF)
-            dh = jnp.dot(g_ref[0, :n], w2t[...], preferred_element_type=F32).astype(BF).astype(F32)
-            a, b = a_ref[0, :n].astype(F32), b_ref[0, :n].astype(F32)
-            sig = jax.nn.sigmoid(a)
-            da_ref[0, :n] = (dh * b * (sig * (1.0 + a * (1.0 - sig)))).astype(BF)
-            db_ref[0, :n] = (dh * (a * sig)).astype(BF)
+
+            def outer(k, carry):
+                at = pl.ds(pl.multiple_of(k * step, step), step)
+                got = jnp.dot(onehot, dy[0, pl.ds(begin, span), at], preferred_element_type=F32)
+                g_ref[0, :n, at] = (gate * got).astype(BF)
+                return carry
+
+            lax.fori_loop(0, dim // step, outer, 0)
+
+            def hidden(k, carry):
+                at = pl.ds(pl.multiple_of(k * narrow, narrow), narrow)
+                dh = jnp.dot(g_ref[0, :n], w2t[:, at], preferred_element_type=F32).astype(BF).astype(F32)
+                a, b = a_ref[0, :n, at].astype(F32), b_ref[0, :n, at].astype(F32)
+                sig = jax.nn.sigmoid(a)
+                da_ref[0, :n, at] = (dh * b * (sig * (1.0 + a * (1.0 - sig)))).astype(BF)
+                db_ref[0, :n, at] = (dh * (a * sig)).astype(BF)
+                return carry
+
+            lax.fori_loop(0, da_ref.shape[2] // narrow, hidden, 0)
         if n < cap:
             for ref in (g_ref, da_ref, db_ref):
                 ref[0, n:] = jnp.zeros((cap - n, ref.shape[2]), BF)
@@ -252,7 +263,7 @@
         rows = group * cap
         half = dim // 2
         tiles = toks // TILE
-        tiers = [toks * n // 48 for n in (44, 49, 55, 71)]
+        tiers = [toks * n // 48 for n in (49, 54, 60, 71)]
         stage = tiers[-1]
         place = 2 * stage
         me = lax.axis_index('expert')
@@ -551,11 +562,12 @@
             size = tiers[tier]
             out_first = shift(*cut[tier])
             g, da, db = inner_grads_of(all_dy)
+            out_second = second_rows(after(out_first, da), out_up[1][:size], out_down[1][:size])
+            out_last = shift(*out_second)
+            da, db = after((da, db), *out_second)
             theirs = input_grad(da, db, 1)
             dx_got = mate(theirs)
-            out_second = second_rows(after(out_first, theirs), out_up[1][:size], out_down[1][:size])
-            out_last = shift(*out_second)
-            ours = input_grad(*after((da, db), *out_second), 0)
+            ours = input_grad(after(da, theirs), db, 0)
             dx_tables = (ours, dx_got)
             dx_up, dx_down = packed(dx_tables, size, False)
             dx_first = shift(dx_up[0], dx_down[0])

time: 972 us -> 916 us (0.942)
  waiting for transfers between devices: 254 us -> 197 us
  Pallas kernels: 174 us -> 187 us
    ppermute x4, waiting for transfers between devices: 78.2 us -> 24.9 us  [shift(): got_down = lax.ppermute(down_rows, 'expert', to_prev)]
  transfers between devices with their start and end apart: 14 -> 14, of which waited for: 9 -> 8; matrix products, arithmetic and copies ran while one was open for 41% -> 43% of each run, Pallas kernels for 10% -> 16%
where the time goes in v3:
time: 916 us; the launch traced here: 907 us
  matrix products  247 us (27%)
  waiting for transfers between devices  197 us (22%)
  Pallas kernels  187 us (20%)
  local copies, waits for them, and re-layouts  88.4 us (10%)
  other arithmetic  78.5 us (9%)
  blocking collectives  54.5 us (6%)
  between operations  24.9 us (3%)
  loops' own time  16.8 us (2%)
  starting transfers between devices  12.5 us (1%)
    dot_general x11, matrix products, dot(): return jnp.einsum(form, a, b, preferred_element_type=F32)  247 us
    ppermute x4, waiting for transfers between devices, shift(): got_up = lax.ppermute(up_rows, 'expert', to_next)  99 us
    pallas_call x2, Pallas kernels, packed(): pl.pallas_call(functools.partial(pack_kernel, scaled), grid_spec=pltpu.Pr...  55.5 us
    pallas_call x1, Pallas kernels, inner_grads_of(): pl.pallas_call(inner_kernel, grid_spec=pltpu.PrefetchScalarGridSpec(num_s...  50.6 us
    pallas_call x2, Pallas kernels, input_grad(): pl.pallas_call(input_kernel, grid_spec=pltpu.PrefetchScalarGridSpec(num_s...  48.4 us
    unnamed x82, local copies, waits for them, and re-layouts  47.1 us
    all_gather x1, waiting for transfers between devices, layer(): all_x = lax.all_gather(tok_x, 'expert')  45.2 us
    pallas_call x4, Pallas kernels, arrived(): pl.pallas_call(functools.partial(arrive_kernel, scaled), grid_spec=pltpu....  32.6 us
  transfers between devices with their start and end apart: 14, of which 8 were waited for; matrix products, arithmetic and copies ran while one was open for 43% of the time, Pallas kernels for 16%

profile of v3, /device:TPU:112, one launch (start us, length us, event | category | flops | bytes accessed | tf_op | source)
XLA Modules:
  0.0 906.5 jit_solution(17729210594172746274)
XLA Ops:
  8.9 24.7 %all-gather.3 = f32[8,4,768]{2,1,0:T(4,128)S(1)} all-gather(f32[1,4,768]{2,1,0:T(4,128)S(1)} %maximum_bitcast_fusion), channel_id=3, replica_groups=mesh['data'=2,'expert'=8] {'expert'}, dimensions={0}, use_global_device_ids=true | all-gather | bytes 110592 | tf_op jit(solution)/shard_map/all_gather | solution.py:281
  45.2 29.8 %pmax.7 = s32[]{:T(128)} all-reduce(s32[]{:T(128)S(6)} %select_n.856), channel_id=1, replica_groups=mesh['data'=2,'expert'=8] {'data','expert'}, use_global_device_ids=true, to_apply=%region_10.11 | all-reduce | flops 1 | bytes 8 | tf_op jit(solution)/shard_map/pmax | solution.py:317
  97.7 12.0 %copy.116 = bf16[1,1024,4096]{1,2,0:T(8,128)(2,1)} copy(bf16[1,1024,4096]{2,1,0:T(8,128)(2,1)} %param.18) | data formatting | bytes 16777216 | tf_op args[6]
  190.7 45.2 %all-gather.7.cloned.1.call-done = bf16[6144,4096]{1,0:T(8,128)(2,1)} async-done(((bf16[768,4096]{1,0:T(8,128)(2,1)}), bf16[6144,4096]{1,0:T(8,128)(2,1)}) %all-gather.7.cloned.1.call-update) | async-done | bytes 50331664 | tf_op jit(solution)/shard_map/all_gather | solution.py:277
  236.0 36.1 %convolution_convert_fusion.10 = bf16[8,384,4096]{2,1,0:T(8,128)(2,1)} fusion(bf16[8,384,768]{2,1,0:T(8,128)(2,1)} %fusion.42, bf16[8,768,4096]{2,1,0:T(8,128)(2,1)} %bitcast.441), kind=kOutput, calls=%fused_computation.153 | convolution fusion | flops 19339935744 | bytes 80216064 | tf_op jit(solution)/shard_map/gcs,gsd->gcd/dot_general | solution.py:22
  272.0 32.6 %convolution_convert_fusion.13 = bf16[3072,1024]{1,0:T(8,128)(2,1)S(1)} fusion(bf16[3072,4096]{1,0:T(8,128)(2,1)} %bitcast.448, bf16[1,4096,1024]{2,1,0:T(8,128)(2,1)} %param.17), kind=kOutput, calls=%fused_computation.164 | convolution fusion | flops 25772949504 | bytes 39845888 | tf_op jit(solution)/shard_map/cd,df->cf/dot_general | solution.py:22
  304.7 34.4 %convolution_convert_fusion.14 = bf16[3072,1024]{1,0:T(8,128)(2,1)S(1)} fusion(bf16[3072,4096]{1,0:T(8,128)(2,1)} %bitcast.449, bf16[1,4096,1024]{2,1,0:T(8,128)(2,1)} %param.16), kind=kOutput, calls=%fused_computation.165 | convolution fusion | flops 25772949504 | bytes 39845888 | tf_op jit(solution)/shard_map/cd,df->cf/dot_general | solution.py:22
  345.8 20.0 %convolution_convert_fusion.12 = bf16[3072,2048]{1,0:T(8,128)(2,1)} fusion(bf16[3072,1024]{1,0:T(8,128)(2,1)S(1)} %fusion.41, bf16[1024,2048]{0,1:T(8,128)(2,1)} %get-tuple-element.602), kind=kOutput, calls=%fused_computation.160 | convolution fusion | flops 12891193344 | bytes 23068672 | tf_op jit(solution)/shard_map/cf,fd->cd/dot_general | solution.py:22
  367.1 19.3 %convolution_convert_fusion.11 = bf16[3072,2048]{1,0:T(8,128)(2,1)} fusion(bf16[3072,1024]{1,0:T(8,128)(2,1)} %copy-done.37, bf16[1024,2048]{0,1:T(8,128)(2,1)} %get-tuple-element.604), kind=kOutput, calls=%fused_computation.159 | convolution fusion | flops 12891193344 | bytes 23068672 | tf_op jit(solution)/shard_map/cf,fd->cd/dot_general | solution.py:22
  387.6 32.5 %pack.9 = (bf16[1136,2048]{1,0:T(8,128)(2,1)S(1)}, bf16[1136,2048]{1,0:T(8,128)(2,1)}, bf16[1136,2048]{1,0:T(8,128)(2,1)S(1)}, bf16[1136,2048]{1,0:T(8,128)(2,1)}) custom-call(s32[6]{0:T(128)S(1)} %copy-done.91, s32[6,4]{1,0:T(8,128)S(1)} %copy-done.71, s32[6,12]{1,0:T(8,128)S(1)} %copy-done.74, bf16[8,384,2048]{2,1,0:T(8,128)(2,1)} %bitcast.394, ...), custom_call_target="tpu_custom_call" | custom-call | flops 4831838208 | bytes 75497472 | tf_op jit(solution)/shard_map/pack/pallas_call | solution.py:469
  434.8 25.3 %all-gather.9.cloned.1.call-done = bf16[6144,4096]{1,0:T(8,128)(2,1)} async-done(((bf16[768,4096]{1,0:T(8,128)(2,1)}), bf16[6144,4096]{1,0:T(8,128)(2,1)}) %all-gather.9.cloned.1.call-update) | async-done | bytes 50331664 | tf_op jit(solution)/shard_map/all_gather | solution.py:278
  460.7 438.7 %conditional.1 = (bf16[768,4096]{1,0:T(8,128)(2,1)}, bf16[768,4096]{1,0:T(8,128)(2,1)}, f32[1,4096,1024]{2,1,0:T(8,128)}, f32[1,4096,1024]{2,1,0:T(8,128)}, f32[1,1024,4096]{2,1,0:T(8,128)}) conditional(s32[]{:T(128)} %clamp.3, (s32[]{:T(128)}, s32[2,1]{0,1:T(1,128)S(1)}, s32[2,6,24]{2,1,0:T(8,128)S(1)}, ...), branch_computations={%region_54.55_spmd, %region_55.56_spmd, %region_56.57_spmd, %regio... | conditional | flops 657602379776 | bytes 2084082560 | solution.py:628
  472.6 50.6 %inner.5 = (bf16[8,384,4096]{2,1,0:T(8,128)(2,1)}, bf16[8,384,1024]{2,1,0:T(8,128)(2,1)}, bf16[8,384,1024]{2,1,0:T(8,128)(2,1)}) custom-call(s32[8]{0:T(128)} %copy-done.100, s32[8]{0:T(128)} %copy-done.105, f32[8,8,768]{2,1,0:T(8,128)S(1)} %get-tuple-element.328.info, bf16[8,768,4096]{2,1,0:T(8,128)(2,1)} %get-tuple-element.329.dy, ...), custom_call_target="tpu_custom_call" | custom-call | flops 45097156608 | bytes 100663296 | tf_op jit(solution)/shard_map/cond/branch_1_fun/inner/pallas_call | solution.py:534
  523.2 24.9 %collective-permute-done.12.down1 = bf16[864,2048]{1,0:T(8,128)(2,1)S(1)} collective-permute-done((bf16[864,2048]{1,0:T(8,128)(2,1)}, bf16[864,2048]{1,0:T(8,128)(2,1)S(1)}, u32[]{:S(2)}, u32[]{:S(2)}) %collective-permute-start.12) | collective-permute-done | bytes 3538976 | tf_op jit(solution)/shard_map/cond/branch_1_fun/ppermute | solution.py:506
  555.8 23.7 %input_grad.10 = bf16[8,384,2048]{2,1,0:T(8,128)(2,1)} custom-call(s32[8]{0:T(128)S(1)} %copy-done.101, bf16[8,384,1024]{2,1,0:T(8,128)(2,1)} %get-tuple-element.370.da, bf16[8,384,1024]{2,1,0:T(8,128)(2,1)} %get-tuple-element.372.db, bf16[1024,2048]{1,0:T(8,128)(2,1)} %get-tuple-element.346.w1t, bf16[1024,2048]{1,0:T(8,128)(2,1)S(1)} %copy-done.45), custom_call_target="tpu_custom_call" | custom-call | flops 25769803776 | bytes 25165824 | tf_op jit(solution)/shard_map/cond/branch_1_fun/input_grad/pallas_call | solution.py:549
  584.3 24.6 %input_grad.11.tab0 = bf16[8,384,2048]{2,1,0:T(8,128)(2,1)} custom-call(s32[8]{0:T(128)S(1)} %copy-done.101, bf16[8,384,1024]{2,1,0:T(8,128)(2,1)} %get-tuple-element.370.da, bf16[8,384,1024]{2,1,0:T(8,128)(2,1)} %get-tuple-element.372.db, bf16[1024,2048]{1,0:T(8,128)(2,1)} %get-tuple-element.349.w1t, bf16[1024,2048]{1,0:T(8,128)(2,1)} %get-tuple-element.350.w3t), custom_call_target="tpu_custom_call" | custom-call | flops 25769803776 | bytes 25165824 | tf_op jit(solution)/shard_map/cond/branch_1_fun/input_grad/pallas_call | solution.py:549
  608.9 22.9 %pack.6 = (bf16[864,2048]{1,0:T(8,128)(2,1)}, bf16[864,2048]{1,0:T(8,128)(2,1)}, bf16[864,2048]{1,0:T(8,128)(2,1)}, bf16[864,2048]{1,0:T(8,128)(2,1)}) custom-call(s32[6]{0:T(128)S(1)} %get-tuple-element.343.dev_ref, s32[6,4]{1,0:T(8,128)S(1)} %get-tuple-element.344.seg_ref, s32[6,12]{1,0:T(8,128)S(1)} %get-tuple-element.345.low_ref, ...), custom_call_target="tpu_custom_call" | custom-call | flops 4831838208 | bytes 75497472 | tf_op jit(solution)/shard_map/cond/branch_1_fun/pack/pallas_call | solution.py:469
  631.9 28.2 %collective-permute-done.13.up2 = bf16[864,2048]{1,0:T(8,128)(2,1)} collective-permute-done((bf16[864,2048]{1,0:T(8,128)(2,1)}, bf16[864,2048]{1,0:T(8,128)(2,1)}, u32[]{:S(2)}, u32[]{:S(2)}) %collective-permute-start.13) | collective-permute-done | bytes 3538976 | tf_op jit(solution)/shard_map/cond/branch_1_fun/ppermute | solution.py:505
  660.1 9.0 arrive.20
  681.6 33.8 %convolution_bitcast_fusion.5 = f32[1,4096,1024]{2,1,0:T(8,128)} fusion(bf16[3072,1024]{1,0:T(8,128)(2,1)} %bitcast.476, bf16[3072,4096]{1,0:T(8,128)(2,1)} %get-tuple-element.371), kind=kOutput, calls=%fused_computation.17 | convolution fusion | flops 25769803776 | bytes 48234496 | tf_op jit(solution)/shard_map/cond/branch_1_fun/cd,cf->df/dot_general | solution.py:22
  723.6 26.3 %collective-permute-done.17.up1 = bf16[864,2048]{1,0:T(8,128)(2,1)S(1)} collective-permute-done((bf16[864,2048]{1,0:T(8,128)(2,1)}, bf16[864,2048]{1,0:T(8,128)(2,1)S(1)}, u32[]{:S(2)}, u32[]{:S(2)}) %collective-permute-start.17) | collective-permute-done | bytes 3538976 | tf_op jit(solution)/shard_map/cond/branch_1_fun/ppermute | solution.py:505
  758.3 33.8 %convolution_bitcast_fusion.4 = f32[1,4096,1024]{2,1,0:T(8,128)} fusion(bf16[3072,1024]{1,0:T(8,128)(2,1)} %bitcast.471, bf16[3072,4096]{1,0:T(8,128)(2,1)} %get-tuple-element.371), kind=kOutput, calls=%fused_computation.16 | convolution fusion | flops 25769803776 | bytes 48234496 | tf_op jit(solution)/shard_map/cond/branch_1_fun/cd,cf->df/dot_general | solution.py:22
  792.1 42.6 %collective-permute-done.19.up2 = bf16[864,2048]{1,0:T(8,128)(2,1)S(1)} collective-permute-done((bf16[864,2048]{1,0:T(8,128)(2,1)}, bf16[864,2048]{1,0:T(8,128)(2,1)S(1)}, u32[]{:S(2)}, u32[]{:S(2)}) %collective-permute-start.19) | collective-permute-done | bytes 3538976 | tf_op jit(solution)/shard_map/cond/branch_1_fun/ppermute | solution.py:505
  845.8 33.9 %convolution_bitcast_fusion.3 = f32[1,1024,4096]{2,1,0:T(8,128)} fusion(bf16[3072,1024]{1,0:T(8,128)(2,1)} %get-tuple-element.375, bf16[3072,4096]{1,0:T(8,128)(2,1)} %bitcast.455), kind=kOutput, calls=%fused_computation.15 | convolution fusion | flops 25769803776 | bytes 48234496 | tf_op jit(solution)/shard_map/cond/branch_1_fun/cf,cd->fd/dot_general | solution.py:22
  (341 shorter events, 198.2 us)
Async XLA Ops:
  7.2 228.8 %all-gather.7.cloned.1.call-start = ((), (), s32[]{:S(2)}) async-start(), calls=%async_computation.4 | async-start | bytes 56623104 | tf_op jit(solution)/shard_map/all_gather | solution.py:277
  8.0 452.1 %all-gather.9.cloned.1.call-start = ((), (), s32[]{:S(2)}) async-start(), calls=%async_computation.5 | async-start | bytes 56623104 | tf_op jit(solution)/shard_map/all_gather | solution.py:278
  33.7 116.8 %copy-start.62 = (f32[8,768]{1,0:T(8,128)}, f32[8,768]{1,0:T(8,128)S(1)}, u32[]{:S(2)}) copy-start(f32[8,768]{1,0:T(8,128)S(1)} %get-tuple-element.928) | copy-start | bytes 73732
  33.8 75.9 %copy-start.60 = (pred[8,8,768]{2,1,0:T(8,128)(4,1)}, pred[8,8,768]{2,1,0:T(8,128)(4,1)S(1)}, u32[]{:S(2)}) copy-start(pred[8,8,768]{2,1,0:T(8,128)(4,1)S(1)} %fusion.58) | copy-start | bytes 147460
  304.7 34.4 %copy-start.35 = (bf16[3072,1024]{1,0:T(8,128)(2,1)}, bf16[3072,1024]{1,0:T(8,128)(2,1)S(1)}, u32[]{:S(2)}) copy-start(bf16[3072,1024]{1,0:T(8,128)(2,1)S(1)} %convolution_convert_fusion.13) | copy-start | bytes 18874372
  365.8 21.7 %collective-permute-start.44 = (bf16[3072,2048]{1,0:T(8,128)(2,1)}, bf16[3072,2048]{1,0:T(8,128)(2,1)}, u32[]{:S(2)}, u32[]{:S(2)}) collective-permute-start(bf16[3072,2048]{1,0:T(8,128)(2,1)} %convolution_convert_fusion.12), channel_id=1, source_target_pairs={{0,1},{1,0},{2,3},{3,2},{4,5},{5,4},{6,7},{7,6},{8,9},{9,8},{10,11... | collective-permute-start | bytes 37748744 | tf_op jit(solution)/shard_map/ppermute | solution.py:275
  429.8 30.8 %copy-start.55 = (f32[2,6,8,128]{3,2,1,0:T(8,128)S(1)}, f32[2,6,8,128]{3,2,1,0:T(8,128)}, u32[]{:S(2)}) copy-start(f32[2,6,8,128]{3,2,1,0:T(8,128)} %stack.282) | copy-start | bytes 147460
  429.8 30.8 %copy-start.59 = (s32[8,8,768]{2,1,0:T(8,128)S(1)}, s32[8,8,768]{2,1,0:T(8,128)}, u32[]{:S(2)}) copy-start(s32[8,8,768]{2,1,0:T(8,128)} %copy-done.58) | copy-start | bytes 589828
  429.8 30.8 %copy-start.61 = (pred[8,8,768]{2,1,0:T(8,128)(4,1)S(1)}, pred[8,8,768]{2,1,0:T(8,128)(4,1)}, u32[]{:S(2)}) copy-start(pred[8,8,768]{2,1,0:T(8,128)(4,1)} %copy-done.60) | copy-start | bytes 147460
  429.8 30.8 %copy-start.66 = (s32[2,6,24]{2,1,0:T(8,128)S(1)}, s32[2,6,24]{2,1,0:T(8,128)}, u32[]{:S(2)}) copy-start(s32[2,6,24]{2,1,0:T(8,128)} %reshape.1193) | copy-start | bytes 3460
  429.8 30.8 %copy-start.69 = (f32[8,8,768]{2,1,0:T(8,128)S(1)}, f32[8,8,768]{2,1,0:T(8,128)}, u32[]{:S(2)}) copy-start(f32[8,8,768]{2,1,0:T(8,128)} %maximum_maximum_fusion) | copy-start | bytes 589828
  469.2 79.0 %collective-permute-start.12 = (bf16[864,2048]{1,0:T(8,128)(2,1)}, bf16[864,2048]{1,0:T(8,128)(2,1)S(1)}, u32[]{:S(2)}, u32[]{:S(2)}) collective-permute-start(bf16[864,2048]{1,0:T(8,128)(2,1)} %get-tuple-element.324), channel_id=1, source_target_pairs={{0,6},{1,7},{2,0},{3,1},{4,2},{5,3},{6,4},{7,5},{8,14},{9,15},{10,... | collective-permute-start | bytes 10616840 | tf_op jit(solution)/shard_map/cond/branch_1_fun/ppermute | solution.py:506
  470.1 79.8 %collective-permute-start.11 = (bf16[864,2048]{1,0:T(8,128)(2,1)}, bf16[864,2048]{1,0:T(8,128)(2,1)S(1)}, u32[]{:S(2)}, u32[]{:S(2)}) collective-permute-start(bf16[864,2048]{1,0:T(8,128)(2,1)} %get-tuple-element.323), channel_id=1, source_target_pairs={{0,2},{1,3},{2,4},{3,5},{4,6},{5,7},{6,0},{7,1},{8,10},{9,11},{10,... | collective-permute-start | bytes 10616840 | tf_op jit(solution)/shard_map/cond/branch_1_fun/ppermute | solution.py:505
  472.6 77.3 %copy-start.2 = (bf16[1136,2048]{1,0:T(8,128)(2,1)S(1)}, bf16[1136,2048]{1,0:T(8,128)(2,1)}, u32[]{:S(2)}) copy-start(bf16[1136,2048]{1,0:T(8,128)(2,1)} %get-tuple-element.338) | copy-start | bytes 13959172 | tf_op jit(solution)/shard_map/cond
  579.6 29.4 %collective-permute-start.15 = (bf16[8,384,2048]{2,1,0:T(8,128)(2,1)}, bf16[8,384,2048]{2,1,0:T(8,128)(2,1)}, u32[]{:S(2)}, u32[]{:S(2)}) collective-permute-start(bf16[8,384,2048]{2,1,0:T(8,128)(2,1)} %input_grad.10), channel_id=1, source_target_pairs={{0,1},{1,0},{2,3},{3,2},{4,5},{5,4},{6,7},{7,6},{8,9},{9,8},{10,11... | collective-permute-start | bytes 37748744 | tf_op jit(solution)/shard_map/cond/branch_1_fun/ppermute | solution.py:275
  579.7 80.4 %collective-permute-start.13 = (bf16[864,2048]{1,0:T(8,128)(2,1)}, bf16[864,2048]{1,0:T(8,128)(2,1)}, u32[]{:S(2)}, u32[]{:S(2)}) collective-permute-start(bf16[864,2048]{1,0:T(8,128)(2,1)} %slice_select_fusion.3), channel_id=1, source_target_pairs={{0,2},{1,3},{2,4},{3,5},{4,6},{5,7},{6,0},{7,1},{8,10},{9,11},{10,... | collective-permute-start | bytes 10616840 | tf_op jit(solution)/shard_map/cond/branch_1_fun/ppermute | solution.py:505
  579.8 80.3 %collective-permute-start.14 = (bf16[864,2048]{1,0:T(8,128)(2,1)}, bf16[864,2048]{1,0:T(8,128)(2,1)}, u32[]{:S(2)}, u32[]{:S(2)}) collective-permute-start(bf16[864,2048]{1,0:T(8,128)(2,1)} %slice_select_fusion.2), channel_id=1, source_target_pairs={{0,6},{1,7},{2,0},{3,1},{4,2},{5,3},{6,4},{7,5},{8,14},{9,15},{10,... | collective-permute-start | bytes 10616840 | tf_op jit(solution)/shard_map/cond/branch_1_fun/ppermute | solution.py:506
  669.1 46.3 %collective-permute-start.16 = (bf16[768,2048]{1,0:T(8,128)(2,1)S(1)}, bf16[768,2048]{1,0:T(8,128)(2,1)}, u32[]{:S(2)}, u32[]{:S(2)}) collective-permute-start(bf16[768,2048]{1,0:T(8,128)(2,1)S(1)} %arrive.20), channel_id=1, source_target_pairs={{0,1},{1,0},{2,3},{3,2},{4,5},{5,4},{6,7},{7,6},{8,9},{9,8},{10,11... | collective-permute-start | bytes 9437192 | tf_op jit(solution)/shard_map/cond/branch_1_fun/ppermute | solution.py:275
  669.2 80.6 %collective-permute-start.17 = (bf16[864,2048]{1,0:T(8,128)(2,1)}, bf16[864,2048]{1,0:T(8,128)(2,1)S(1)}, u32[]{:S(2)}, u32[]{:S(2)}) collective-permute-start(bf16[864,2048]{1,0:T(8,128)(2,1)} %get-tuple-element.352), channel_id=1, source_target_pairs={{0,2},{1,3},{2,4},{3,5},{4,6},{5,7},{6,0},{7,1},{8,10},{9,11},{10,... | collective-permute-start | bytes 10616840 | tf_op jit(solution)/shard_map/cond/branch_1_fun/ppermute | solution.py:505
  670.7 79.2 %collective-permute-start.18 = (bf16[864,2048]{1,0:T(8,128)(2,1)}, bf16[864,2048]{1,0:T(8,128)(2,1)S(1)}, u32[]{:S(2)}, u32[]{:S(2)}) collective-permute-start(bf16[864,2048]{1,0:T(8,128)(2,1)} %get-tuple-element.354), channel_id=1, source_target_pairs={{0,6},{1,7},{2,0},{3,1},{4,2},{5,3},{6,4},{7,5},{8,14},{9,15},{10,... | collective-permute-start | bytes 10616840 | tf_op jit(solution)/shard_map/cond/branch_1_fun/ppermute | solution.py:506
  715.4 34.5 %copy-start.52 = (bf16[864,2048]{1,0:T(8,128)(2,1)S(1)}, bf16[864,2048]{1,0:T(8,128)(2,1)}, u32[]{:S(2)}) copy-start(bf16[864,2048]{1,0:T(8,128)(2,1)} %get-tuple-element.355) | copy-start | bytes 10616836 | tf_op jit(solution)/shard_map/cond
  755.1 79.7 %collective-permute-start.19 = (bf16[864,2048]{1,0:T(8,128)(2,1)}, bf16[864,2048]{1,0:T(8,128)(2,1)S(1)}, u32[]{:S(2)}, u32[]{:S(2)}) collective-permute-start(bf16[864,2048]{1,0:T(8,128)(2,1)} %broadcast_select_fusion.3), channel_id=1, source_target_pairs={{0,2},{1,3},{2,4},{3,5},{4,6},{5,7},{6,0},{7,1},{8,10},{9,11},{10,... | collective-permute-start | bytes 10616840 | tf_op jit(solution)/shard_map/cond/branch_1_fun/ppermute | solution.py:505
  756.1 80.5 %collective-permute-start.20 = (bf16[864,2048]{1,0:T(8,128)(2,1)}, bf16[864,2048]{1,0:T(8,128)(2,1)S(1)}, u32[]{:S(2)}, u32[]{:S(2)}) collective-permute-start(bf16[864,2048]{1,0:T(8,128)(2,1)} %broadcast_select_fusion.2), channel_id=1, source_target_pairs={{0,6},{1,7},{2,0},{3,1},{4,2},{5,3},{6,4},{7,5},{8,14},{9,15},{10,... | collective-permute-start | bytes 10616840 | tf_op jit(solution)/shard_map/cond/branch_1_fun/ppermute | solution.py:506
  845.7 41.3 %collective-permute-start.21 = (bf16[768,2048]{1,0:T(8,128)(2,1)S(1)}, bf16[768,2048]{1,0:T(8,128)(2,1)S(1)}, u32[]{:S(2)}, u32[]{:S(2)}) collective-permute-start(bf16[768,2048]{1,0:T(8,128)(2,1)S(1)} %arrive.22), channel_id=1, source_target_pairs={{0,1},{1,0},{2,3},{3,2},{4,5},{5,4},{6,7},{7,6},{8,9},{9,8},{10,11... | collective-permute-start | bytes 9437192 | tf_op jit(solution)/shard_map/cond/branch_1_fun/ppermute | solution.py:275
  (31 other events, 358.2 us)
Sparse Core Ops, SparseCore 0:
  9.6 226.2 all-gather.6
  237.5 222.5 all-gather.8

commit v4 on v3

--- a/solution.py
+++ b/solution.py
@@ -263,7 +263,7 @@
         rows = group * cap
         half = dim // 2
         tiles = toks // TILE
-        tiers = [toks * n // 48 for n in (49, 54, 60, 71)]
+        tiers = [toks * n // 48 for n in (49, 57, 71)]
         stage = tiers[-1]
         place = 2 * stage
         me = lax.axis_index('expert')
@@ -408,6 +408,7 @@
         there = spots >= 0
         begin = jnp.min(jnp.where(there, spots, place), axis=2) // PIECE * PIECE
         count = jnp.maximum(jnp.max(spots, axis=2) - begin + PIECE, 0) // PIECE
+        count = jnp.where(state == len(tiers), 0, count)
         to = jnp.cumsum(count, axis=0) * PIECE - count * PIECE
         at = jnp.where(there, spots + (to - begin)[:, :, None], -1)
         first = jnp.max(at, axis=0)
@@ -624,7 +625,8 @@
             sums = [u + v for u, v in zip(first, second)]
             return sums[0].astype(BF), sums[1].astype(BF), *[v[None] for v in sums[2:]]
 
-        branches = [functools.partial(rest, tier) for tier in range(len(tiers))] + [general]
-        return lax.switch(state, branches)
+        branches = [functools.partial(rest, tier) for tier in range(len(tiers))]
+        done = lax.switch(jnp.minimum(state, len(tiers) - 1), branches)
+        return lax.cond(state == len(tiers), lambda done: general(), lambda done: done, done)
 
     return jax.shard_map(layer, mesh=mesh, in_specs=(tok_spec,) * 4 + (w_spec,) * 3, out_specs=(tok_spec,) * 5, check_vma=False)

time: 916 us -> 950 us (1.037)
  waiting for transfers between devices: 197 us -> 222 us
  loops' own time: 16.8 us -> 32.4 us
    another operation x1 -> x2, loops' own time: 16.8 us -> 32.4 us  [the longest x1 24.3 us: layer(): done = lax.switch(jnp.minimum(state, len(tiers) - 1), branches)]
    ppermute x4, waiting for transfers between devices: 99 us -> 112 us  [shift(): got_up = lax.ppermute(up_rows, 'expert', to_next)]
    unnamed x82 -> x84, local copies, waits for them, and re-layouts: 47.1 us -> 47.5 us
  transfers between devices with their start and end apart: 14 -> 14, of which waited for: 8 -> 8; matrix products, arithmetic and copies ran while one was open for 43% -> 40% of each run, Pallas kernels for 16% -> 16%
where the time goes in v4:
time: 950 us; the launch traced here: 941 us
  matrix products  244 us (26%)
  waiting for transfers between devices  222 us (23%)
  Pallas kernels  187 us (20%)
  local copies, waits for them, and re-layouts  84.4 us (9%)
  other arithmetic  78.6 us (8%)
  blocking collectives  54.5 us (6%)
  loops' own time  32.4 us (3%)
  between operations  25.2 us (3%)
  starting transfers between devices  12.5 us (1%)
    dot_general x11, matrix products, dot(): return jnp.einsum(form, a, b, preferred_element_type=F32)  244 us
    ppermute x4, waiting for transfers between devices, shift(): got_up = lax.ppermute(up_rows, 'expert', to_next)  112 us
    pallas_call x2, Pallas kernels, packed(): pl.pallas_call(functools.partial(pack_kernel, scaled), grid_spec=pltpu.Pr...  56 us
    pallas_call x1, Pallas kernels, inner_grads_of(): pl.pallas_call(inner_kernel, grid_spec=pltpu.PrefetchScalarGridSpec(num_s...  50.2 us
    pallas_call x2, Pallas kernels, input_grad(): pl.pallas_call(input_kernel, grid_spec=pltpu.PrefetchScalarGridSpec(num_s...  48.4 us
    unnamed x84, local copies, waits for them, and re-layouts  47.5 us
    all_gather x1, waiting for transfers between devices, layer(): all_x = lax.all_gather(tok_x, 'expert')  46.7 us
    pallas_call x4, Pallas kernels, arrived(): pl.pallas_call(functools.partial(arrive_kernel, scaled), grid_spec=pltpu....  32.6 us
  transfers between devices with their start and end apart: 14, of which 8 were waited for; matrix products, arithmetic and copies ran while one was open for 40% of the time, Pallas kernels for 16%

profile of v4, /device:TPU:112, one launch (start us, length us, event | category | flops | bytes accessed | tf_op | source)
XLA Modules:
  0.0 940.9 jit_solution(2561625717923012684)
XLA Ops:
  8.9 24.7 %all-gather.3 = f32[8,4,768]{2,1,0:T(4,128)S(1)} all-gather(f32[1,4,768]{2,1,0:T(4,128)S(1)} %maximum_bitcast_fusion), channel_id=3, replica_groups=mesh['data'=2,'expert'=8] {'expert'}, dimensions={0}, use_global_device_ids=true | all-gather | bytes 110592 | tf_op jit(solution)/shard_map/all_gather | solution.py:281
  44.6 29.8 %pmax.7 = s32[]{:T(128)} all-reduce(s32[]{:T(128)S(6)} %select_n.857), channel_id=1, replica_groups=mesh['data'=2,'expert'=8] {'data','expert'}, use_global_device_ids=true, to_apply=%region_10.11 | all-reduce | flops 1 | bytes 8 | tf_op jit(solution)/shard_map/pmax | solution.py:317
  96.9 12.1 %copy.100 = bf16[1,1024,4096]{1,2,0:T(8,128)(2,1)} copy(bf16[1,1024,4096]{2,1,0:T(8,128)(2,1)} %param.18) | data formatting | bytes 16777216 | tf_op args[6]
  189.2 46.7 %all-gather.7.cloned.1.call-done = bf16[6144,4096]{1,0:T(8,128)(2,1)} async-done(((bf16[768,4096]{1,0:T(8,128)(2,1)}), bf16[6144,4096]{1,0:T(8,128)(2,1)}) %all-gather.7.cloned.1.call-update) | async-done | bytes 50331664 | tf_op jit(solution)/shard_map/all_gather | solution.py:277
  236.0 36.2 %convolution_convert_fusion.10 = bf16[8,384,4096]{2,1,0:T(8,128)(2,1)} fusion(bf16[8,384,768]{2,1,0:T(8,128)(2,1)} %fusion.42, bf16[8,768,4096]{2,1,0:T(8,128)(2,1)} %bitcast.406), kind=kOutput, calls=%fused_computation.138 | convolution fusion | flops 19339935744 | bytes 80216064 | tf_op jit(solution)/shard_map/gcs,gsd->gcd/dot_general | solution.py:22
  272.1 32.6 %convolution_convert_fusion.13 = bf16[3072,1024]{1,0:T(8,128)(2,1)S(1)} fusion(bf16[3072,4096]{1,0:T(8,128)(2,1)} %bitcast.412, bf16[1,4096,1024]{2,1,0:T(8,128)(2,1)} %param.17), kind=kOutput, calls=%fused_computation.149 | convolution fusion | flops 25772949504 | bytes 39845888 | tf_op jit(solution)/shard_map/cd,df->cf/dot_general | solution.py:22
  304.7 34.4 %convolution_convert_fusion.14 = bf16[3072,1024]{1,0:T(8,128)(2,1)S(1)} fusion(bf16[3072,4096]{1,0:T(8,128)(2,1)} %bitcast.413, bf16[1,4096,1024]{2,1,0:T(8,128)(2,1)} %param.16), kind=kOutput, calls=%fused_computation.150 | convolution fusion | flops 25772949504 | bytes 39845888 | tf_op jit(solution)/shard_map/cd,df->cf/dot_general | solution.py:22
  345.9 16.8 %convolution_convert_fusion.12 = bf16[3072,2048]{1,0:T(8,128)(2,1)} fusion(bf16[3072,1024]{1,0:T(8,128)(2,1)S(1)} %fusion.41, bf16[1024,2048]{0,1:T(8,128)(2,1)S(1)} %copy-done.36), kind=kOutput, calls=%fused_computation.145 | convolution fusion | flops 12891193344 | bytes 23068672 | tf_op jit(solution)/shard_map/cf,fd->cd/dot_general | solution.py:22
  364.7 19.3 %convolution_convert_fusion.11 = bf16[3072,2048]{1,0:T(8,128)(2,1)} fusion(bf16[3072,1024]{1,0:T(8,128)(2,1)} %copy-done.29, bf16[1024,2048]{0,1:T(8,128)(2,1)} %get-tuple-element.496), kind=kOutput, calls=%fused_computation.144 | convolution fusion | flops 12891193344 | bytes 23068672 | tf_op jit(solution)/shard_map/cf,fd->cd/dot_general | solution.py:22
  384.4 33.0 %pack.7 = (bf16[1136,2048]{1,0:T(8,128)(2,1)S(1)}, bf16[1136,2048]{1,0:T(8,128)(2,1)}, bf16[1136,2048]{1,0:T(8,128)(2,1)S(1)}, bf16[1136,2048]{1,0:T(8,128)(2,1)}) custom-call(s32[6]{0:T(128)S(1)} %copy-done.80, s32[6,4]{1,0:T(8,128)S(1)} %copy-done.60, s32[6,12]{1,0:T(8,128)S(1)} %copy-done.63, bf16[8,384,2048]{2,1,0:T(8,128)(2,1)} %bitcast.363, ...), custom_call_target="tpu_custom_call" | custom-call | flops 4831838208 | bytes 75497472 | tf_op jit(solution)/shard_map/pack/pallas_call | solution.py:470
  427.6 32.5 %all-gather.9.cloned.1.call-done = bf16[6144,4096]{1,0:T(8,128)(2,1)} async-done(((bf16[768,4096]{1,0:T(8,128)(2,1)}), bf16[6144,4096]{1,0:T(8,128)(2,1)}) %all-gather.9.cloned.1.call-update) | async-done | bytes 50331664 | tf_op jit(solution)/shard_map/all_gather | solution.py:278
  461.6 463.7 %conditional.2 = (bf16[768,4096]{1,0:T(8,128)(2,1)}, bf16[768,4096]{1,0:T(8,128)(2,1)}, f32[1,4096,1024]{2,1,0:T(8,128)}, f32[1,4096,1024]{2,1,0:T(8,128)}, f32[1,1024,4096]{2,1,0:T(8,128)}) conditional(s32[]{:T(128)} %clamp.3, (s32[]{:T(128)}, s32[2,1]{0,1:T(1,128)S(1)}, s32[2,6,24]{2,1,0:T(8,128)S(1)}, ...), branch_computations={%region_54.55_spmd, %region_55.56_spmd, %region_56.57_spmd} | conditional | flops 198171295744 | bytes 986733120 | solution.py:629
  473.5 50.2 %inner.4 = (bf16[8,384,4096]{2,1,0:T(8,128)(2,1)}, bf16[8,384,1024]{2,1,0:T(8,128)(2,1)}, bf16[8,384,1024]{2,1,0:T(8,128)(2,1)}) custom-call(s32[8]{0:T(128)S(1)} %get-tuple-element.278.count_ref, s32[8]{0:T(128)S(1)} %get-tuple-element.279.from_ref, f32[8,8,768]{2,1,0:T(8,128)S(1)} %get-tuple-element.280.info, bf16[8,768,4096]{2,1,0:T(8,128)(2,1)} %get-tuple-element.281.dy, ...), custom_call_target="tpu_custom_call" | custom-call | flops 45097156608 | bytes 100663296 | tf_op jit(solution)/shard_map/cond/branch_1_fun/inner/pallas_call | solution.py:535
  523.7 29.6 %collective-permute-done.12.down1 = bf16[912,2048]{1,0:T(8,128)(2,1)S(1)} collective-permute-done((bf16[912,2048]{1,0:T(8,128)(2,1)}, bf16[912,2048]{1,0:T(8,128)(2,1)S(1)}, u32[]{:S(2)}, u32[]{:S(2)}) %collective-permute-start.12) | collective-permute-done | bytes 3735584 | tf_op jit(solution)/shard_map/cond/branch_1_fun/ppermute | solution.py:507
  561.2 23.7 %input_grad.8 = bf16[8,384,2048]{2,1,0:T(8,128)(2,1)} custom-call(s32[8]{0:T(128)S(1)} %get-tuple-element.278.count_ref, bf16[8,384,1024]{2,1,0:T(8,128)(2,1)} %get-tuple-element.322.da, bf16[8,384,1024]{2,1,0:T(8,128)(2,1)} %get-tuple-element.324.db, bf16[1024,2048]{1,0:T(8,128)(2,1)} %get-tuple-element.298.w1t, bf16[1024,2048]{1,0:T(8,128)(2,1)S(1)} %copy-done.34), custom_call_target="tpu_custom_call" | custom-call | flops 25769803776 | bytes 25165824 | tf_op jit(solution)/shard_map/cond/branch_1_fun/input_grad/pallas_call | solution.py:550
  589.6 24.6 %input_grad.9.tab0 = bf16[8,384,2048]{2,1,0:T(8,128)(2,1)} custom-call(s32[8]{0:T(128)S(1)} %get-tuple-element.278.count_ref, bf16[8,384,1024]{2,1,0:T(8,128)(2,1)} %get-tuple-element.322.da, bf16[8,384,1024]{2,1,0:T(8,128)(2,1)} %get-tuple-element.324.db, bf16[1024,2048]{1,0:T(8,128)(2,1)} %get-tuple-element.301.w1t, bf16[1024,2048]{1,0:T(8,128)(2,1)} %get-tuple-element.302.w3t), custom_call_target="tpu_custom_call" | custom-call | flops 25769803776 | bytes 25165824 | tf_op jit(solution)/shard_map/cond/branch_1_fun/input_grad/pallas_call | solution.py:550
  614.3 22.9 %pack.5 = (bf16[912,2048]{1,0:T(8,128)(2,1)}, bf16[912,2048]{1,0:T(8,128)(2,1)}, bf16[912,2048]{1,0:T(8,128)(2,1)}, bf16[912,2048]{1,0:T(8,128)(2,1)}) custom-call(s32[6]{0:T(128)S(1)} %get-tuple-element.295.dev_ref, s32[6,4]{1,0:T(8,128)S(1)} %get-tuple-element.296.seg_ref, s32[6,12]{1,0:T(8,128)S(1)} %get-tuple-element.297.low_ref, ...), custom_call_target="tpu_custom_call" | custom-call | flops 4831838208 | bytes 75497472 | tf_op jit(solution)/shard_map/cond/branch_1_fun/pack/pallas_call | solution.py:470
  637.2 32.5 %collective-permute-done.13.up2 = bf16[912,2048]{1,0:T(8,128)(2,1)} collective-permute-done((bf16[912,2048]{1,0:T(8,128)(2,1)}, bf16[912,2048]{1,0:T(8,128)(2,1)}, u32[]{:S(2)}, u32[]{:S(2)}) %collective-permute-start.13) | collective-permute-done | bytes 3735584 | tf_op jit(solution)/shard_map/cond/branch_1_fun/ppermute | solution.py:506
  669.7 9.1 arrive.16
  691.2 33.8 %convolution_bitcast_fusion.5 = f32[1,4096,1024]{2,1,0:T(8,128)} fusion(bf16[3072,1024]{1,0:T(8,128)(2,1)} %bitcast.437, bf16[3072,4096]{1,0:T(8,128)(2,1)} %get-tuple-element.323), kind=kOutput, calls=%fused_computation.17 | convolution fusion | flops 25769803776 | bytes 48234496 | tf_op jit(solution)/shard_map/cond/branch_1_fun/cd,cf->df/dot_general | solution.py:22
  732.9 30.7 %collective-permute-done.17.up1 = bf16[912,2048]{1,0:T(8,128)(2,1)S(1)} collective-permute-done((bf16[912,2048]{1,0:T(8,128)(2,1)}, bf16[912,2048]{1,0:T(8,128)(2,1)S(1)}, u32[]{:S(2)}, u32[]{:S(2)}) %collective-permute-start.17) | collective-permute-done | bytes 3735584 | tf_op jit(solution)/shard_map/cond/branch_1_fun/ppermute | solution.py:506
  772.4 33.8 %convolution_bitcast_fusion.4 = f32[1,4096,1024]{2,1,0:T(8,128)} fusion(bf16[3072,1024]{1,0:T(8,128)(2,1)} %bitcast.433, bf16[3072,4096]{1,0:T(8,128)(2,1)} %get-tuple-element.323), kind=kOutput, calls=%fused_computation.16 | convolution fusion | flops 25769803776 | bytes 48234496 | tf_op jit(solution)/shard_map/cond/branch_1_fun/cd,cf->df/dot_general | solution.py:22
  806.1 46.9 %collective-permute-done.19.up2 = bf16[912,2048]{1,0:T(8,128)(2,1)S(1)} collective-permute-done((bf16[912,2048]{1,0:T(8,128)(2,1)}, bf16[912,2048]{1,0:T(8,128)(2,1)S(1)}, u32[]{:S(2)}, u32[]{:S(2)}) %collective-permute-start.19) | collective-permute-done | bytes 3735584 | tf_op jit(solution)/shard_map/cond/branch_1_fun/ppermute | solution.py:506
  864.2 34.0 %convolution_bitcast_fusion.3 = f32[1,1024,4096]{2,1,0:T(8,128)} fusion(bf16[3072,1024]{1,0:T(8,128)(2,1)} %get-tuple-element.327, bf16[3072,4096]{1,0:T(8,128)(2,1)} %bitcast.418), kind=kOutput, calls=%fused_computation.15 | convolution fusion | flops 25769803776 | bytes 48234496 | tf_op jit(solution)/shard_map/cond/branch_1_fun/cf,cd->fd/dot_general | solution.py:22
  (336 shorter events, 201.6 us)
Async XLA Ops:
  7.2 228.8 %all-gather.7.cloned.1.call-start = ((), (), s32[]{:S(2)}) async-start(), calls=%async_computation.4 | async-start | bytes 56623104 | tf_op jit(solution)/shard_map/all_gather | solution.py:277
  8.0 452.1 %all-gather.9.cloned.1.call-start = ((), (), s32[]{:S(2)}) async-start(), calls=%async_computation.5 | async-start | bytes 56623104 | tf_op jit(solution)/shard_map/all_gather | solution.py:278
  33.7 115.8 %copy-start.51 = (f32[8,768]{1,0:T(8,128)}, f32[8,768]{1,0:T(8,128)S(1)}, u32[]{:S(2)}) copy-start(f32[8,768]{1,0:T(8,128)S(1)} %get-tuple-element.767) | copy-start | bytes 73732
  33.8 75.2 %copy-start.49 = (pred[8,8,768]{2,1,0:T(8,128)(4,1)}, pred[8,8,768]{2,1,0:T(8,128)(4,1)S(1)}, u32[]{:S(2)}) copy-start(pred[8,8,768]{2,1,0:T(8,128)(4,1)S(1)} %fusion.58) | copy-start | bytes 147460
  362.6 21.7 %collective-permute-start.33 = (bf16[3072,2048]{1,0:T(8,128)(2,1)}, bf16[3072,2048]{1,0:T(8,128)(2,1)}, u32[]{:S(2)}, u32[]{:S(2)}) collective-permute-start(bf16[3072,2048]{1,0:T(8,128)(2,1)} %convolution_convert_fusion.12), channel_id=1, source_target_pairs={{0,1},{1,0},{2,3},{3,2},{4,5},{5,4},{6,7},{7,6},{8,9},{9,8},{10,11... | collective-permute-start | bytes 37748744 | tf_op jit(solution)/shard_map/ppermute | solution.py:275
  423.1 37.6 %copy-start.46 = (f32[2,6,8,128]{3,2,1,0:T(8,128)S(1)}, f32[2,6,8,128]{3,2,1,0:T(8,128)}, u32[]{:S(2)}) copy-start(f32[2,6,8,128]{3,2,1,0:T(8,128)} %stack.282) | copy-start | bytes 147460
  423.1 37.6 %copy-start.55 = (f32[8,8,768]{2,1,0:T(8,128)S(1)}, f32[8,8,768]{2,1,0:T(8,128)}, u32[]{:S(2)}) copy-start(f32[8,8,768]{2,1,0:T(8,128)} %maximum_maximum_fusion) | copy-start | bytes 589828
  423.1 37.6 %copy-start.57 = (s32[2,6,24]{2,1,0:T(8,128)S(1)}, s32[2,6,24]{2,1,0:T(8,128)}, u32[]{:S(2)}) copy-start(s32[2,6,24]{2,1,0:T(8,128)} %reshape.1172) | copy-start | bytes 3460
  423.1 37.6 %copy-start.77 = (s32[2,1]{0,1:T(1,128)S(1)}, s32[2,1]{0,1:T(1,128)}, u32[]{:S(2)}) copy-start(s32[2,1]{0,1:T(1,128)} %fusion.140) | copy-start | bytes 28
  423.1 37.6 %copy-start.88 = (s32[8]{0:T(128)S(1)}, s32[8]{0:T(128)}, u32[]{:S(2)}) copy-start(s32[8]{0:T(128)} %get-tuple-element.500) | copy-start | bytes 100
  423.1 37.6 %copy-start.91 = (s32[8]{0:T(128)S(1)}, s32[8]{0:T(128)}, u32[]{:S(2)}) copy-start(s32[8]{0:T(128)} %compare_select_fusion.20) | copy-start | bytes 100
  470.1 83.2 %collective-permute-start.12 = (bf16[912,2048]{1,0:T(8,128)(2,1)}, bf16[912,2048]{1,0:T(8,128)(2,1)S(1)}, u32[]{:S(2)}, u32[]{:S(2)}) collective-permute-start(bf16[912,2048]{1,0:T(8,128)(2,1)} %get-tuple-element.276), channel_id=1, source_target_pairs={{0,6},{1,7},{2,0},{3,1},{4,2},{5,3},{6,4},{7,5},{8,14},{9,15},{10,... | collective-permute-start | bytes 11206664 | tf_op jit(solution)/shard_map/cond/branch_1_fun/ppermute | solution.py:507
  471.0 84.0 %collective-permute-start.11 = (bf16[912,2048]{1,0:T(8,128)(2,1)}, bf16[912,2048]{1,0:T(8,128)(2,1)S(1)}, u32[]{:S(2)}, u32[]{:S(2)}) collective-permute-start(bf16[912,2048]{1,0:T(8,128)(2,1)} %get-tuple-element.275), channel_id=1, source_target_pairs={{0,2},{1,3},{2,4},{3,5},{4,6},{5,7},{6,0},{7,1},{8,10},{9,11},{10,... | collective-permute-start | bytes 11206664 | tf_op jit(solution)/shard_map/cond/branch_1_fun/ppermute | solution.py:506
  473.5 81.6 %copy-start.9 = (bf16[1136,2048]{1,0:T(8,128)(2,1)S(1)}, bf16[1136,2048]{1,0:T(8,128)(2,1)}, u32[]{:S(2)}) copy-start(bf16[1136,2048]{1,0:T(8,128)(2,1)} %get-tuple-element.290) | copy-start | bytes 13959172 | tf_op jit(solution)/shard_map/cond
  584.9 29.3 %collective-permute-start.15 = (bf16[8,384,2048]{2,1,0:T(8,128)(2,1)}, bf16[8,384,2048]{2,1,0:T(8,128)(2,1)}, u32[]{:S(2)}, u32[]{:S(2)}) collective-permute-start(bf16[8,384,2048]{2,1,0:T(8,128)(2,1)} %input_grad.8), channel_id=1, source_target_pairs={{0,1},{1,0},{2,3},{3,2},{4,5},{5,4},{6,7},{7,6},{8,9},{9,8},{10,11... | collective-permute-start | bytes 37748744 | tf_op jit(solution)/shard_map/cond/branch_1_fun/ppermute | solution.py:275
  585.0 84.7 %collective-permute-start.13 = (bf16[912,2048]{1,0:T(8,128)(2,1)}, bf16[912,2048]{1,0:T(8,128)(2,1)}, u32[]{:S(2)}, u32[]{:S(2)}) collective-permute-start(bf16[912,2048]{1,0:T(8,128)(2,1)} %slice_select_fusion.3), channel_id=1, source_target_pairs={{0,2},{1,3},{2,4},{3,5},{4,6},{5,7},{6,0},{7,1},{8,10},{9,11},{10,... | collective-permute-start | bytes 11206664 | tf_op jit(solution)/shard_map/cond/branch_1_fun/ppermute | solution.py:506
  585.1 84.6 %collective-permute-start.14 = (bf16[912,2048]{1,0:T(8,128)(2,1)}, bf16[912,2048]{1,0:T(8,128)(2,1)}, u32[]{:S(2)}, u32[]{:S(2)}) collective-permute-start(bf16[912,2048]{1,0:T(8,128)(2,1)} %slice_select_fusion.2), channel_id=1, source_target_pairs={{0,6},{1,7},{2,0},{3,1},{4,2},{5,3},{6,4},{7,5},{8,14},{9,15},{10,... | collective-permute-start | bytes 11206664 | tf_op jit(solution)/shard_map/cond/branch_1_fun/ppermute | solution.py:507
  678.7 46.3 %collective-permute-start.16 = (bf16[768,2048]{1,0:T(8,128)(2,1)S(1)}, bf16[768,2048]{1,0:T(8,128)(2,1)}, u32[]{:S(2)}, u32[]{:S(2)}) collective-permute-start(bf16[768,2048]{1,0:T(8,128)(2,1)S(1)} %arrive.16), channel_id=1, source_target_pairs={{0,1},{1,0},{2,3},{3,2},{4,5},{5,4},{6,7},{7,6},{8,9},{9,8},{10,11... | collective-permute-start | bytes 9437192 | tf_op jit(solution)/shard_map/cond/branch_1_fun/ppermute | solution.py:275
  678.8 84.8 %collective-permute-start.17 = (bf16[912,2048]{1,0:T(8,128)(2,1)}, bf16[912,2048]{1,0:T(8,128)(2,1)S(1)}, u32[]{:S(2)}, u32[]{:S(2)}) collective-permute-start(bf16[912,2048]{1,0:T(8,128)(2,1)} %get-tuple-element.304), channel_id=1, source_target_pairs={{0,2},{1,3},{2,4},{3,5},{4,6},{5,7},{6,0},{7,1},{8,10},{9,11},{10,... | collective-permute-start | bytes 11206664 | tf_op jit(solution)/shard_map/cond/branch_1_fun/ppermute | solution.py:506
  680.4 83.3 %collective-permute-start.18 = (bf16[912,2048]{1,0:T(8,128)(2,1)}, bf16[912,2048]{1,0:T(8,128)(2,1)S(1)}, u32[]{:S(2)}, u32[]{:S(2)}) collective-permute-start(bf16[912,2048]{1,0:T(8,128)(2,1)} %get-tuple-element.306), channel_id=1, source_target_pairs={{0,6},{1,7},{2,0},{3,1},{4,2},{5,3},{6,4},{7,5},{8,14},{9,15},{10,... | collective-permute-start | bytes 11206664 | tf_op jit(solution)/shard_map/cond/branch_1_fun/ppermute | solution.py:507
  725.0 38.7 %copy-start.38 = (bf16[912,2048]{1,0:T(8,128)(2,1)S(1)}, bf16[912,2048]{1,0:T(8,128)(2,1)}, u32[]{:S(2)}) copy-start(bf16[912,2048]{1,0:T(8,128)(2,1)} %get-tuple-element.307) | copy-start | bytes 11206660 | tf_op jit(solution)/shard_map/cond
  769.1 83.9 %collective-permute-start.19 = (bf16[912,2048]{1,0:T(8,128)(2,1)}, bf16[912,2048]{1,0:T(8,128)(2,1)S(1)}, u32[]{:S(2)}, u32[]{:S(2)}) collective-permute-start(bf16[912,2048]{1,0:T(8,128)(2,1)} %broadcast_select_fusion.3), channel_id=1, source_target_pairs={{0,2},{1,3},{2,4},{3,5},{4,6},{5,7},{6,0},{7,1},{8,10},{9,11},{10,... | collective-permute-start | bytes 11206664 | tf_op jit(solution)/shard_map/cond/branch_1_fun/ppermute | solution.py:506
  770.1 82.9 %collective-permute-start.20 = (bf16[912,2048]{1,0:T(8,128)(2,1)}, bf16[912,2048]{1,0:T(8,128)(2,1)S(1)}, u32[]{:S(2)}, u32[]{:S(2)}) collective-permute-start(bf16[912,2048]{1,0:T(8,128)(2,1)} %broadcast_select_fusion.2), channel_id=1, source_target_pairs={{0,6},{1,7},{2,0},{3,1},{4,2},{5,3},{6,4},{7,5},{8,14},{9,15},{10,... | collective-permute-start | bytes 11206664 | tf_op jit(solution)/shard_map/cond/branch_1_fun/ppermute | solution.py:507
  864.1 41.3 %collective-permute-start.21 = (bf16[768,2048]{1,0:T(8,128)(2,1)S(1)}, bf16[768,2048]{1,0:T(8,128)(2,1)S(1)}, u32[]{:S(2)}, u32[]{:S(2)}) collective-permute-start(bf16[768,2048]{1,0:T(8,128)(2,1)S(1)} %arrive.18), channel_id=1, source_target_pairs={{0,1},{1,0},{2,3},{3,2},{4,5},{5,4},{6,7},{7,6},{8,9},{9,8},{10,11... | collective-permute-start | bytes 9437192 | tf_op jit(solution)/shard_map/cond/branch_1_fun/ppermute | solution.py:275
  (29 other events, 293.1 us)
Sparse Core Ops, SparseCore 0:
  9.6 226.2 all-gather.6
  237.5 222.5 all-gather.8

commit v5 on v3

--- a/solution.py
+++ b/solution.py
@@ -605,7 +605,13 @@
                 onehot_out = (goal[:, :, None] == iota((1, 1, rows), 2)).astype(BF)
 
                 def swap(r):
-                    return lax.all_to_all(r.reshape(group, cap, dim), 'expert', 0, 0).reshape(rows, dim)
+                    blocks = r.reshape(group, cap, dim)
+                    got = blocks
+                    for by in range(1, group):
+                        block = lax.dynamic_index_in_dim(blocks, (me + by) % group, 0)
+                        block = lax.ppermute(block, 'expert', [(i, (i + by) % group) for i in range(group)])
+                        got = lax.dynamic_update_slice_in_dim(got, block, (me + group - by) % group, 0)
+                    return got.reshape(rows, dim)
 
                 x = take(onehot, all_x)
                 pre_a, pre_b, hid = up_front(x)

time: 916 us -> 915 us (level)
    unnamed x82 -> x84, local copies, waits for them, and re-layouts: 47.1 us -> 47.1 us
where the time goes in v5:
time: 915 us; the launch traced here: 906 us
  matrix products  247 us (27%)
  waiting for transfers between devices  197 us (22%)
  Pallas kernels  187 us (20%)
  local copies, waits for them, and re-layouts  87.8 us (10%)
  other arithmetic  78 us (9%)
  blocking collectives  54.5 us (6%)
  between operations  25.2 us (3%)
  loops' own time  16.8 us (2%)
  starting transfers between devices  12.5 us (1%)
    dot_general x11, matrix products, dot(): return jnp.einsum(form, a, b, preferred_element_type=F32)  247 us
    ppermute x4, waiting for transfers between devices, shift(): got_up = lax.ppermute(up_rows, 'expert', to_next)  99 us
    pallas_call x2, Pallas kernels, packed(): pl.pallas_call(functools.partial(pack_kernel, scaled), grid_spec=pltpu.Pr...  55.5 us
    pallas_call x1, Pallas kernels, inner_grads_of(): pl.pallas_call(inner_kernel, grid_spec=pltpu.PrefetchScalarGridSpec(num_s...  50.5 us
    pallas_call x2, Pallas kernels, input_grad(): pl.pallas_call(input_kernel, grid_spec=pltpu.PrefetchScalarGridSpec(num_s...  48.4 us
    unnamed x84, local copies, waits for them, and re-layouts  47.1 us
    all_gather x1, waiting for transfers between devices, layer(): all_x = lax.all_gather(tok_x, 'expert')  45.3 us
    pallas_call x4, Pallas kernels, arrived(): pl.pallas_call(functools.partial(arrive_kernel, scaled), grid_spec=pltpu....  32.4 us
  transfers between devices with their start and end apart: 14, of which 8 were waited for; matrix products, arithmetic and copies ran while one was open for 43% of the time, Pallas kernels for 16%

profile of v5, /device:TPU:112, one launch (start us, length us, event | category | flops | bytes accessed | tf_op | source)
XLA Modules:
  0.0 905.8 jit_solution(16276466050763111583)
XLA Ops:
  8.9 24.7 %all-gather.3 = f32[8,4,768]{2,1,0:T(4,128)S(1)} all-gather(f32[1,4,768]{2,1,0:T(4,128)S(1)} %maximum_bitcast_fusion), channel_id=3, replica_groups=mesh['data'=2,'expert'=8] {'expert'}, dimensions={0}, use_global_device_ids=true | all-gather | bytes 110592 | tf_op jit(solution)/shard_map/all_gather | solution.py:281
  45.2 29.8 %pmax.7 = s32[]{:T(128)} all-reduce(s32[]{:T(128)S(6)} %select_n.1053), channel_id=1, replica_groups=mesh['data'=2,'expert'=8] {'data','expert'}, use_global_device_ids=true, to_apply=%region_10.11 | all-reduce | flops 1 | bytes 8 | tf_op jit(solution)/shard_map/pmax | solution.py:317
  97.7 12.0 %copy.116 = bf16[1,1024,4096]{1,2,0:T(8,128)(2,1)} copy(bf16[1,1024,4096]{2,1,0:T(8,128)(2,1)} %param.18) | data formatting | bytes 16777216 | tf_op args[6]
  190.6 45.3 %all-gather.7.cloned.1.call-done = bf16[6144,4096]{1,0:T(8,128)(2,1)} async-done(((bf16[768,4096]{1,0:T(8,128)(2,1)}), bf16[6144,4096]{1,0:T(8,128)(2,1)}) %all-gather.7.cloned.1.call-update) | async-done | bytes 50331664 | tf_op jit(solution)/shard_map/all_gather | solution.py:277
  236.0 36.3 %convolution_convert_fusion.10 = bf16[8,384,4096]{2,1,0:T(8,128)(2,1)} fusion(bf16[8,384,768]{2,1,0:T(8,128)(2,1)} %fusion.42, bf16[8,768,4096]{2,1,0:T(8,128)(2,1)} %bitcast.450), kind=kOutput, calls=%fused_computation.209 | convolution fusion | flops 19339935744 | bytes 80216064 | tf_op jit(solution)/shard_map/gcs,gsd->gcd/dot_general | solution.py:22
  272.2 32.5 %convolution_convert_fusion.13 = bf16[3072,1024]{1,0:T(8,128)(2,1)S(1)} fusion(bf16[3072,4096]{1,0:T(8,128)(2,1)} %bitcast.457, bf16[1,4096,1024]{2,1,0:T(8,128)(2,1)} %param.17), kind=kOutput, calls=%fused_computation.220 | convolution fusion | flops 25772949504 | bytes 39845888 | tf_op jit(solution)/shard_map/cd,df->cf/dot_general | solution.py:22
  304.8 34.4 %convolution_convert_fusion.14 = bf16[3072,1024]{1,0:T(8,128)(2,1)S(1)} fusion(bf16[3072,4096]{1,0:T(8,128)(2,1)} %bitcast.458, bf16[1,4096,1024]{2,1,0:T(8,128)(2,1)} %param.16), kind=kOutput, calls=%fused_computation.221 | convolution fusion | flops 25772949504 | bytes 39845888 | tf_op jit(solution)/shard_map/cd,df->cf/dot_general | solution.py:22
  345.9 20.0 %convolution_convert_fusion.12 = bf16[3072,2048]{1,0:T(8,128)(2,1)} fusion(bf16[3072,1024]{1,0:T(8,128)(2,1)S(1)} %fusion.41, bf16[1024,2048]{0,1:T(8,128)(2,1)} %get-tuple-element.602), kind=kOutput, calls=%fused_computation.216 | convolution fusion | flops 12891193344 | bytes 23068672 | tf_op jit(solution)/shard_map/cf,fd->cd/dot_general | solution.py:22
  367.2 19.3 %convolution_convert_fusion.11 = bf16[3072,2048]{1,0:T(8,128)(2,1)} fusion(bf16[3072,1024]{1,0:T(8,128)(2,1)} %copy-done.35, bf16[1024,2048]{0,1:T(8,128)(2,1)} %get-tuple-element.604), kind=kOutput, calls=%fused_computation.215 | convolution fusion | flops 12891193344 | bytes 23068672 | tf_op jit(solution)/shard_map/cf,fd->cd/dot_general | solution.py:22
  387.7 32.5 %pack.9 = (bf16[1136,2048]{1,0:T(8,128)(2,1)S(1)}, bf16[1136,2048]{1,0:T(8,128)(2,1)}, bf16[1136,2048]{1,0:T(8,128)(2,1)S(1)}, bf16[1136,2048]{1,0:T(8,128)(2,1)}) custom-call(s32[6]{0:T(128)S(1)} %copy-done.93, s32[6,4]{1,0:T(8,128)S(1)} %copy-done.72, s32[6,12]{1,0:T(8,128)S(1)} %copy-done.75, bf16[8,384,2048]{2,1,0:T(8,128)(2,1)} %bitcast.394, ...), custom_call_target="tpu_custom_call" | custom-call | flops 4831838208 | bytes 75497472 | tf_op jit(solution)/shard_map/pack/pallas_call | solution.py:469
  435.0 25.1 %all-gather.9.cloned.1.call-done = bf16[6144,4096]{1,0:T(8,128)(2,1)} async-done(((bf16[768,4096]{1,0:T(8,128)(2,1)}), bf16[6144,4096]{1,0:T(8,128)(2,1)}) %all-gather.9.cloned.1.call-update) | async-done | bytes 50331664 | tf_op jit(solution)/shard_map/all_gather | solution.py:278
  460.2 438.5 %conditional.1 = (bf16[768,4096]{1,0:T(8,128)(2,1)}, bf16[768,4096]{1,0:T(8,128)(2,1)}, f32[1,4096,1024]{2,1,0:T(8,128)}, f32[1,4096,1024]{2,1,0:T(8,128)}, f32[1,1024,4096]{2,1,0:T(8,128)}) conditional(s32[]{:T(128)} %clamp.3, (s32[]{:T(128)}, s32[2,1]{0,1:T(1,128)S(1)}, s32[2,6,24]{2,1,0:T(8,128)S(1)}, ...), branch_computations={%region_54.55_spmd, %region_55.56_spmd, %region_56.57_spmd, %regio... | conditional | flops 657602379776 | bytes 2616431360 | solution.py:634
  472.0 50.5 %inner.5 = (bf16[8,384,4096]{2,1,0:T(8,128)(2,1)}, bf16[8,384,1024]{2,1,0:T(8,128)(2,1)}, bf16[8,384,1024]{2,1,0:T(8,128)(2,1)}) custom-call(s32[8]{0:T(128)} %copy-done.102, s32[8]{0:T(128)} %copy-done.108, f32[8,8,768]{2,1,0:T(8,128)S(1)} %get-tuple-element.328.info, bf16[8,768,4096]{2,1,0:T(8,128)(2,1)} %get-tuple-element.329.dy, ...), custom_call_target="tpu_custom_call" | custom-call | flops 45097156608 | bytes 100663296 | tf_op jit(solution)/shard_map/cond/branch_1_fun/inner/pallas_call | solution.py:534
  522.6 25.1 %collective-permute-done.12.down1 = bf16[864,2048]{1,0:T(8,128)(2,1)S(1)} collective-permute-done((bf16[864,2048]{1,0:T(8,128)(2,1)}, bf16[864,2048]{1,0:T(8,128)(2,1)S(1)}, u32[]{:S(2)}, u32[]{:S(2)}) %collective-permute-start.12) | collective-permute-done | bytes 3538976 | tf_op jit(solution)/shard_map/cond/branch_1_fun/ppermute | solution.py:506
  555.3 23.7 %input_grad.10 = bf16[8,384,2048]{2,1,0:T(8,128)(2,1)} custom-call(s32[8]{0:T(128)S(1)} %copy-done.103, bf16[8,384,1024]{2,1,0:T(8,128)(2,1)} %get-tuple-element.370.da, bf16[8,384,1024]{2,1,0:T(8,128)(2,1)} %get-tuple-element.372.db, bf16[1024,2048]{1,0:T(8,128)(2,1)} %get-tuple-element.346.w1t, bf16[1024,2048]{1,0:T(8,128)(2,1)S(1)} %copy-done.42), custom_call_target="tpu_custom_call" | custom-call | flops 25769803776 | bytes 25165824 | tf_op jit(solution)/shard_map/cond/branch_1_fun/input_grad/pallas_call | solution.py:549
  583.8 24.6 %input_grad.11.tab0 = bf16[8,384,2048]{2,1,0:T(8,128)(2,1)} custom-call(s32[8]{0:T(128)S(1)} %copy-done.103, bf16[8,384,1024]{2,1,0:T(8,128)(2,1)} %get-tuple-element.370.da, bf16[8,384,1024]{2,1,0:T(8,128)(2,1)} %get-tuple-element.372.db, bf16[1024,2048]{1,0:T(8,128)(2,1)} %get-tuple-element.349.w1t, bf16[1024,2048]{1,0:T(8,128)(2,1)} %get-tuple-element.350.w3t), custom_call_target="tpu_custom_call" | custom-call | flops 25769803776 | bytes 25165824 | tf_op jit(solution)/shard_map/cond/branch_1_fun/input_grad/pallas_call | solution.py:549
  608.4 22.9 %pack.6 = (bf16[864,2048]{1,0:T(8,128)(2,1)}, bf16[864,2048]{1,0:T(8,128)(2,1)}, bf16[864,2048]{1,0:T(8,128)(2,1)}, bf16[864,2048]{1,0:T(8,128)(2,1)}) custom-call(s32[6]{0:T(128)S(1)} %get-tuple-element.343.dev_ref, s32[6,4]{1,0:T(8,128)S(1)} %get-tuple-element.344.seg_ref, s32[6,12]{1,0:T(8,128)S(1)} %get-tuple-element.345.low_ref, ...), custom_call_target="tpu_custom_call" | custom-call | flops 4831838208 | bytes 75497472 | tf_op jit(solution)/shard_map/cond/branch_1_fun/pack/pallas_call | solution.py:469
  631.3 28.3 %collective-permute-done.13.up2 = bf16[864,2048]{1,0:T(8,128)(2,1)} collective-permute-done((bf16[864,2048]{1,0:T(8,128)(2,1)}, bf16[864,2048]{1,0:T(8,128)(2,1)}, u32[]{:S(2)}, u32[]{:S(2)}) %collective-permute-start.13) | collective-permute-done | bytes 3538976 | tf_op jit(solution)/shard_map/cond/branch_1_fun/ppermute | solution.py:505
  659.6 9.0 arrive.20
  681.1 33.8 %convolution_bitcast_fusion.5 = f32[1,4096,1024]{2,1,0:T(8,128)} fusion(bf16[3072,1024]{1,0:T(8,128)(2,1)} %bitcast.485, bf16[3072,4096]{1,0:T(8,128)(2,1)} %get-tuple-element.371), kind=kOutput, calls=%fused_computation.17 | convolution fusion | flops 25769803776 | bytes 48234496 | tf_op jit(solution)/shard_map/cond/branch_1_fun/cd,cf->df/dot_general | solution.py:22
  723.0 26.4 %collective-permute-done.17.up1 = bf16[864,2048]{1,0:T(8,128)(2,1)S(1)} collective-permute-done((bf16[864,2048]{1,0:T(8,128)(2,1)}, bf16[864,2048]{1,0:T(8,128)(2,1)S(1)}, u32[]{:S(2)}, u32[]{:S(2)}) %collective-permute-start.17) | collective-permute-done | bytes 3538976 | tf_op jit(solution)/shard_map/cond/branch_1_fun/ppermute | solution.py:505
  757.8 33.8 %convolution_bitcast_fusion.4 = f32[1,4096,1024]{2,1,0:T(8,128)} fusion(bf16[3072,1024]{1,0:T(8,128)(2,1)} %bitcast.480, bf16[3072,4096]{1,0:T(8,128)(2,1)} %get-tuple-element.371), kind=kOutput, calls=%fused_computation.16 | convolution fusion | flops 25769803776 | bytes 48234496 | tf_op jit(solution)/shard_map/cond/branch_1_fun/cd,cf->df/dot_general | solution.py:22
  791.6 42.6 %collective-permute-done.19.up2 = bf16[864,2048]{1,0:T(8,128)(2,1)S(1)} collective-permute-done((bf16[864,2048]{1,0:T(8,128)(2,1)}, bf16[864,2048]{1,0:T(8,128)(2,1)S(1)}, u32[]{:S(2)}, u32[]{:S(2)}) %collective-permute-start.19) | collective-permute-done | bytes 3538976 | tf_op jit(solution)/shard_map/cond/branch_1_fun/ppermute | solution.py:505
  845.1 34.0 %convolution_bitcast_fusion.3 = f32[1,1024,4096]{2,1,0:T(8,128)} fusion(bf16[3072,1024]{1,0:T(8,128)(2,1)} %get-tuple-element.375, bf16[3072,4096]{1,0:T(8,128)(2,1)} %bitcast.476), kind=kOutput, calls=%fused_computation.15 | convolution fusion | flops 25769803776 | bytes 48234496 | tf_op jit(solution)/shard_map/cond/branch_1_fun/cf,cd->fd/dot_general | solution.py:22
  (343 shorter events, 197.1 us)
Async XLA Ops:
  7.2 228.8 %all-gather.7.cloned.1.call-start = ((), (), s32[]{:S(2)}) async-start(), calls=%async_computation | async-start | bytes 56623104 | tf_op jit(solution)/shard_map/all_gather | solution.py:277
  8.0 452.1 %all-gather.9.cloned.1.call-start = ((), (), s32[]{:S(2)}) async-start(), calls=%async_computation.1 | async-start | bytes 56623104 | tf_op jit(solution)/shard_map/all_gather | solution.py:278
  33.7 116.9 %copy-start.63 = (f32[8,768]{1,0:T(8,128)}, f32[8,768]{1,0:T(8,128)S(1)}, u32[]{:S(2)}) copy-start(f32[8,768]{1,0:T(8,128)S(1)} %get-tuple-element.928) | copy-start | bytes 73732
  33.8 75.9 %copy-start.61 = (pred[8,8,768]{2,1,0:T(8,128)(4,1)}, pred[8,8,768]{2,1,0:T(8,128)(4,1)S(1)}, u32[]{:S(2)}) copy-start(pred[8,8,768]{2,1,0:T(8,128)(4,1)S(1)} %fusion.58) | copy-start | bytes 147460
  304.8 34.4 %copy-start.33 = (bf16[3072,1024]{1,0:T(8,128)(2,1)}, bf16[3072,1024]{1,0:T(8,128)(2,1)S(1)}, u32[]{:S(2)}) copy-start(bf16[3072,1024]{1,0:T(8,128)(2,1)S(1)} %convolution_convert_fusion.13) | copy-start | bytes 18874372
  365.9 21.7 %collective-permute-start.72 = (bf16[3072,2048]{1,0:T(8,128)(2,1)}, bf16[3072,2048]{1,0:T(8,128)(2,1)}, u32[]{:S(2)}, u32[]{:S(2)}) collective-permute-start(bf16[3072,2048]{1,0:T(8,128)(2,1)} %convolution_convert_fusion.12), channel_id=1, source_target_pairs={{0,1},{1,0},{2,3},{3,2},{4,5},{5,4},{6,7},{7,6},{8,9},{9,8},{10,11... | collective-permute-start | bytes 37748744 | tf_op jit(solution)/shard_map/ppermute | solution.py:275
  429.9 30.2 %copy-start.60 = (s32[8,8,768]{2,1,0:T(8,128)S(1)}, s32[8,8,768]{2,1,0:T(8,128)}, u32[]{:S(2)}) copy-start(s32[8,8,768]{2,1,0:T(8,128)} %copy-done.59) | copy-start | bytes 589828
  429.9 30.2 %copy-start.62 = (pred[8,8,768]{2,1,0:T(8,128)(4,1)S(1)}, pred[8,8,768]{2,1,0:T(8,128)(4,1)}, u32[]{:S(2)}) copy-start(pred[8,8,768]{2,1,0:T(8,128)(4,1)} %copy-done.61) | copy-start | bytes 147460
  429.9 30.2 %copy-start.67 = (s32[2,6,24]{2,1,0:T(8,128)S(1)}, s32[2,6,24]{2,1,0:T(8,128)}, u32[]{:S(2)}) copy-start(s32[2,6,24]{2,1,0:T(8,128)} %reshape.1193) | copy-start | bytes 3460
  429.9 30.2 %copy-start.70 = (f32[8,8,768]{2,1,0:T(8,128)S(1)}, f32[8,8,768]{2,1,0:T(8,128)}, u32[]{:S(2)}) copy-start(f32[8,8,768]{2,1,0:T(8,128)} %maximum_maximum_fusion) | copy-start | bytes 589828
  429.9 30.2 %copy-start.84 = (s32[768,2]{0,1:T(2,128)S(1)}, s32[768,2]{0,1:T(2,128)}, u32[]{:S(2)}) copy-start(s32[768,2]{0,1:T(2,128)} %param.13) | copy-start | bytes 18436
  468.7 79.0 %collective-permute-start.12 = (bf16[864,2048]{1,0:T(8,128)(2,1)}, bf16[864,2048]{1,0:T(8,128)(2,1)S(1)}, u32[]{:S(2)}, u32[]{:S(2)}) collective-permute-start(bf16[864,2048]{1,0:T(8,128)(2,1)} %get-tuple-element.324), channel_id=1, source_target_pairs={{0,6},{1,7},{2,0},{3,1},{4,2},{5,3},{6,4},{7,5},{8,14},{9,15},{10,... | collective-permute-start | bytes 10616840 | tf_op jit(solution)/shard_map/cond/branch_1_fun/ppermute | solution.py:506
  469.6 79.8 %collective-permute-start.11 = (bf16[864,2048]{1,0:T(8,128)(2,1)}, bf16[864,2048]{1,0:T(8,128)(2,1)S(1)}, u32[]{:S(2)}, u32[]{:S(2)}) collective-permute-start(bf16[864,2048]{1,0:T(8,128)(2,1)} %get-tuple-element.323), channel_id=1, source_target_pairs={{0,2},{1,3},{2,4},{3,5},{4,6},{5,7},{6,0},{7,1},{8,10},{9,11},{10,... | collective-permute-start | bytes 10616840 | tf_op jit(solution)/shard_map/cond/branch_1_fun/ppermute | solution.py:505
  472.0 77.4 %copy-start.2 = (bf16[1136,2048]{1,0:T(8,128)(2,1)S(1)}, bf16[1136,2048]{1,0:T(8,128)(2,1)}, u32[]{:S(2)}) copy-start(bf16[1136,2048]{1,0:T(8,128)(2,1)} %get-tuple-element.338) | copy-start | bytes 13959172 | tf_op jit(solution)/shard_map/cond
  579.1 29.3 %collective-permute-start.15 = (bf16[8,384,2048]{2,1,0:T(8,128)(2,1)}, bf16[8,384,2048]{2,1,0:T(8,128)(2,1)}, u32[]{:S(2)}, u32[]{:S(2)}) collective-permute-start(bf16[8,384,2048]{2,1,0:T(8,128)(2,1)} %input_grad.10), channel_id=1, source_target_pairs={{0,1},{1,0},{2,3},{3,2},{4,5},{5,4},{6,7},{7,6},{8,9},{9,8},{10,11... | collective-permute-start | bytes 37748744 | tf_op jit(solution)/shard_map/cond/branch_1_fun/ppermute | solution.py:275
  579.2 80.4 %collective-permute-start.13 = (bf16[864,2048]{1,0:T(8,128)(2,1)}, bf16[864,2048]{1,0:T(8,128)(2,1)}, u32[]{:S(2)}, u32[]{:S(2)}) collective-permute-start(bf16[864,2048]{1,0:T(8,128)(2,1)} %slice_select_fusion.3), channel_id=1, source_target_pairs={{0,2},{1,3},{2,4},{3,5},{4,6},{5,7},{6,0},{7,1},{8,10},{9,11},{10,... | collective-permute-start | bytes 10616840 | tf_op jit(solution)/shard_map/cond/branch_1_fun/ppermute | solution.py:505
  579.3 80.3 %collective-permute-start.14 = (bf16[864,2048]{1,0:T(8,128)(2,1)}, bf16[864,2048]{1,0:T(8,128)(2,1)}, u32[]{:S(2)}, u32[]{:S(2)}) collective-permute-start(bf16[864,2048]{1,0:T(8,128)(2,1)} %slice_select_fusion.2), channel_id=1, source_target_pairs={{0,6},{1,7},{2,0},{3,1},{4,2},{5,3},{6,4},{7,5},{8,14},{9,15},{10,... | collective-permute-start | bytes 10616840 | tf_op jit(solution)/shard_map/cond/branch_1_fun/ppermute | solution.py:506
  668.6 46.2 %collective-permute-start.16 = (bf16[768,2048]{1,0:T(8,128)(2,1)S(1)}, bf16[768,2048]{1,0:T(8,128)(2,1)}, u32[]{:S(2)}, u32[]{:S(2)}) collective-permute-start(bf16[768,2048]{1,0:T(8,128)(2,1)S(1)} %arrive.20), channel_id=1, source_target_pairs={{0,1},{1,0},{2,3},{3,2},{4,5},{5,4},{6,7},{7,6},{8,9},{9,8},{10,11... | collective-permute-start | bytes 9437192 | tf_op jit(solution)/shard_map/cond/branch_1_fun/ppermute | solution.py:275
  668.7 80.6 %collective-permute-start.17 = (bf16[864,2048]{1,0:T(8,128)(2,1)}, bf16[864,2048]{1,0:T(8,128)(2,1)S(1)}, u32[]{:S(2)}, u32[]{:S(2)}) collective-permute-start(bf16[864,2048]{1,0:T(8,128)(2,1)} %get-tuple-element.352), channel_id=1, source_target_pairs={{0,2},{1,3},{2,4},{3,5},{4,6},{5,7},{6,0},{7,1},{8,10},{9,11},{10,... | collective-permute-start | bytes 10616840 | tf_op jit(solution)/shard_map/cond/branch_1_fun/ppermute | solution.py:505
  670.2 79.2 %collective-permute-start.18 = (bf16[864,2048]{1,0:T(8,128)(2,1)}, bf16[864,2048]{1,0:T(8,128)(2,1)S(1)}, u32[]{:S(2)}, u32[]{:S(2)}) collective-permute-start(bf16[864,2048]{1,0:T(8,128)(2,1)} %get-tuple-element.354), channel_id=1, source_target_pairs={{0,6},{1,7},{2,0},{3,1},{4,2},{5,3},{6,4},{7,5},{8,14},{9,15},{10,... | collective-permute-start | bytes 10616840 | tf_op jit(solution)/shard_map/cond/branch_1_fun/ppermute | solution.py:506
  714.9 34.5 %copy-start.49 = (bf16[864,2048]{1,0:T(8,128)(2,1)S(1)}, bf16[864,2048]{1,0:T(8,128)(2,1)}, u32[]{:S(2)}) copy-start(bf16[864,2048]{1,0:T(8,128)(2,1)} %get-tuple-element.355) | copy-start | bytes 10616836 | tf_op jit(solution)/shard_map/cond
  754.6 79.7 %collective-permute-start.19 = (bf16[864,2048]{1,0:T(8,128)(2,1)}, bf16[864,2048]{1,0:T(8,128)(2,1)S(1)}, u32[]{:S(2)}, u32[]{:S(2)}) collective-permute-start(bf16[864,2048]{1,0:T(8,128)(2,1)} %broadcast_select_fusion.3), channel_id=1, source_target_pairs={{0,2},{1,3},{2,4},{3,5},{4,6},{5,7},{6,0},{7,1},{8,10},{9,11},{10,... | collective-permute-start | bytes 10616840 | tf_op jit(solution)/shard_map/cond/branch_1_fun/ppermute | solution.py:505
  755.4 80.5 %collective-permute-start.20 = (bf16[864,2048]{1,0:T(8,128)(2,1)}, bf16[864,2048]{1,0:T(8,128)(2,1)S(1)}, u32[]{:S(2)}, u32[]{:S(2)}) collective-permute-start(bf16[864,2048]{1,0:T(8,128)(2,1)} %broadcast_select_fusion.2), channel_id=1, source_target_pairs={{0,6},{1,7},{2,0},{3,1},{4,2},{5,3},{6,4},{7,5},{8,14},{9,15},{10,... | collective-permute-start | bytes 10616840 | tf_op jit(solution)/shard_map/cond/branch_1_fun/ppermute | solution.py:506
  845.0 41.3 %collective-permute-start.21 = (bf16[768,2048]{1,0:T(8,128)(2,1)S(1)}, bf16[768,2048]{1,0:T(8,128)(2,1)S(1)}, u32[]{:S(2)}, u32[]{:S(2)}) collective-permute-start(bf16[768,2048]{1,0:T(8,128)(2,1)S(1)} %arrive.22), channel_id=1, source_target_pairs={{0,1},{1,0},{2,3},{3,2},{4,5},{5,4},{6,7},{7,6},{8,9},{9,8},{10,11... | collective-permute-start | bytes 9437192 | tf_op jit(solution)/shard_map/cond/branch_1_fun/ppermute | solution.py:275
  (32 other events, 386.4 us)
Sparse Core Ops, SparseCore 0:
  9.6 226.2 all-gather.6
  237.5 222.5 all-gather.8
